TPU v7x, 256 devices: a 8x8x2 block of a 8x8x16 slice. The times are simulated.
256 devices in a mesh: grp: 2 (over z), row: 16 (over x, core), col: 8 (over y).
Axes of the slice: x: 8, y: 8, z: 2, core: 2. Of those that a mesh axis runs over, the one named last changes fastest.
The devices are a block of a 8x8x16 slice.
Arguments:
- perturbation: bfloat16 [4, 12000, 12000], P('grp', 'row', 'col'), parts along dimension 0, may hold values from -96 to 96
- occ_coeffs: bfloat16 [12000, 2000], P('row', 'col'), may hold values from -0.0546875 to 0.0546875
- vir_coeffs: bfloat16 [12000, 512], P('col', 'row'), may hold values from -0.0546875 to 0.0546875
- occ_energies: float32 [2000], replicated, may hold values from -1 to -0.1
- vir_energies: float32 [512], replicated, may hold values from 0.1 to 1.5
Outputs:
- density_response: bfloat16 [4, 12000, 12000], P('grp', 'row', 'col'), parts along dimension 0
There are 2 independent parts, one for each index of `grp`. A program takes and returns all parts, laid end to end along the dimension named above; an argument that names none is the same for every part. Nothing has to cross between parts.
All inputs are finite; a program needn't handle non-finite values.
Results may differ from a plain program's by a relative error of at most 0.0098.
Values may be sent and summed in bfloat16 or wider, within the bound.
No kernel may reach another device: no remote copies, remote signals or barrier semaphores. Data moves between devices by JAX's collectives and lax.ppermute only.
A program may use at most 64 MiB of HBM per device.

v0:
```python
import jax
import jax.numpy as jnp
from jax import lax
from jax.experimental import pallas as pl
from jax.experimental.pallas import tpu as pltpu
from jax.sharding import Mesh
from jax.sharding import PartitionSpec as P

CORES = 2
LANES = 128
SWAP = [(0, 1), (1, 0)]
WIDE, NARROW = jnp.float32, jnp.bfloat16
ROOMY = pltpu.CompilerParams(vmem_limit_bytes=20 * 2**20)
SCALAR = pl.BlockSpec(memory_space=pltpu.SMEM)


def up_to(size, unit):
    return -(-size // unit) * unit


def shape_of(*dims, dtype=NARROW):
    return jax.ShapeDtypeStruct(dims, dtype)


def turn(shard, axis, step):
    size = lax.axis_size(axis)
    return lax.ppermute(shard, axis, [(i, (i + step) % size) for i in range(size)])


def ring_gather(shard, axis, mid):
    half = lax.axis_size(axis) // 2
    pieces, down, up = [shard], shard, shard
    for _ in range(half - 1):
        down, up = turn(down, axis, 1), turn(up, axis, -1)
        pieces += [down, up]
    far = [turn(down[:mid], axis, 1), turn(up[mid:], axis, -1)]
    return pieces + far


def ring_order(size):
    steps = [0]
    for s in range(1, size // 2):
        steps += [size - s, s]
    return steps + [size // 2]


def exchanged(pieces, axis):
    return lax.all_to_all(pieces, axis, split_axis=0, concat_axis=0, tiled=True)


def dot(a, b, over):
    return lax.dot_general(a, b, ((over[:1], over[1:]), ((), ())), preferred_element_type=WIDE)


def image_kernel(at, own, other, pert, turned, first, last, *near):
    y, k = at[0], at[1]
    size, share, _ = own.shape
    for d in range(size):
        source = lax.rem(y + d, size)
        for core, held in ((k, own), (1 - k, other)):
            start = pl.multiple_of((CORES * d + core) * share, share)
            turned[pl.ds(start, share), :] = held[source]
    block = CORES * share
    for p in range(pert.shape[0]):
        image = dot(turned[...], pert[p], (1, 1)).astype(NARROW)
        for d in range(size):
            part = image[d * block : (d + 1) * block]
            if d == size // 2:
                (first, last)[p][...] = part
            else:
                near[d - (d > size // 2)][p * block : (p + 1) * block, :] = part


def coupling_kernel(at, here, down, up, *refs):
    *chunks, far_low, far_high, send, keep, image = refs
    k = at[1]
    image[...] = (here[...].astype(WIDE) + down[...].astype(WIDE) + up[...].astype(WIDE)).astype(NARROW)
    block = image.shape[0] // CORES
    held = [image[pl.ds(pl.multiple_of(c * block, block), block), :] for c in (1 - k, k)]
    left = jnp.concatenate(held, axis=0)
    chunks = [c[...] for c in chunks] + [jnp.concatenate([far_low[...], far_high[...]], axis=0)]
    width = chunks[0].shape[1]
    spare = send.shape[2] - width
    for n, chunk in enumerate(chunks):
        value = dot(left, chunk, (1, 0))
        send[n, :, :width] = value[:block].astype(NARROW)
        keep[n, :, :width] = value[block:]
        send[n, :, width:] = jnp.zeros((block, spare), NARROW)
        keep[n, :, width:] = jnp.zeros((block, spare), WIDE)


def response_kernel(terms, levels, virtual, out):
    coupling = terms[0].astype(WIDE)
    for n in range(1, terms.shape[0]):
        coupling += terms[n].astype(WIDE)
    response = (coupling / (levels[...] - virtual[...])).astype(NARROW)
    for n in range(out.shape[0]):
        out[n] = response


def mixed_kernel(at, own, other, *refs):
    *chunks, far_low, far_high, out = refs
    k = at[1]
    chunks = [c[...] for c in chunks] + [jnp.concatenate([far_low[...], far_high[...]], axis=0)]
    width = chunks[0].shape[1]
    total = 0.0
    for n, chunk in enumerate(chunks):
        left = jnp.concatenate([own[n], other[n]], axis=0)[:, :width]
        total += dot(left, chunk, (1, 1))
    block = own.shape[1]
    total = total.astype(NARROW)
    for core, part in ((k, total[:block]), (1 - k, total[block:])):
        out[pl.ds(pl.multiple_of(core * block, block), block), :] = part


def density_kernel(turned, *refs):
    *pieces, first, last, out = refs
    size = len(pieces) + 1
    block = first.shape[0]
    for p in range(out.shape[1]):
        at_block = {d: piece[p * block : (p + 1) * block, :] for d, piece in zip(ring_order(size), pieces)}
        at_block[size // 2] = (first, last)[p][...]
        left = jnp.concatenate([at_block[d] for d in range(size)], axis=0)
        out[:, p, :] = dot(left, turned[...], (0, 0)).astype(NARROW)


def per_device(perturbation, occ_coeffs, vir_coeffs, occ_energies, vir_energies):
    nx, ny = lax.axis_size("x"), lax.axis_size("y")
    x, k, y = (lax.axis_index(a) for a in ("x", "k", "y"))
    perts, rows, cols = perturbation.shape
    own_occ = occ_coeffs.shape[1]
    share = vir_coeffs.shape[1]
    block = CORES * share
    at = jnp.stack([y, k]).astype(jnp.int32)

    mid = up_to(rows // 2, LANES)
    occ = ring_gather(occ_coeffs, "y", mid)
    own = exchanged(jnp.broadcast_to(vir_coeffs.T, (nx, share, cols)), "x")
    other = lax.ppermute(own, "k", SWAP)

    piece = shape_of(perts * block, rows)
    half = shape_of(block, rows)
    turned, first, last, *near = pl.pallas_call(
        image_kernel,
        in_specs=[SCALAR] + [pl.BlockSpec(memory_space=pltpu.VMEM)] * 3,
        out_shape=[shape_of(ny * block, cols), half, half] + [piece] * (ny - 1),
        compiler_params=ROOMY,
    )(at, own, other, perturbation)
    down, up = turn(first, "y", 1), turn(last, "y", -1)
    down = jnp.pad(down, [(0, block), (0, 0)])
    up = jnp.pad(up, [(block, 0), (0, 0)])
    for d in range(ny // 2 - 1, 0, -1):
        down = turn((near[d].astype(WIDE) + down).astype(NARROW), "y", 1)
        up = turn((near[-d].astype(WIDE) + up).astype(NARROW), "y", -1)

    wide_occ = up_to(own_occ, LANES)
    send, keep = pl.pallas_call(
        coupling_kernel,
        in_specs=[SCALAR] + [pl.BlockSpec(memory_space=pltpu.VMEM)] * (3 + len(occ)),
        out_shape=[shape_of(ny, block, wide_occ), shape_of(ny, block, wide_occ, dtype=WIDE)],
        scratch_shapes=[pltpu.VMEM((perts * block, rows), NARROW)],
        compiler_params=ROOMY,
    )(at, near[0], down, up, *occ)
    terms = (keep + lax.ppermute(send, "k", SWAP)).astype(NARROW)
    terms = exchanged(terms, "x")

    chunk = (y + jnp.array(ring_order(ny), jnp.int32)[x]) % ny
    levels = jnp.pad(occ_energies.reshape(ny, own_occ), [(0, 0), (0, wide_occ - own_occ)], constant_values=-1.0)
    levels = lax.dynamic_slice_in_dim(levels, chunk, 1, 0)
    virtual = lax.dynamic_slice_in_dim(vir_energies, y * block, block, 0)[:, None]
    response = pl.pallas_call(
        response_kernel, out_shape=shape_of(nx, block, wide_occ), compiler_params=ROOMY
    )(terms, levels, virtual)
    response = exchanged(response, "x")
    sibling = lax.ppermute(response, "k", SWAP)
    mixed = pl.pallas_call(
        mixed_kernel,
        in_specs=[SCALAR] + [pl.BlockSpec(memory_space=pltpu.VMEM)] * (2 + len(occ)),
        out_shape=piece,
        compiler_params=ROOMY,
    )(at, response, sibling, *occ)

    pieces = ring_gather(mixed, "y", block)
    tile = 2 * LANES
    narrow = [pl.BlockSpec((p.shape[0], tile), lambda i: (0, i)) for p in pieces]
    total = pl.pallas_call(
        density_kernel,
        grid=(pl.cdiv(rows, tile),),
        in_specs=[pl.BlockSpec(turned.shape, lambda i: (0, 0))] + narrow,
        out_specs=pl.BlockSpec((tile, perts, cols), lambda i: (i, 0, 0)),
        out_shape=shape_of(rows, perts, cols),
        compiler_params=ROOMY,
    )(turned, *pieces)
    return jnp.transpose(total, (1, 0, 2))


def solution(mesh):
    rows, cols = mesh.shape["row"], mesh.shape["col"]
    torus = Mesh(
        mesh.devices.reshape(mesh.shape["grp"], rows // CORES, CORES, cols),
        ("grp", "x", "k", "y"),
    )
    row = ("x", "k")
    in_specs = (P("grp", row, "y"), P(row, "y"), P("y", row), P(), P())

    return jax.shard_map(per_device, mesh=torus, in_specs=in_specs, out_specs=P("grp", row, "y"), check_vma=False)
```

profile of v0, /device:TPU:516, one launch (start us, length us, event | category | flops | bytes accessed | tf_op | source)
XLA Modules:
  0.0 172.8 jit_solution(16438233922018756497)
XLA Ops:
  0.0 1.8 %broadcast_in_dim.6 = bf16[8,32,1500]{2,1,0:T(8,128)(2,1)} broadcast(bf16[32,1500]{1,0:T(8,128)(2,1)} %bitcast.7), dimensions={1,2} | broadcast | bytes 864000 | tf_op jit(solution)/shard_map/broadcast_in_dim | solution.py:138
  1.9 22.7 %all-to-all-start = ((bf16[8,32,1500]{2,1,0:T(8,128)(2,1)}), bf16[8,32,1500]{2,1,0:T(8,128)(2,1)S(1)}, u32[]{:S(2)}, u32[]{:S(2)}) async-start(bf16[8,32,1500]{2,1,0:T(8,128)(2,1)} %broadcast_in_dim.6), calls=%async_computation | async-start | bytes 1572864 | tf_op jit(solution)/shard_map/all_to_all | solution.py:48
  24.6 0.0 collective-permute-start.9
  24.6 12.8 %all-to-all-done.own = bf16[8,32,1500]{2,1,0:T(8,128)(2,1)S(1)} async-done(((bf16[8,32,1500]{2,1,0:T(8,128)(2,1)}), bf16[8,32,1500]{2,1,0:T(8,128)(2,1)S(1)}, u32[]{:S(2)}, u32[]{:S(2)}) %all-to-all-start) | async-done | bytes 768032 | tf_op jit(solution)/shard_map/all_to_all | solution.py:48
  37.4 0.0 collective-permute-start
  37.4 4.6 %collective-permute-start.10 = (bf16[750,250]{1,0:T(8,128)(2,1)}, bf16[750,250]{1,0:T(8,128)(2,1)}, u32[]{:S(2)}, u32[]{:S(2)}) collective-permute-start(bf16[750,250]{1,0:T(8,128)(2,1)} %refs_0_.3), channel_id=1, source_target_pairs={{0,7},{1,0},{2,1},{3,2},{4,3},{5,4},{6,5},{7,6},{8,15},{9,8},{10,9... | collective-permute-start | bytes 1125008 | tf_op jit(solution)/shard_map/ppermute | solution.py:27
  42.0 0.0 collective-permute-done.9.refs_1_
  42.0 0.0 collective-permute-start.11
  42.0 9.2 %collective-permute-done.10.refs_2_ = bf16[750,250]{1,0:T(8,128)(2,1)} collective-permute-done((bf16[750,250]{1,0:T(8,128)(2,1)}, bf16[750,250]{1,0:T(8,128)(2,1)}, u32[]{:S(2)}, u32[]{:S(2)}) %collective-permute-start.10) | collective-permute-done | bytes 375032 | tf_op jit(solution)/shard_map/ppermute | solution.py:27
  51.2 3.7 %collective-permute-start.12 = (bf16[750,250]{1,0:T(8,128)(2,1)}, bf16[750,250]{1,0:T(8,128)(2,1)}, u32[]{:S(2)}, u32[]{:S(2)}) collective-permute-start(bf16[750,250]{1,0:T(8,128)(2,1)} %collective-permute-done.10.refs_2_), channel_id=1, source_target_pairs={{0,7},{1,0},{2,1},{3,2},{4,3},{5,4},{6,5},{7,6},{8,15},{9,8},{10,9... | collective-permute-start | bytes 1125008 | tf_op jit(solution)/shard_map/ppermute | solution.py:27
  54.8 0.0 collective-permute-done.11.refs_3_
  54.9 3.0 %copy.7.pert = bf16[2,750,1500]{2,1,0:T(8,128)(2,1)S(1)} copy(bf16[2,750,1500]{2,0,1:T(2,128)(2,1)} %param.6) | data formatting | bytes 9000000 | tf_op args[0]
  57.9 0.1 pad_add_fusion.at
  58.0 0.9 copy-done.2
  58.8 1.1 copy-done.3
  60.0 3.2 %shard_map.64 = (bf16[512,1500]{1,0:T(8,128)(2,1)S(1)}, bf16[64,750]{1,0:T(8,128)(2,1)S(1)}, bf16[64,750]{1,0:T(8,128)(2,1)S(1)}, bf16[128,750]{1,0:T(8,128)(2,1...) custom-call(s32[2]{0:T(128)S(1)} %pad_add_fusion.at, ...), custom_call_target="tpu_custom_call" | custom-call | tf_op jit(solution)/shard_map/pallas_call | solution.py:143
  63.2 0.0 copy-start.9
  63.2 3.3 %collective-permute-start.5 = (bf16[64,750]{1,0:T(8,128)(2,1)S(1)}, bf16[64,750]{1,0:T(8,128)(2,1)S(1)}, u32[]{:S(2)}, u32[]{:S(2)}) collective-permute-start(bf16[64,750]{1,0:T(8,128)(2,1)S(1)} %get-tuple-element.26), channel_id=1, source_target_pairs={{0,7},{1,0},{2,1},{3,2},{4,3},{5,4},{6,5},{7,6},{8,15},{9,8},{10,9... | collective-permute-start | bytes 288008 | tf_op jit(solution)/shard_map/ppermute | solution.py:27
  66.6 0.0 collective-permute-done.12.refs_4_
  66.6 0.3 collective-permute-start.14
  66.9 0.0 copy-start.8
  66.9 1.8 %collective-permute-start.15 = (bf16[384,250]{1,0:T(8,128)(2,1)S(1)}, bf16[384,250]{1,0:T(8,128)(2,1)S(1)}, u32[]{:S(2)}, u32[]{:S(2)}) collective-permute-start(bf16[384,250]{1,0:T(8,128)(2,1)S(1)} %slice.16), channel_id=1, source_target_pairs={{0,1},{1,2},{2,3},{3,4},{4,5},{5,6},{6,7},{7,0},{8,9},{9,10},{10,1... | collective-permute-start | bytes 576008 | tf_op jit(solution)/shard_map/ppermute | solution.py:27
  68.7 0.1 collective-permute-start.1
  68.9 0.9 collective-permute-done.5
  69.8 3.8 %collective-permute-start.6 = (bf16[128,750]{1,0:T(8,128)(2,1)S(1)}, bf16[128,750]{1,0:T(8,128)(2,1)S(1)}, u32[]{:S(2)}, u32[]{:S(2)}) collective-permute-start(bf16[128,750]{1,0:T(8,128)(2,1)S(1)} %add_convert_fusion.3), channel_id=1, source_target_pairs={{0,7},{1,0},{2,1},{3,2},{4,3},{5,4},{6,5},{7,6},{8,15},{9,8},{10,9... | collective-permute-start | bytes 576008 | tf_op jit(solution)/shard_map/ppermute | solution.py:27
  73.6 2.2 %collective-permute-done.1 = bf16[64,750]{1,0:T(8,128)(2,1)S(1)} collective-permute-done((bf16[64,750]{1,0:T(8,128)(2,1)S(1)}, bf16[64,750]{1,0:T(8,128)(2,1)S(1)}, u32[]{:S(2)}, u32[]{:S(2)}) %collective-permute-start.1) | collective-permute-done | bytes 96032 | tf_op jit(solution)/shard_map/ppermute | solution.py:27
  75.8 0.7 collective-permute-start.2
  76.5 4.1 %collective-permute-done.6 = bf16[128,750]{1,0:T(8,128)(2,1)S(1)} collective-permute-done((bf16[128,750]{1,0:T(8,128)(2,1)S(1)}, bf16[128,750]{1,0:T(8,128)(2,1)S(1)}, u32[]{:S(2)}, u32[]{:S(2)}) %collective-permute-start.6) | collective-permute-done | bytes 192032 | tf_op jit(solution)/shard_map/ppermute | solution.py:27
  80.7 3.5 %collective-permute-start.7 = (bf16[128,750]{1,0:T(8,128)(2,1)S(1)}, bf16[128,750]{1,0:T(8,128)(2,1)S(1)}, u32[]{:S(2)}, u32[]{:S(2)}) collective-permute-start(bf16[128,750]{1,0:T(8,128)(2,1)S(1)} %add_convert_fusion.2), channel_id=1, source_target_pairs={{0,7},{1,0},{2,1},{3,2},{4,3},{5,4},{6,5},{7,6},{8,15},{9,8},{10,9... | collective-permute-start | bytes 576008 | tf_op jit(solution)/shard_map/ppermute | solution.py:27
  84.2 0.1 collective-permute-start.3
  84.4 3.0 %collective-permute-done.7 = bf16[128,750]{1,0:T(8,128)(2,1)S(1)} collective-permute-done((bf16[128,750]{1,0:T(8,128)(2,1)S(1)}, bf16[128,750]{1,0:T(8,128)(2,1)S(1)}, u32[]{:S(2)}, u32[]{:S(2)}) %collective-permute-start.7) | collective-permute-done | bytes 192032 | tf_op jit(solution)/shard_map/ppermute | solution.py:27
  87.4 3.8 %collective-permute-start.8 = (bf16[128,750]{1,0:T(8,128)(2,1)S(1)}, bf16[128,750]{1,0:T(8,128)(2,1)S(1)}, u32[]{:S(2)}, u32[]{:S(2)}) collective-permute-start(bf16[128,750]{1,0:T(8,128)(2,1)S(1)} %add_convert_fusion.1), channel_id=1, source_target_pairs={{0,7},{1,0},{2,1},{3,2},{4,3},{5,4},{6,5},{7,6},{8,15},{9,8},{10,9... | collective-permute-start | bytes 576008 | tf_op jit(solution)/shard_map/ppermute | solution.py:27
  91.2 0.0 collective-permute-done.3
  91.3 0.1 collective-permute-start.4
  91.5 3.3 %collective-permute-start.16 = (bf16[366,250]{1,0:T(8,128)(2,1)S(1)}, bf16[366,250]{1,0:T(8,128)(2,1)S(1)}, u32[]{:S(2)}, u32[]{:S(2)}) collective-permute-start(bf16[366,250]{1,0:T(8,128)(2,1)S(1)} %slice.17), channel_id=1, source_target_pairs={{0,7},{1,0},{2,1},{3,2},{4,3},{5,4},{6,5},{7,6},{8,15},{9,8},{10,9... | collective-permute-start | bytes 549008 | tf_op jit(solution)/shard_map/ppermute | solution.py:27
  94.8 3.1 %collective-permute-done.16.refs_8_ = bf16[366,250]{1,0:T(8,128)(2,1)S(1)} collective-permute-done((bf16[366,250]{1,0:T(8,128)(2,1)S(1)}, bf16[366,250]{1,0:T(8,128)(2,1)S(1)}, u32[]{:S(2)}, u32[]{:S(2)}) %collective-permute-start.16) | collective-permute-done | bytes 183032 | tf_op jit(solution)/shard_map/ppermute | solution.py:27
  97.9 0.4 collective-permute-done.4.down
  98.3 1.9 %shard_map.65 = (bf16[8,64,256]{2,1,0:T(8,128)(2,1)S(1)}, f32[8,64,256]{2,1,0:T(8,128)S(1)}) custom-call(s32[2]{0:T(128)S(1)} %pad_add_fusion.at, bf16[128,750]{1,0:T(8,128)(2,1)S(1)} %get-tuple-element.18.here, bf16[128,750]{1,0:T(8,128)(2,1)S(1)} %collective-permute-done.4.down, bf16[128,750]{1,0:T(8,128)(2,1)S(1)} %collective-permute-done.8.up, ...), custom_call_target="tpu_custom_call" | custom-call | tf_op jit(solution)/shard_map/pallas_call | solution.py:157
  100.2 0.1 collective-permute-start.17
  100.4 1.5 collective-permute-done.17
  101.9 0.8 add_convert_fusion
  102.6 5.8 %all-to-all-start.1 = ((bf16[8,64,256]{2,1,0:T(8,128)(2,1)}), bf16[8,64,256]{2,1,0:T(8,128)(2,1)S(1)}, u32[]{:S(2)}, u32[]{:S(2)}) async-start(bf16[8,64,256]{2,1,0:T(8,128)(2,1)} %add_convert_fusion), calls=%async_computation.1 | async-start | bytes 524288 | tf_op jit(solution)/shard_map/all_to_all | solution.py:48
  108.5 0.6 dynamic_slice.9
  109.8 0.1 reshape.3
  109.9 0.1 dynamic-slice_bitcast_fusion
  110.0 0.1 copy.8.virtual
  110.1 7.8 %all-to-all-done.1.terms = bf16[8,64,256]{2,1,0:T(8,128)(2,1)S(1)} async-done(((bf16[8,64,256]{2,1,0:T(8,128)(2,1)}), bf16[8,64,256]{2,1,0:T(8,128)(2,1)S(1)}, u32[]{:S(2)}, u32[]{:S(2)}) %all-to-all-start.1) | async-done | bytes 262176 | tf_op jit(solution)/shard_map/all_to_all | solution.py:48
  118.0 0.1 shard_map.66
  118.1 14.8 %all_to_all.15.own = bf16[8,64,256]{2,1,0:T(8,128)(2,1)S(1)} all-to-all(bf16[8,64,256]{2,1,0:T(8,128)(2,1)S(1)} %shard_map.66), channel_id=1, replica_groups=mesh['grp'=2,'x'=8,'k'=2,'y'=8] {'x'}, dimensions={0} | all-to-all | bytes 524288 | tf_op jit(solution)/shard_map/all_to_all | solution.py:48
  132.8 1.5 collective-permute-done.18.other
  134.4 0.9 copy-done.5
  135.3 0.9 copy-done.7
  136.2 2.3 %shard_map.67.refs_0_ = bf16[128,750]{1,0:T(8,128)(2,1)S(1)} custom-call(s32[2]{0:T(128)S(1)} %pad_add_fusion.at, bf16[8,64,256]{2,1,0:T(8,128)(2,1)S(1)} %all_to_all.15.own, bf16[8,64,256]{2,1,0:T(8,128)(2,1)S(1)} %collective-permute-done.18.other, bf16[750,250]{1,0:T(8,128)(2,1)S(1)} %copy-done.1, bf16[750,250]{1,0:T(8,128)(2,1)S(1)} %collective-permute-done.9.refs_1_, ...), custom_call_target="tpu_custom_call" | custom-call | tf_op jit(solution)/shard_map/pallas_call | solution.py:176
  138.5 0.1 collective-permute-start.19
  138.7 3.5 %collective-permute-start.20 = (bf16[128,750]{1,0:T(8,128)(2,1)S(1)}, bf16[128,750]{1,0:T(8,128)(2,1)S(1)}, u32[]{:S(2)}, u32[]{:S(2)}) collective-permute-start(bf16[128,750]{1,0:T(8,128)(2,1)S(1)} %shard_map.67.refs_0_), channel_id=1, source_target_pairs={{0,7},{1,0},{2,1},{3,2},{4,3},{5,4},{6,5},{7,6},{8,15},{9,8},{10,9... | collective-permute-start | bytes 576008 | tf_op jit(solution)/shard_map/ppermute | solution.py:27
  142.2 5.1 %collective-permute-done.19.refs_1_ = bf16[128,750]{1,0:T(8,128)(2,1)S(1)} collective-permute-done((bf16[128,750]{1,0:T(8,128)(2,1)S(1)}, bf16[128,750]{1,0:T(8,128)(2,1)S(1)}, u32[]{:S(2)}, u32[]{:S(2)}) %collective-permute-start.19) | collective-permute-done | bytes 192032 | tf_op jit(solution)/shard_map/ppermute | solution.py:27
  147.3 3.2 %collective-permute-start.22 = (bf16[128,750]{1,0:T(8,128)(2,1)S(1)}, bf16[128,750]{1,0:T(8,128)(2,1)S(1)}, u32[]{:S(2)}, u32[]{:S(2)}) collective-permute-start(bf16[128,750]{1,0:T(8,128)(2,1)S(1)} %collective-permute-done.20.refs_2_), channel_id=1, source_target_pairs={{0,7},{1,0},{2,1},{3,2},{4,3},{5,4},{6,5},{7,6},{8,15},{9,8},{10,9... | collective-permute-start | bytes 576008 | tf_op jit(solution)/shard_map/ppermute | solution.py:27
  150.5 4.3 %collective-permute-done.21.refs_3_ = bf16[128,750]{1,0:T(8,128)(2,1)S(1)} collective-permute-done((bf16[128,750]{1,0:T(8,128)(2,1)S(1)}, bf16[128,750]{1,0:T(8,128)(2,1)S(1)}, u32[]{:S(2)}, u32[]{:S(2)}) %collective-permute-start.21) | collective-permute-done | bytes 192032 | tf_op jit(solution)/shard_map/ppermute | solution.py:27
  154.9 3.2 %collective-permute-start.24 = (bf16[128,750]{1,0:T(8,128)(2,1)S(1)}, bf16[128,750]{1,0:T(8,128)(2,1)S(1)}, u32[]{:S(2)}, u32[]{:S(2)}) collective-permute-start(bf16[128,750]{1,0:T(8,128)(2,1)S(1)} %collective-permute-done.22.refs_4_), channel_id=1, source_target_pairs={{0,7},{1,0},{2,1},{3,2},{4,3},{5,4},{6,5},{7,6},{8,15},{9,8},{10,9... | collective-permute-start | bytes 576008 | tf_op jit(solution)/shard_map/ppermute | solution.py:27
  158.1 3.6 %collective-permute-done.23.refs_5_ = bf16[128,750]{1,0:T(8,128)(2,1)S(1)} collective-permute-done((bf16[128,750]{1,0:T(8,128)(2,1)S(1)}, bf16[128,750]{1,0:T(8,128)(2,1)S(1)}, u32[]{:S(2)}, u32[]{:S(2)}) %collective-permute-start.23) | collective-permute-done | bytes 192032 | tf_op jit(solution)/shard_map/ppermute | solution.py:27
  161.8 0.1 collective-permute-start.25
  161.9 3.3 %collective-permute-start.26 = (bf16[64,750]{1,0:T(8,128)(2,1)S(1)}, bf16[64,750]{1,0:T(8,128)(2,1)S(1)}, u32[]{:S(2)}, u32[]{:S(2)}) collective-permute-start(bf16[64,750]{1,0:T(8,128)(2,1)S(1)} %slice.19), channel_id=1, source_target_pairs={{0,7},{1,0},{2,1},{3,2},{4,3},{5,4},{6,5},{7,6},{8,15},{9,8},{10,9... | collective-permute-start | bytes 288008 | tf_op jit(solution)/shard_map/ppermute | solution.py:27
  165.2 2.5 %collective-permute-done.25.refs_7_ = bf16[64,750]{1,0:T(8,128)(2,1)S(1)} collective-permute-done((bf16[64,750]{1,0:T(8,128)(2,1)S(1)}, bf16[64,750]{1,0:T(8,128)(2,1)S(1)}, u32[]{:S(2)}, u32[]{:S(2)}) %collective-permute-start.25) | collective-permute-done | bytes 96032 | tf_op jit(solution)/shard_map/ppermute | solution.py:27
  167.7 5.1 %shard_map.68 = bf16[750,2,1500]{2,1,0:T(2,128)(2,1)} custom-call(bf16[512,1500]{1,0:T(8,128)(2,1)S(1)} %get-tuple-element.17.turned, bf16[128,750]{1,0:T(8,128)(2,1)S(1)} %shard_map.67.refs_0_, bf16[128,750]{1,0:T(8,128)(2,1)S(1)} %collective-permute-done.19.refs_1_, bf16[128,750]{1,0:T(8,128)(2,1)S(1)} %collective-permute-done.20.refs_2_, ...), custom_call_target="tpu_custom_call" | custom-call | tf_op jit(solution)/shard_map/pallas_call | solution.py:186
  (39 shorter events, 0.4 us)
Async XLA Ops:
  0.0 109.9 %copy-start = (f32[512]{0:T(512)S(1)}, f32[512]{0:T(512)}, u32[]{:S(2)}) copy-start(f32[512]{0:T(512)} %param.10) | copy-start | bytes 6148
  1.9 35.5 %all-to-all-start = ((bf16[8,32,1500]{2,1,0:T(8,128)(2,1)}), bf16[8,32,1500]{2,1,0:T(8,128)(2,1)S(1)}, u32[]{:S(2)}, u32[]{:S(2)}) async-start(bf16[8,32,1500]{2,1,0:T(8,128)(2,1)} %broadcast_in_dim.6), calls=%async_computation | async-start | bytes 1572864 | tf_op jit(solution)/shard_map/all_to_all | solution.py:48
  24.6 17.4 %collective-permute-start.9 = (bf16[750,250]{1,0:T(8,128)(2,1)}, bf16[750,250]{1,0:T(8,128)(2,1)S(1)}, u32[]{:S(2)}, u32[]{:S(2)}) collective-permute-start(bf16[750,250]{1,0:T(8,128)(2,1)} %refs_0_.3), channel_id=1, source_target_pairs={{0,1},{1,2},{2,3},{3,4},{4,5},{5,6},{6,7},{7,0},{8,9},{9,10},{10,1... | collective-permute-start | bytes 1125008 | tf_op jit(solution)/shard_map/ppermute | solution.py:27
  37.4 20.6 %collective-permute-start = (bf16[8,32,1500]{2,1,0:T(8,128)(2,1)S(1)}, bf16[8,32,1500]{2,1,0:T(8,128)(2,1)S(1)}, u32[]{:S(2)}, u32[]{:S(2)}) collective-permute-start(bf16[8,32,1500]{2,1,0:T(8,128)(2,1)S(1)} %all-to-all-done.own), channel_id=1, source_target_pairs={{0,8},{8,0},{1,9},{9,1},{2,10},{10,2},{3,11},{11,3},{4,12},{12,4},... | collective-permute-start | bytes 2304008 | tf_op jit(solution)/shard_map/ppermute | solution.py:139
  37.4 13.8 %collective-permute-start.10 = (bf16[750,250]{1,0:T(8,128)(2,1)}, bf16[750,250]{1,0:T(8,128)(2,1)}, u32[]{:S(2)}, u32[]{:S(2)}) collective-permute-start(bf16[750,250]{1,0:T(8,128)(2,1)} %refs_0_.3), channel_id=1, source_target_pairs={{0,7},{1,0},{2,1},{3,2},{4,3},{5,4},{6,5},{7,6},{8,15},{9,8},{10,9... | collective-permute-start | bytes 1125008 | tf_op jit(solution)/shard_map/ppermute | solution.py:27
  42.0 12.9 %collective-permute-start.11 = (bf16[750,250]{1,0:T(8,128)(2,1)S(1)}, bf16[750,250]{1,0:T(8,128)(2,1)}, u32[]{:S(2)}, u32[]{:S(2)}) collective-permute-start(bf16[750,250]{1,0:T(8,128)(2,1)S(1)} %collective-permute-done.9.refs_1_), channel_id=1, source_target_pairs={{0,1},{1,2},{2,3},{3,4},{4,5},{5,6},{6,7},{7,0},{8,9},{9,10},{10,1... | collective-permute-start | bytes 1125008 | tf_op jit(solution)/shard_map/ppermute | solution.py:27
  51.2 15.4 %collective-permute-start.12 = (bf16[750,250]{1,0:T(8,128)(2,1)}, bf16[750,250]{1,0:T(8,128)(2,1)}, u32[]{:S(2)}, u32[]{:S(2)}) collective-permute-start(bf16[750,250]{1,0:T(8,128)(2,1)} %collective-permute-done.10.refs_2_), channel_id=1, source_target_pairs={{0,7},{1,0},{2,1},{3,2},{4,3},{5,4},{6,5},{7,6},{8,15},{9,8},{10,9... | collective-permute-start | bytes 1125008 | tf_op jit(solution)/shard_map/ppermute | solution.py:27
  54.8 12.0 %collective-permute-start.13 = (bf16[750,250]{1,0:T(8,128)(2,1)}, bf16[750,250]{1,0:T(8,128)(2,1)S(1)}, u32[]{:S(2)}, u32[]{:S(2)}) collective-permute-start(bf16[750,250]{1,0:T(8,128)(2,1)} %collective-permute-done.11.refs_3_), channel_id=1, source_target_pairs={{0,1},{1,2},{2,3},{3,4},{4,5},{5,6},{6,7},{7,0},{8,9},{9,10},{10,1... | collective-permute-start | bytes 1125008 | tf_op jit(solution)/shard_map/ppermute | solution.py:27
  58.0 40.3 %copy-start.1 = (bf16[750,250]{1,0:T(8,128)(2,1)S(1)}, bf16[750,250]{1,0:T(8,128)(2,1)}, u32[]{:S(2)}) copy-start(bf16[750,250]{1,0:T(8,128)(2,1)} %refs_0_.3) | copy-start | bytes 1125004
  58.0 0.9 copy-start.2
  58.8 1.1 copy-start.3
  63.2 45.3 %copy-start.9 = (s32[8]{0:T(128)S(1)}, s32[8]{0:T(128)}, u32[]{:S(2)}) copy-start(s32[8]{0:T(128)} %constant.37.clone) | copy-start | bytes 100
  63.2 6.5 %collective-permute-start.5 = (bf16[64,750]{1,0:T(8,128)(2,1)S(1)}, bf16[64,750]{1,0:T(8,128)(2,1)S(1)}, u32[]{:S(2)}, u32[]{:S(2)}) collective-permute-start(bf16[64,750]{1,0:T(8,128)(2,1)S(1)} %get-tuple-element.26), channel_id=1, source_target_pairs={{0,7},{1,0},{2,1},{3,2},{4,3},{5,4},{6,5},{7,6},{8,15},{9,8},{10,9... | collective-permute-start | bytes 288008 | tf_op jit(solution)/shard_map/ppermute | solution.py:27
  66.6 24.9 %collective-permute-start.14 = (bf16[750,250]{1,0:T(8,128)(2,1)}, bf16[750,250]{1,0:T(8,128)(2,1)S(1)}, u32[]{:S(2)}, u32[]{:S(2)}) collective-permute-start(bf16[750,250]{1,0:T(8,128)(2,1)} %collective-permute-done.12.refs_4_), channel_id=1, source_target_pairs={{0,7},{1,0},{2,1},{3,2},{4,3},{5,4},{6,5},{7,6},{8,15},{9,8},{10,9... | collective-permute-start | bytes 1125008 | tf_op jit(solution)/shard_map/ppermute | solution.py:27
  66.9 42.9 %copy-start.8 = (f32[2000]{0:T(1024)S(1)}, f32[2000]{0:T(1024)}, u32[]{:S(2)}) copy-start(f32[2000]{0:T(1024)} %param.9) | copy-start | bytes 24004
  66.9 31.0 %collective-permute-start.15 = (bf16[384,250]{1,0:T(8,128)(2,1)S(1)}, bf16[384,250]{1,0:T(8,128)(2,1)S(1)}, u32[]{:S(2)}, u32[]{:S(2)}) collective-permute-start(bf16[384,250]{1,0:T(8,128)(2,1)S(1)} %slice.16), channel_id=1, source_target_pairs={{0,1},{1,2},{2,3},{3,4},{4,5},{5,6},{6,7},{7,0},{8,9},{9,10},{10,1... | collective-permute-start | bytes 576008 | tf_op jit(solution)/shard_map/ppermute | solution.py:27
  68.7 7.1 %collective-permute-start.1 = (bf16[64,750]{1,0:T(8,128)(2,1)S(1)}, bf16[64,750]{1,0:T(8,128)(2,1)S(1)}, u32[]{:S(2)}, u32[]{:S(2)}) collective-permute-start(bf16[64,750]{1,0:T(8,128)(2,1)S(1)} %get-tuple-element.22), channel_id=1, source_target_pairs={{0,1},{1,2},{2,3},{3,4},{4,5},{5,6},{6,7},{7,0},{8,9},{9,10},{10,1... | collective-permute-start | bytes 288008 | tf_op jit(solution)/shard_map/ppermute | solution.py:27
  69.8 10.9 %collective-permute-start.6 = (bf16[128,750]{1,0:T(8,128)(2,1)S(1)}, bf16[128,750]{1,0:T(8,128)(2,1)S(1)}, u32[]{:S(2)}, u32[]{:S(2)}) collective-permute-start(bf16[128,750]{1,0:T(8,128)(2,1)S(1)} %add_convert_fusion.3), channel_id=1, source_target_pairs={{0,7},{1,0},{2,1},{3,2},{4,3},{5,4},{6,5},{7,6},{8,15},{9,8},{10,9... | collective-permute-start | bytes 576008 | tf_op jit(solution)/shard_map/ppermute | solution.py:27
  75.8 8.4 %collective-permute-start.2 = (bf16[128,750]{1,0:T(8,128)(2,1)S(1)}, bf16[128,750]{1,0:T(8,128)(2,1)S(1)}, u32[]{:S(2)}, u32[]{:S(2)}) collective-permute-start(bf16[128,750]{1,0:T(8,128)(2,1)S(1)} %add_convert_fusion.6), channel_id=1, source_target_pairs={{0,1},{1,2},{2,3},{3,4},{4,5},{5,6},{6,7},{7,0},{8,9},{9,10},{10,1... | collective-permute-start | bytes 576008 | tf_op jit(solution)/shard_map/ppermute | solution.py:27
  80.7 6.7 %collective-permute-start.7 = (bf16[128,750]{1,0:T(8,128)(2,1)S(1)}, bf16[128,750]{1,0:T(8,128)(2,1)S(1)}, u32[]{:S(2)}, u32[]{:S(2)}) collective-permute-start(bf16[128,750]{1,0:T(8,128)(2,1)S(1)} %add_convert_fusion.2), channel_id=1, source_target_pairs={{0,7},{1,0},{2,1},{3,2},{4,3},{5,4},{6,5},{7,6},{8,15},{9,8},{10,9... | collective-permute-start | bytes 576008 | tf_op jit(solution)/shard_map/ppermute | solution.py:27
  84.2 7.0 %collective-permute-start.3 = (bf16[128,750]{1,0:T(8,128)(2,1)S(1)}, bf16[128,750]{1,0:T(8,128)(2,1)S(1)}, u32[]{:S(2)}, u32[]{:S(2)}) collective-permute-start(bf16[128,750]{1,0:T(8,128)(2,1)S(1)} %add_convert_fusion.5), channel_id=1, source_target_pairs={{0,1},{1,2},{2,3},{3,4},{4,5},{5,6},{6,7},{7,0},{8,9},{9,10},{10,1... | collective-permute-start | bytes 576008 | tf_op jit(solution)/shard_map/ppermute | solution.py:27
  87.4 10.5 %collective-permute-start.8 = (bf16[128,750]{1,0:T(8,128)(2,1)S(1)}, bf16[128,750]{1,0:T(8,128)(2,1)S(1)}, u32[]{:S(2)}, u32[]{:S(2)}) collective-permute-start(bf16[128,750]{1,0:T(8,128)(2,1)S(1)} %add_convert_fusion.1), channel_id=1, source_target_pairs={{0,7},{1,0},{2,1},{3,2},{4,3},{5,4},{6,5},{7,6},{8,15},{9,8},{10,9... | collective-permute-start | bytes 576008 | tf_op jit(solution)/shard_map/ppermute | solution.py:27
  91.3 7.0 %collective-permute-start.4 = (bf16[128,750]{1,0:T(8,128)(2,1)S(1)}, bf16[128,750]{1,0:T(8,128)(2,1)S(1)}, u32[]{:S(2)}, u32[]{:S(2)}) collective-permute-start(bf16[128,750]{1,0:T(8,128)(2,1)S(1)} %add_convert_fusion.4), channel_id=1, source_target_pairs={{0,1},{1,2},{2,3},{3,4},{4,5},{5,6},{6,7},{7,0},{8,9},{9,10},{10,1... | collective-permute-start | bytes 576008 | tf_op jit(solution)/shard_map/ppermute | solution.py:27
  91.5 6.4 %collective-permute-start.16 = (bf16[366,250]{1,0:T(8,128)(2,1)S(1)}, bf16[366,250]{1,0:T(8,128)(2,1)S(1)}, u32[]{:S(2)}, u32[]{:S(2)}) collective-permute-start(bf16[366,250]{1,0:T(8,128)(2,1)S(1)} %slice.17), channel_id=1, source_target_pairs={{0,7},{1,0},{2,1},{3,2},{4,3},{5,4},{6,5},{7,6},{8,15},{9,8},{10,9... | collective-permute-start | bytes 549008 | tf_op jit(solution)/shard_map/ppermute | solution.py:27
  97.9 4.8 %copy-start.6 = (bf16[366,250]{1,0:T(8,128)(2,1)}, bf16[366,250]{1,0:T(8,128)(2,1)S(1)}, u32[]{:S(2)}) copy-start(bf16[366,250]{1,0:T(8,128)(2,1)S(1)} %collective-permute-done.16.refs_8_) | copy-start | bytes 549004
  97.9 4.8 %copy-start.4 = (bf16[384,250]{1,0:T(8,128)(2,1)}, bf16[384,250]{1,0:T(8,128)(2,1)S(1)}, u32[]{:S(2)}) copy-start(bf16[384,250]{1,0:T(8,128)(2,1)S(1)} %collective-permute-done.15.refs_7_) | copy-start | bytes 576004
  100.2 1.7 collective-permute-start.17
  102.6 15.3 %all-to-all-start.1 = ((bf16[8,64,256]{2,1,0:T(8,128)(2,1)}), bf16[8,64,256]{2,1,0:T(8,128)(2,1)S(1)}, u32[]{:S(2)}, u32[]{:S(2)}) async-start(bf16[8,64,256]{2,1,0:T(8,128)(2,1)} %add_convert_fusion), calls=%async_computation.1 | async-start | bytes 524288 | tf_op jit(solution)/shard_map/all_to_all | solution.py:48
  132.8 1.5 collective-permute-start.18
  134.4 0.9 copy-start.5
  135.3 0.9 copy-start.7
  138.5 8.8 %collective-permute-start.19 = (bf16[128,750]{1,0:T(8,128)(2,1)S(1)}, bf16[128,750]{1,0:T(8,128)(2,1)S(1)}, u32[]{:S(2)}, u32[]{:S(2)}) collective-permute-start(bf16[128,750]{1,0:T(8,128)(2,1)S(1)} %shard_map.67.refs_0_), channel_id=1, source_target_pairs={{0,1},{1,2},{2,3},{3,4},{4,5},{5,6},{6,7},{7,0},{8,9},{9,10},{10,1... | collective-permute-start | bytes 576008 | tf_op jit(solution)/shard_map/ppermute | solution.py:27
  138.7 8.6 %collective-permute-start.20 = (bf16[128,750]{1,0:T(8,128)(2,1)S(1)}, bf16[128,750]{1,0:T(8,128)(2,1)S(1)}, u32[]{:S(2)}, u32[]{:S(2)}) collective-permute-start(bf16[128,750]{1,0:T(8,128)(2,1)S(1)} %shard_map.67.refs_0_), channel_id=1, source_target_pairs={{0,7},{1,0},{2,1},{3,2},{4,3},{5,4},{6,5},{7,6},{8,15},{9,8},{10,9... | collective-permute-start | bytes 576008 | tf_op jit(solution)/shard_map/ppermute | solution.py:27
  147.3 7.6 %collective-permute-start.21 = (bf16[128,750]{1,0:T(8,128)(2,1)S(1)}, bf16[128,750]{1,0:T(8,128)(2,1)S(1)}, u32[]{:S(2)}, u32[]{:S(2)}) collective-permute-start(bf16[128,750]{1,0:T(8,128)(2,1)S(1)} %collective-permute-done.19.refs_1_), channel_id=1, source_target_pairs={{0,1},{1,2},{2,3},{3,4},{4,5},{5,6},{6,7},{7,0},{8,9},{9,10},{10,1... | collective-permute-start | bytes 576008 | tf_op jit(solution)/shard_map/ppermute | solution.py:27
  147.3 7.6 %collective-permute-start.22 = (bf16[128,750]{1,0:T(8,128)(2,1)S(1)}, bf16[128,750]{1,0:T(8,128)(2,1)S(1)}, u32[]{:S(2)}, u32[]{:S(2)}) collective-permute-start(bf16[128,750]{1,0:T(8,128)(2,1)S(1)} %collective-permute-done.20.refs_2_), channel_id=1, source_target_pairs={{0,7},{1,0},{2,1},{3,2},{4,3},{5,4},{6,5},{7,6},{8,15},{9,8},{10,9... | collective-permute-start | bytes 576008 | tf_op jit(solution)/shard_map/ppermute | solution.py:27
  154.9 6.9 %collective-permute-start.23 = (bf16[128,750]{1,0:T(8,128)(2,1)S(1)}, bf16[128,750]{1,0:T(8,128)(2,1)S(1)}, u32[]{:S(2)}, u32[]{:S(2)}) collective-permute-start(bf16[128,750]{1,0:T(8,128)(2,1)S(1)} %collective-permute-done.21.refs_3_), channel_id=1, source_target_pairs={{0,1},{1,2},{2,3},{3,4},{4,5},{5,6},{6,7},{7,0},{8,9},{9,10},{10,1... | collective-permute-start | bytes 576008 | tf_op jit(solution)/shard_map/ppermute | solution.py:27
  154.9 7.0 %collective-permute-start.24 = (bf16[128,750]{1,0:T(8,128)(2,1)S(1)}, bf16[128,750]{1,0:T(8,128)(2,1)S(1)}, u32[]{:S(2)}, u32[]{:S(2)}) collective-permute-start(bf16[128,750]{1,0:T(8,128)(2,1)S(1)} %collective-permute-done.22.refs_4_), channel_id=1, source_target_pairs={{0,7},{1,0},{2,1},{3,2},{4,3},{5,4},{6,5},{7,6},{8,15},{9,8},{10,9... | collective-permute-start | bytes 576008 | tf_op jit(solution)/shard_map/ppermute | solution.py:27
  161.8 5.9 %collective-permute-start.25 = (bf16[64,750]{1,0:T(8,128)(2,1)S(1)}, bf16[64,750]{1,0:T(8,128)(2,1)S(1)}, u32[]{:S(2)}, u32[]{:S(2)}) collective-permute-start(bf16[64,750]{1,0:T(8,128)(2,1)S(1)} %slice.18), channel_id=1, source_target_pairs={{0,1},{1,2},{2,3},{3,4},{4,5},{5,6},{6,7},{7,0},{8,9},{9,10},{10,1... | collective-permute-start | bytes 288008 | tf_op jit(solution)/shard_map/ppermute | solution.py:27
  161.9 5.8 %collective-permute-start.26 = (bf16[64,750]{1,0:T(8,128)(2,1)S(1)}, bf16[64,750]{1,0:T(8,128)(2,1)S(1)}, u32[]{:S(2)}, u32[]{:S(2)}) collective-permute-start(bf16[64,750]{1,0:T(8,128)(2,1)S(1)} %slice.19), channel_id=1, source_target_pairs={{0,7},{1,0},{2,1},{3,2},{4,3},{5,4},{6,5},{7,6},{8,15},{9,8},{10,9... | collective-permute-start | bytes 288008 | tf_op jit(solution)/shard_map/ppermute | solution.py:27
where the time goes:
time: 176 us; the launch traced here: 173 us
  starting transfers between devices  71.5 us (41%)
  waiting for transfers between devices  62.1 us (35%)
  blocking collectives  14.8 us (8%)
  Pallas kernels  12.6 us (7%)
  local copies, waits for them, and re-layouts  9.72 us (6%)
    ppermute x24, starting transfers between devices, turn(): lax.ppermute(shard, axis, [(i, (i + step) % size) for i in range(size)])  42.9 us
    ppermute x24, waiting for transfers between devices, turn(): lax.ppermute(shard, axis, [(i, (i + step) % size) for i in range(size)])  38.4 us
    all_to_all x2, starting transfers between devices, exchanged(): return lax.all_to_all(pieces, axis, split_axis=0, concat_axis=0, tiled=True)  28.5 us
    all_to_all x2, waiting for transfers between devices, exchanged(): return lax.all_to_all(pieces, axis, split_axis=0, concat_axis=0, tiled=True)  20.6 us
    all_to_all x1, blocking collectives, exchanged(): return lax.all_to_all(pieces, axis, split_axis=0, concat_axis=0, tiled=True)  14.8 us
    unnamed x21, local copies, waits for them, and re-layouts  6.91 us
    pallas_call x1, Pallas kernels, per_device(): pl.pallas_call(density_kernel, grid=(pl.cdiv(rows, tile),), in_specs=[pl....  5.08 us
  transfers between devices with their start and end apart: 29, of which 15 were waited for; matrix products, arithmetic and copies ran while one was open for 2% of the time, Pallas kernels for 2%

commit v1 on v0

--- a/solution.py
+++ b/solution.py
@@ -1,3 +1,5 @@
+import functools
+
 import jax
 import jax.numpy as jnp
 from jax import lax
@@ -52,33 +54,44 @@
     return lax.dot_general(a, b, ((over[:1], over[1:]), ((), ())), preferred_element_type=WIDE)
 
 
-def image_kernel(at, own, other, pert, turned, first, last, *near):
-    y, k = at[0], at[1]
-    size, share, _ = own.shape
+def turn_and_multiply(at, held, pert, turned, image):
+    size, share, _ = held.shape
     for d in range(size):
-        source = lax.rem(y + d, size)
-        for core, held in ((k, own), (1 - k, other)):
-            start = pl.multiple_of((CORES * d + core) * share, share)
-            turned[pl.ds(start, share), :] = held[source]
-    block = CORES * share
+        turned[d * share : (d + 1) * share, :] = held[lax.rem(at[0] + d, size)]
     for p in range(pert.shape[0]):
-        image = dot(turned[...], pert[p], (1, 1)).astype(NARROW)
+        image[p] = dot(turned[...], pert[p], (1, 1)).astype(NARROW)
+
+
+def own_image_kernel(at, held, pert, turned, image):
+    turn_and_multiply(at, held, pert, turned, image)
+
+
+def image_kernel(at, held, pert, own_image, turned, first, last, *refs):
+    *near, image = refs
+    turn_and_multiply(at, held, pert, turned, image)
+    k = at[1]
+    size, share, _ = held.shape
+    for p in range(pert.shape[0]):
         for d in range(size):
-            part = image[d * block : (d + 1) * block]
-            if d == size // 2:
-                (first, last)[p][...] = part
-            else:
-                near[d - (d > size // 2)][p * block : (p + 1) * block, :] = part
+            for core, source in ((k, own_image), (1 - k, image)):
+                part = source[p, d * share : (d + 1) * share, :]
+                start = pl.multiple_of(core * share, share)
+                if d == size // 2:
+                    (first, last)[p][pl.ds(start, share), :] = part
+                else:
+                    near[d - (d > size // 2)][pl.ds(CORES * p * share + start, share), :] = part
 
 
 def coupling_kernel(at, here, down, up, *refs):
-    *chunks, far_low, far_high, send, keep, image = refs
-    k = at[1]
+    *chunks, far_low, far_high, send, keep, far, image = refs
+    k = at[1]
+    far[: far_low.shape[0], :] = far_low[...]
+    far[far_low.shape[0] :, :] = far_high[...]
     image[...] = (here[...].astype(WIDE) + down[...].astype(WIDE) + up[...].astype(WIDE)).astype(NARROW)
     block = image.shape[0] // CORES
     held = [image[pl.ds(pl.multiple_of(c * block, block), block), :] for c in (1 - k, k)]
     left = jnp.concatenate(held, axis=0)
-    chunks = [c[...] for c in chunks] + [jnp.concatenate([far_low[...], far_high[...]], axis=0)]
+    chunks = [c[...] for c in (*chunks, far)]
     width = chunks[0].shape[1]
     spare = send.shape[2] - width
     for n, chunk in enumerate(chunks):
@@ -99,9 +112,9 @@
 
 
 def mixed_kernel(at, own, other, *refs):
-    *chunks, far_low, far_high, out = refs
-    k = at[1]
-    chunks = [c[...] for c in chunks] + [jnp.concatenate([far_low[...], far_high[...]], axis=0)]
+    *chunks, out = refs
+    k = at[1]
+    chunks = [c[...] for c in chunks]
     width = chunks[0].shape[1]
     total = 0.0
     for n, chunk in enumerate(chunks):
@@ -113,15 +126,27 @@
         out[pl.ds(pl.multiple_of(core * block, block), block), :] = part
 
 
-def density_kernel(turned, *refs):
+def density_kernel(at, turned, other_turned, *refs):
     *pieces, first, last, out = refs
+    k = at[1]
     size = len(pieces) + 1
-    block = first.shape[0]
-    for p in range(out.shape[1]):
-        at_block = {d: piece[p * block : (p + 1) * block, :] for d, piece in zip(ring_order(size), pieces)}
-        at_block[size // 2] = (first, last)[p][...]
-        left = jnp.concatenate([at_block[d] for d in range(size)], axis=0)
-        out[:, p, :] = dot(left, turned[...], (0, 0)).astype(NARROW)
+    share = turned.shape[0] // size
+    tile, rows = out.shape[0], first.shape[1]
+
+    def stretch(low, high):
+        for p in range(out.shape[1]):
+            total = 0.0
+            for core, right in ((k, turned), (1 - k, other_turned)):
+                start = pl.multiple_of(core * share, share)
+                near = pl.ds(CORES * p * share + start, share)
+                at_block = {d: piece[near, low:high] for d, piece in zip(ring_order(size), pieces)}
+                at_block[size // 2] = (first, last)[p][pl.ds(start, share), low:high]
+                left = jnp.concatenate([at_block[d] for d in range(size)], axis=0)
+                total += dot(left, right[...], (0, 0))
+            out[: high - low, p, :] = total.astype(NARROW)
+
+    for n, low in enumerate(range(0, rows, tile)):
+        pl.when(pl.program_id(0) == n)(functools.partial(stretch, low, min(low + tile, rows)))
 
 
 def per_device(perturbation, occ_coeffs, vir_coeffs, occ_energies, vir_energies):
@@ -140,12 +165,23 @@
 
     piece = shape_of(perts * block, rows)
     half = shape_of(block, rows)
-    turned, first, last, *near = pl.pallas_call(
+    kept = pl.BlockSpec(memory_space=pltpu.VMEM)
+    some = shape_of(nx * share, cols)
+    turned, own_image = pl.pallas_call(
+        own_image_kernel,
+        in_specs=[SCALAR, kept, kept],
+        out_specs=[kept, kept],
+        out_shape=[some, shape_of(perts, nx * share, rows)],
+        compiler_params=ROOMY,
+    )(at, own, perturbation)
+    other_turned, first, last, *near = pl.pallas_call(
         image_kernel,
-        in_specs=[SCALAR] + [pl.BlockSpec(memory_space=pltpu.VMEM)] * 3,
-        out_shape=[shape_of(ny * block, cols), half, half] + [piece] * (ny - 1),
-        compiler_params=ROOMY,
-    )(at, own, other, perturbation)
+        in_specs=[SCALAR, kept, kept, kept],
+        out_specs=[kept] * (ny + 2),
+        out_shape=[some, half, half] + [piece] * (ny - 1),
+        scratch_shapes=[pltpu.VMEM((perts, nx * share, rows), NARROW)],
+        compiler_params=ROOMY,
+    )(at, other, perturbation, own_image)
     down, up = turn(first, "y", 1), turn(last, "y", -1)
     down = jnp.pad(down, [(0, block), (0, 0)])
     up = jnp.pad(up, [(block, 0), (0, 0)])
@@ -154,10 +190,15 @@
         up = turn((near[-d].astype(WIDE) + up).astype(NARROW), "y", -1)
 
     wide_occ = up_to(own_occ, LANES)
-    send, keep = pl.pallas_call(
+    send, keep, far = pl.pallas_call(
         coupling_kernel,
-        in_specs=[SCALAR] + [pl.BlockSpec(memory_space=pltpu.VMEM)] * (3 + len(occ)),
-        out_shape=[shape_of(ny, block, wide_occ), shape_of(ny, block, wide_occ, dtype=WIDE)],
+        in_specs=[SCALAR] + [kept] * (3 + len(occ)),
+        out_specs=[kept] * 3,
+        out_shape=[
+            shape_of(ny, block, wide_occ),
+            shape_of(ny, block, wide_occ, dtype=WIDE),
+            shape_of(*occ_coeffs.shape),
+        ],
         scratch_shapes=[pltpu.VMEM((perts * block, rows), NARROW)],
         compiler_params=ROOMY,
     )(at, near[0], down, up, *occ)
@@ -175,22 +216,22 @@
     sibling = lax.ppermute(response, "k", SWAP)
     mixed = pl.pallas_call(
         mixed_kernel,
-        in_specs=[SCALAR] + [pl.BlockSpec(memory_space=pltpu.VMEM)] * (2 + len(occ)),
+        in_specs=[SCALAR] + [kept] * (1 + len(occ)),
+        out_specs=kept,
         out_shape=piece,
         compiler_params=ROOMY,
-    )(at, response, sibling, *occ)
+    )(at, response, sibling, *occ[:-2], far)
 
     pieces = ring_gather(mixed, "y", block)
     tile = 2 * LANES
-    narrow = [pl.BlockSpec((p.shape[0], tile), lambda i: (0, i)) for p in pieces]
     total = pl.pallas_call(
         density_kernel,
         grid=(pl.cdiv(rows, tile),),
-        in_specs=[pl.BlockSpec(turned.shape, lambda i: (0, 0))] + narrow,
+        in_specs=[SCALAR] + [kept] * (2 + len(pieces)),
         out_specs=pl.BlockSpec((tile, perts, cols), lambda i: (i, 0, 0)),
         out_shape=shape_of(rows, perts, cols),
         compiler_params=ROOMY,
-    )(turned, *pieces)
+    )(at, turned, other_turned, *pieces)
     return jnp.transpose(total, (1, 0, 2))
 
 

time: 176 us -> 175 us (level)
  waiting for transfers between devices: 62.1 us -> 66.9 us
  local copies, waits for them, and re-layouts: 9.72 us -> 5.77 us
  starting transfers between devices: 71.5 us -> 69.5 us
    ppermute x24, waiting for transfers between devices: 38.4 us -> 43 us  [turn(): lax.ppermute(shard, axis, [(i, (i + step) % size) for i in range(size)])]
    unnamed x21 -> x17, local copies, waits for them, and re-layouts: 6.91 us -> 3.06 us
    ppermute x24, starting transfers between devices: 42.9 us -> 40.8 us  [turn(): lax.ppermute(shard, axis, [(i, (i + step) % size) for i in range(size)])]
    pallas_call x4 -> x5, Pallas kernels: 12.5 us -> 12.6 us  [the longest x1 5.72 us: per_device(): pl.pallas_call(density_kernel, grid=(pl.cdiv(rows, tile),), in_specs=[SCA...]
where the time goes in v1:
time: 175 us; the launch traced here: 172 us
  starting transfers between devices  69.5 us (40%)
  waiting for transfers between devices  66.9 us (38%)
  blocking collectives  14.9 us (9%)
  Pallas kernels  12.6 us (7%)
  local copies, waits for them, and re-layouts  5.77 us (3%)
    ppermute x24, waiting for transfers between devices, turn(): lax.ppermute(shard, axis, [(i, (i + step) % size) for i in range(size)])  43 us
    ppermute x24, starting transfers between devices, turn(): lax.ppermute(shard, axis, [(i, (i + step) % size) for i in range(size)])  40.8 us
    all_to_all x2, starting transfers between devices, exchanged(): return lax.all_to_all(pieces, axis, split_axis=0, concat_axis=0, tiled=True)  28.5 us
    all_to_all x2, waiting for transfers between devices, exchanged(): return lax.all_to_all(pieces, axis, split_axis=0, concat_axis=0, tiled=True)  20.9 us
    all_to_all x1, blocking collectives, exchanged(): return lax.all_to_all(pieces, axis, split_axis=0, concat_axis=0, tiled=True)  14.9 us
    pallas_call x1, Pallas kernels, per_device(): pl.pallas_call(density_kernel, grid=(pl.cdiv(rows, tile),), in_specs=[SCA...  5.72 us
  transfers between devices with their start and end apart: 29, of which 15 were waited for; matrix products, arithmetic and copies ran while one was open for 2% of the time, Pallas kernels for 2%

profile of v1, /device:TPU:516, one launch (start us, length us, event | category | flops | bytes accessed | tf_op | source)
XLA Modules:
  0.0 171.7 jit_solution(10517804004454340124)
XLA Ops:
  0.0 1.8 %broadcast_in_dim.6 = bf16[8,32,1500]{2,1,0:T(8,128)(2,1)} broadcast(bf16[32,1500]{1,0:T(8,128)(2,1)} %bitcast.7), dimensions={1,2} | broadcast | bytes 864000 | tf_op jit(solution)/shard_map/broadcast_in_dim | solution.py:163
  1.9 22.7 %all-to-all-start = ((bf16[8,32,1500]{2,1,0:T(8,128)(2,1)}), bf16[8,32,1500]{2,1,0:T(8,128)(2,1)S(1)}, u32[]{:S(2)}, u32[]{:S(2)}) async-start(bf16[8,32,1500]{2,1,0:T(8,128)(2,1)} %broadcast_in_dim.6), calls=%async_computation | async-start | bytes 1572864 | tf_op jit(solution)/shard_map/all_to_all | solution.py:50
  24.6 0.0 collective-permute-start.9
  24.6 12.8 %all-to-all-done.held = bf16[8,32,1500]{2,1,0:T(8,128)(2,1)S(1)} async-done(((bf16[8,32,1500]{2,1,0:T(8,128)(2,1)}), bf16[8,32,1500]{2,1,0:T(8,128)(2,1)S(1)}, u32[]{:S(2)}, u32[]{:S(2)}) %all-to-all-start) | async-done | bytes 768032 | tf_op jit(solution)/shard_map/all_to_all | solution.py:50
  37.4 0.0 collective-permute-start
  37.4 4.6 %collective-permute-start.10 = (bf16[750,250]{1,0:T(8,128)(2,1)}, bf16[750,250]{1,0:T(8,128)(2,1)S(1)}, u32[]{:S(2)}, u32[]{:S(2)}) collective-permute-start(bf16[750,250]{1,0:T(8,128)(2,1)} %refs_0_.3), channel_id=1, source_target_pairs={{0,7},{1,0},{2,1},{3,2},{4,3},{5,4},{6,5},{7,6},{8,15},{9,8},{10,9... | collective-permute-start | bytes 1125008 | tf_op jit(solution)/shard_map/ppermute | solution.py:29
  42.0 0.0 collective-permute-done.9.refs_1_
  42.0 0.0 collective-permute-start.11
  42.0 9.2 %collective-permute-done.10.refs_2_ = bf16[750,250]{1,0:T(8,128)(2,1)S(1)} collective-permute-done((bf16[750,250]{1,0:T(8,128)(2,1)}, bf16[750,250]{1,0:T(8,128)(2,1)S(1)}, u32[]{:S(2)}, u32[]{:S(2)}) %collective-permute-start.10) | collective-permute-done | bytes 375032 | tf_op jit(solution)/shard_map/ppermute | solution.py:29
  51.2 3.6 %collective-permute-start.12 = (bf16[750,250]{1,0:T(8,128)(2,1)S(1)}, bf16[750,250]{1,0:T(8,128)(2,1)S(1)}, u32[]{:S(2)}, u32[]{:S(2)}) collective-permute-start(bf16[750,250]{1,0:T(8,128)(2,1)S(1)} %collective-permute-done.10.refs_2_), channel_id=1, source_target_pairs={{0,7},{1,0},{2,1},{3,2},{4,3},{5,4},{6,5},{7,6},{8,15},{9,8},{10,9... | collective-permute-start | bytes 1125008 | tf_op jit(solution)/shard_map/ppermute | solution.py:29
  54.7 3.0 %copy.7.pert = bf16[2,750,1500]{2,1,0:T(8,128)(2,1)S(1)} copy(bf16[2,750,1500]{2,0,1:T(2,128)(2,1)} %param.6) | data formatting | bytes 9000000 | tf_op args[0]
  57.8 0.1 pad_add_fusion.at
  57.9 2.0 %shard_map.64 = (bf16[256,1500]{1,0:T(8,128)(2,1)S(1)}, bf16[2,256,750]{2,1,0:T(8,128)(2,1)S(1)}) custom-call(s32[2]{0:T(128)S(1)} %pad_add_fusion.at, bf16[8,32,1500]{2,1,0:T(8,128)(2,1)S(1)} %all-to-all-done.held, bf16[2,750,1500]{2,1,0:T(8,128)(2,1)S(1)} %copy.7.pert), custom_call_target="tpu_custom_call" | custom-call | tf_op jit(solution)/shard_map/pallas_call | solution.py:170
  59.8 0.0 copy-start.2
  59.8 0.0 copy-start.1
  59.9 2.0 %shard_map.65 = (bf16[256,1500]{1,0:T(8,128)(2,1)S(1)}, bf16[64,750]{1,0:T(8,128)(2,1)S(1)}, bf16[64,750]{1,0:T(8,128)(2,1)S(1)}, bf16[128,750]{1,0:T(8,128)(2,1...) custom-call(s32[2]{0:T(128)S(1)} %pad_add_fusion.at, ...), custom_call_target="tpu_custom_call" | custom-call | tf_op jit(solution)/shard_map/pallas_call | solution.py:177
  61.9 0.0 copy-start.7
  61.9 0.1 collective-permute-start.1
  62.1 0.7 collective-permute-done.12.refs_4_
  62.8 3.7 %collective-permute-start.14 = (bf16[750,250]{1,0:T(8,128)(2,1)S(1)}, bf16[750,250]{1,0:T(8,128)(2,1)S(1)}, u32[]{:S(2)}, u32[]{:S(2)}) collective-permute-start(bf16[750,250]{1,0:T(8,128)(2,1)S(1)} %collective-permute-done.12.refs_4_), channel_id=1, source_target_pairs={{0,7},{1,0},{2,1},{3,2},{4,3},{5,4},{6,5},{7,6},{8,15},{9,8},{10,9... | collective-permute-start | bytes 1125008 | tf_op jit(solution)/shard_map/ppermute | solution.py:29
  66.4 0.7 collective-permute-done.13.refs_5_
  67.1 0.0 copy-start.6
  67.1 0.1 collective-permute-start.15
  67.3 3.2 %collective-permute-start.5 = (bf16[64,750]{1,0:T(8,128)(2,1)S(1)}, bf16[64,750]{1,0:T(8,128)(2,1)S(1)}, u32[]{:S(2)}, u32[]{:S(2)}) collective-permute-start(bf16[64,750]{1,0:T(8,128)(2,1)S(1)} %get-tuple-element.31), channel_id=1, source_target_pairs={{0,7},{1,0},{2,1},{3,2},{4,3},{5,4},{6,5},{7,6},{8,15},{9,8},{10,9... | collective-permute-start | bytes 288008 | tf_op jit(solution)/shard_map/ppermute | solution.py:29
  70.5 0.1 collective-permute-start.2
  70.7 5.0 %collective-permute-done.5 = bf16[64,750]{1,0:T(8,128)(2,1)S(1)} collective-permute-done((bf16[64,750]{1,0:T(8,128)(2,1)S(1)}, bf16[64,750]{1,0:T(8,128)(2,1)S(1)}, u32[]{:S(2)}, u32[]{:S(2)}) %collective-permute-start.5) | collective-permute-done | bytes 96032 | tf_op jit(solution)/shard_map/ppermute | solution.py:29
  75.7 4.0 %collective-permute-start.6 = (bf16[128,750]{1,0:T(8,128)(2,1)S(1)}, bf16[128,750]{1,0:T(8,128)(2,1)S(1)}, u32[]{:S(2)}, u32[]{:S(2)}) collective-permute-start(bf16[128,750]{1,0:T(8,128)(2,1)S(1)} %add_convert_fusion.3), channel_id=1, source_target_pairs={{0,7},{1,0},{2,1},{3,2},{4,3},{5,4},{6,5},{7,6},{8,15},{9,8},{10,9... | collective-permute-start | bytes 576008 | tf_op jit(solution)/shard_map/ppermute | solution.py:29
  79.7 0.0 collective-permute-done.2
  79.8 0.1 collective-permute-start.3
  79.9 3.0 %collective-permute-done.6 = bf16[128,750]{1,0:T(8,128)(2,1)S(1)} collective-permute-done((bf16[128,750]{1,0:T(8,128)(2,1)S(1)}, bf16[128,750]{1,0:T(8,128)(2,1)S(1)}, u32[]{:S(2)}, u32[]{:S(2)}) %collective-permute-start.6) | collective-permute-done | bytes 192032 | tf_op jit(solution)/shard_map/ppermute | solution.py:29
  83.0 3.8 %collective-permute-start.7 = (bf16[128,750]{1,0:T(8,128)(2,1)S(1)}, bf16[128,750]{1,0:T(8,128)(2,1)S(1)}, u32[]{:S(2)}, u32[]{:S(2)}) collective-permute-start(bf16[128,750]{1,0:T(8,128)(2,1)S(1)} %add_convert_fusion.2), channel_id=1, source_target_pairs={{0,7},{1,0},{2,1},{3,2},{4,3},{5,4},{6,5},{7,6},{8,15},{9,8},{10,9... | collective-permute-start | bytes 576008 | tf_op jit(solution)/shard_map/ppermute | solution.py:29
  86.8 0.0 collective-permute-done.3
  86.8 0.1 collective-permute-start.4
  87.0 3.4 %collective-permute-done.7 = bf16[128,750]{1,0:T(8,128)(2,1)S(1)} collective-permute-done((bf16[128,750]{1,0:T(8,128)(2,1)S(1)}, bf16[128,750]{1,0:T(8,128)(2,1)S(1)}, u32[]{:S(2)}, u32[]{:S(2)}) %collective-permute-start.7) | collective-permute-done | bytes 192032 | tf_op jit(solution)/shard_map/ppermute | solution.py:29
  90.4 3.8 %collective-permute-start.8 = (bf16[128,750]{1,0:T(8,128)(2,1)S(1)}, bf16[128,750]{1,0:T(8,128)(2,1)S(1)}, u32[]{:S(2)}, u32[]{:S(2)}) collective-permute-start(bf16[128,750]{1,0:T(8,128)(2,1)S(1)} %add_convert_fusion.1), channel_id=1, source_target_pairs={{0,7},{1,0},{2,1},{3,2},{4,3},{5,4},{6,5},{7,6},{8,15},{9,8},{10,9... | collective-permute-start | bytes 576008 | tf_op jit(solution)/shard_map/ppermute | solution.py:29
  94.2 0.2 collective-permute-start.16
  94.4 5.5 %collective-permute-done.16.refs_8_ = bf16[366,250]{1,0:T(8,128)(2,1)S(1)} collective-permute-done((bf16[366,250]{1,0:T(8,128)(2,1)S(1)}, bf16[366,250]{1,0:T(8,128)(2,1)S(1)}, u32[]{:S(2)}, u32[]{:S(2)}) %collective-permute-start.16) | collective-permute-done | bytes 183032 | tf_op jit(solution)/shard_map/ppermute | solution.py:29
  99.9 0.0 collective-permute-done.15.refs_7_
  99.9 0.0 collective-permute-done.4.down
  99.9 1.2 shard_map.66
  101.2 0.1 collective-permute-start.17
  101.4 1.5 collective-permute-done.17
  102.9 0.8 add_convert_fusion
  103.6 5.8 %all-to-all-start.1 = ((bf16[8,64,256]{2,1,0:T(8,128)(2,1)}), bf16[8,64,256]{2,1,0:T(8,128)(2,1)S(1)}, u32[]{:S(2)}, u32[]{:S(2)}) async-start(bf16[8,64,256]{2,1,0:T(8,128)(2,1)} %add_convert_fusion), calls=%async_computation.1 | async-start | bytes 524288 | tf_op jit(solution)/shard_map/all_to_all | solution.py:50
  109.5 0.6 dynamic_slice.9
  110.6 0.1 reshape.3
  110.7 0.1 dynamic-slice_bitcast_fusion
  110.8 0.1 copy.9.virtual
  110.9 8.1 %all-to-all-done.1.terms = bf16[8,64,256]{2,1,0:T(8,128)(2,1)S(1)} async-done(((bf16[8,64,256]{2,1,0:T(8,128)(2,1)}), bf16[8,64,256]{2,1,0:T(8,128)(2,1)S(1)}, u32[]{:S(2)}, u32[]{:S(2)}) %all-to-all-start.1) | async-done | bytes 262176 | tf_op jit(solution)/shard_map/all_to_all | solution.py:50
  119.0 0.1 shard_map.67
  119.0 14.9 %all_to_all.15.own = bf16[8,64,256]{2,1,0:T(8,128)(2,1)S(1)} all-to-all(bf16[8,64,256]{2,1,0:T(8,128)(2,1)S(1)} %shard_map.67), channel_id=1, replica_groups=mesh['grp'=2,'x'=8,'k'=2,'y'=8] {'x'}, dimensions={0} | all-to-all | bytes 524288 | tf_op jit(solution)/shard_map/all_to_all | solution.py:50
  134.0 1.5 collective-permute-done.18.other
  135.5 1.6 shard_map.68.refs_0_
  137.1 0.1 collective-permute-start.19
  137.2 3.3 %collective-permute-start.20 = (bf16[128,750]{1,0:T(8,128)(2,1)S(1)}, bf16[128,750]{1,0:T(8,128)(2,1)S(1)}, u32[]{:S(2)}, u32[]{:S(2)}) collective-permute-start(bf16[128,750]{1,0:T(8,128)(2,1)S(1)} %shard_map.68.refs_0_), channel_id=1, source_target_pairs={{0,7},{1,0},{2,1},{3,2},{4,3},{5,4},{6,5},{7,6},{8,15},{9,8},{10,9... | collective-permute-start | bytes 576008 | tf_op jit(solution)/shard_map/ppermute | solution.py:29
  140.5 5.1 %collective-permute-done.19.refs_1_ = bf16[128,750]{1,0:T(8,128)(2,1)S(1)} collective-permute-done((bf16[128,750]{1,0:T(8,128)(2,1)S(1)}, bf16[128,750]{1,0:T(8,128)(2,1)S(1)}, u32[]{:S(2)}, u32[]{:S(2)}) %collective-permute-start.19) | collective-permute-done | bytes 192032 | tf_op jit(solution)/shard_map/ppermute | solution.py:29
  145.6 3.2 %collective-permute-start.22 = (bf16[128,750]{1,0:T(8,128)(2,1)S(1)}, bf16[128,750]{1,0:T(8,128)(2,1)S(1)}, u32[]{:S(2)}, u32[]{:S(2)}) collective-permute-start(bf16[128,750]{1,0:T(8,128)(2,1)S(1)} %collective-permute-done.20.refs_2_), channel_id=1, source_target_pairs={{0,7},{1,0},{2,1},{3,2},{4,3},{5,4},{6,5},{7,6},{8,15},{9,8},{10,9... | collective-permute-start | bytes 576008 | tf_op jit(solution)/shard_map/ppermute | solution.py:29
  148.8 4.3 %collective-permute-done.21.refs_3_ = bf16[128,750]{1,0:T(8,128)(2,1)S(1)} collective-permute-done((bf16[128,750]{1,0:T(8,128)(2,1)S(1)}, bf16[128,750]{1,0:T(8,128)(2,1)S(1)}, u32[]{:S(2)}, u32[]{:S(2)}) %collective-permute-start.21) | collective-permute-done | bytes 192032 | tf_op jit(solution)/shard_map/ppermute | solution.py:29
  153.2 3.2 %collective-permute-start.24 = (bf16[128,750]{1,0:T(8,128)(2,1)S(1)}, bf16[128,750]{1,0:T(8,128)(2,1)S(1)}, u32[]{:S(2)}, u32[]{:S(2)}) collective-permute-start(bf16[128,750]{1,0:T(8,128)(2,1)S(1)} %collective-permute-done.22.refs_4_), channel_id=1, source_target_pairs={{0,7},{1,0},{2,1},{3,2},{4,3},{5,4},{6,5},{7,6},{8,15},{9,8},{10,9... | collective-permute-start | bytes 576008 | tf_op jit(solution)/shard_map/ppermute | solution.py:29
  156.4 3.6 %collective-permute-done.23.refs_5_ = bf16[128,750]{1,0:T(8,128)(2,1)S(1)} collective-permute-done((bf16[128,750]{1,0:T(8,128)(2,1)S(1)}, bf16[128,750]{1,0:T(8,128)(2,1)S(1)}, u32[]{:S(2)}, u32[]{:S(2)}) %collective-permute-start.23) | collective-permute-done | bytes 192032 | tf_op jit(solution)/shard_map/ppermute | solution.py:29
  160.0 0.1 collective-permute-start.25
  160.2 3.3 %collective-permute-start.26 = (bf16[64,750]{1,0:T(8,128)(2,1)S(1)}, bf16[64,750]{1,0:T(8,128)(2,1)S(1)}, u32[]{:S(2)}, u32[]{:S(2)}) collective-permute-start(bf16[64,750]{1,0:T(8,128)(2,1)S(1)} %slice.19), channel_id=1, source_target_pairs={{0,7},{1,0},{2,1},{3,2},{4,3},{5,4},{6,5},{7,6},{8,15},{9,8},{10,9... | collective-permute-start | bytes 288008 | tf_op jit(solution)/shard_map/ppermute | solution.py:29
  163.5 2.5 %collective-permute-done.25.refs_7_ = bf16[64,750]{1,0:T(8,128)(2,1)S(1)} collective-permute-done((bf16[64,750]{1,0:T(8,128)(2,1)S(1)}, bf16[64,750]{1,0:T(8,128)(2,1)S(1)}, u32[]{:S(2)}, u32[]{:S(2)}) %collective-permute-start.25) | collective-permute-done | bytes 96032 | tf_op jit(solution)/shard_map/ppermute | solution.py:29
  166.0 5.7 %shard_map.69 = bf16[750,2,1500]{2,1,0:T(2,128)(2,1)} custom-call(s32[2]{0:T(128)S(1)} %pad_add_fusion.at, bf16[256,1500]{1,0:T(8,128)(2,1)S(1)} %copy-done.3, bf16[256,1500]{1,0:T(8,128)(2,1)S(1)} %copy-done.5, bf16[128,750]{1,0:T(8,128)(2,1)S(1)} %shard_map.68.refs_0_, bf16[128,750]{1,0:T(8,128)(2,1)S(1)} %collective-permute-done.19.refs_1_, ...), custom_call_target="tpu_custom_call" | custom-call | tf_op jit(solution)/shard_map/pallas_call | solution.py:227
  (36 shorter events, 0.4 us)
Async XLA Ops:
  0.0 110.7 %copy-start = (f32[512]{0:T(512)S(1)}, f32[512]{0:T(512)}, u32[]{:S(2)}) copy-start(f32[512]{0:T(512)} %param.10) | copy-start | bytes 6148
  1.9 35.5 %all-to-all-start = ((bf16[8,32,1500]{2,1,0:T(8,128)(2,1)}), bf16[8,32,1500]{2,1,0:T(8,128)(2,1)S(1)}, u32[]{:S(2)}, u32[]{:S(2)}) async-start(bf16[8,32,1500]{2,1,0:T(8,128)(2,1)} %broadcast_in_dim.6), calls=%async_computation | async-start | bytes 1572864 | tf_op jit(solution)/shard_map/all_to_all | solution.py:50
  24.6 17.4 %collective-permute-start.9 = (bf16[750,250]{1,0:T(8,128)(2,1)}, bf16[750,250]{1,0:T(8,128)(2,1)S(1)}, u32[]{:S(2)}, u32[]{:S(2)}) collective-permute-start(bf16[750,250]{1,0:T(8,128)(2,1)} %refs_0_.3), channel_id=1, source_target_pairs={{0,1},{1,2},{2,3},{3,4},{4,5},{5,6},{6,7},{7,0},{8,9},{9,10},{10,1... | collective-permute-start | bytes 1125008 | tf_op jit(solution)/shard_map/ppermute | solution.py:29
  37.4 22.5 %collective-permute-start = (bf16[8,32,1500]{2,1,0:T(8,128)(2,1)S(1)}, bf16[8,32,1500]{2,1,0:T(8,128)(2,1)S(1)}, u32[]{:S(2)}, u32[]{:S(2)}) collective-permute-start(bf16[8,32,1500]{2,1,0:T(8,128)(2,1)S(1)} %all-to-all-done.held), channel_id=1, source_target_pairs={{0,8},{8,0},{1,9},{9,1},{2,10},{10,2},{3,11},{11,3},{4,12},{12,4},... | collective-permute-start | bytes 2304008 | tf_op jit(solution)/shard_map/ppermute | solution.py:164
  37.4 13.8 %collective-permute-start.10 = (bf16[750,250]{1,0:T(8,128)(2,1)}, bf16[750,250]{1,0:T(8,128)(2,1)S(1)}, u32[]{:S(2)}, u32[]{:S(2)}) collective-permute-start(bf16[750,250]{1,0:T(8,128)(2,1)} %refs_0_.3), channel_id=1, source_target_pairs={{0,7},{1,0},{2,1},{3,2},{4,3},{5,4},{6,5},{7,6},{8,15},{9,8},{10,9... | collective-permute-start | bytes 1125008 | tf_op jit(solution)/shard_map/ppermute | solution.py:29
  42.0 12.8 %collective-permute-start.11 = (bf16[750,250]{1,0:T(8,128)(2,1)S(1)}, bf16[750,250]{1,0:T(8,128)(2,1)S(1)}, u32[]{:S(2)}, u32[]{:S(2)}) collective-permute-start(bf16[750,250]{1,0:T(8,128)(2,1)S(1)} %collective-permute-done.9.refs_1_), channel_id=1, source_target_pairs={{0,1},{1,2},{2,3},{3,4},{4,5},{5,6},{6,7},{7,0},{8,9},{9,10},{10,1... | collective-permute-start | bytes 1125008 | tf_op jit(solution)/shard_map/ppermute | solution.py:29
  51.2 11.6 %collective-permute-start.12 = (bf16[750,250]{1,0:T(8,128)(2,1)S(1)}, bf16[750,250]{1,0:T(8,128)(2,1)S(1)}, u32[]{:S(2)}, u32[]{:S(2)}) collective-permute-start(bf16[750,250]{1,0:T(8,128)(2,1)S(1)} %collective-permute-done.10.refs_2_), channel_id=1, source_target_pairs={{0,7},{1,0},{2,1},{3,2},{4,3},{5,4},{6,5},{7,6},{8,15},{9,8},{10,9... | collective-permute-start | bytes 1125008 | tf_op jit(solution)/shard_map/ppermute | solution.py:29
  54.7 12.4 %collective-permute-start.13 = (bf16[750,250]{1,0:T(8,128)(2,1)S(1)}, bf16[750,250]{1,0:T(8,128)(2,1)S(1)}, u32[]{:S(2)}, u32[]{:S(2)}) collective-permute-start(bf16[750,250]{1,0:T(8,128)(2,1)S(1)} %collective-permute-done.11.refs_3_), channel_id=1, source_target_pairs={{0,1},{1,2},{2,3},{3,4},{4,5},{5,6},{6,7},{7,0},{8,9},{9,10},{10,1... | collective-permute-start | bytes 1125008 | tf_op jit(solution)/shard_map/ppermute | solution.py:29
  59.8 27.0 %copy-start.2 = (bf16[256,1500]{1,0:T(8,128)(2,1)}, bf16[256,1500]{1,0:T(8,128)(2,1)S(1)}, u32[]{:S(2)}) copy-start(bf16[256,1500]{1,0:T(8,128)(2,1)S(1)} %get-tuple-element.20.turned) | copy-start | bytes 2304004
  59.8 40.1 %copy-start.1 = (bf16[750,250]{1,0:T(8,128)(2,1)S(1)}, bf16[750,250]{1,0:T(8,128)(2,1)}, u32[]{:S(2)}) copy-start(bf16[750,250]{1,0:T(8,128)(2,1)} %refs_0_.3) | copy-start | bytes 1125004
  61.9 32.3 %copy-start.4 = (bf16[256,1500]{1,0:T(8,128)(2,1)}, bf16[256,1500]{1,0:T(8,128)(2,1)S(1)}, u32[]{:S(2)}) copy-start(bf16[256,1500]{1,0:T(8,128)(2,1)S(1)} %get-tuple-element.22.other_turned) | copy-start | bytes 2304004
  61.9 47.6 %copy-start.7 = (s32[8]{0:T(128)S(1)}, s32[8]{0:T(128)}, u32[]{:S(2)}) copy-start(s32[8]{0:T(128)} %constant.37.clone) | copy-start | bytes 100
  61.9 8.6 %collective-permute-start.1 = (bf16[64,750]{1,0:T(8,128)(2,1)S(1)}, bf16[64,750]{1,0:T(8,128)(2,1)S(1)}, u32[]{:S(2)}, u32[]{:S(2)}) collective-permute-start(bf16[64,750]{1,0:T(8,128)(2,1)S(1)} %get-tuple-element.27), channel_id=1, source_target_pairs={{0,1},{1,2},{2,3},{3,4},{4,5},{5,6},{6,7},{7,0},{8,9},{9,10},{10,1... | collective-permute-start | bytes 288008 | tf_op jit(solution)/shard_map/ppermute | solution.py:29
  62.8 31.5 %collective-permute-start.14 = (bf16[750,250]{1,0:T(8,128)(2,1)S(1)}, bf16[750,250]{1,0:T(8,128)(2,1)S(1)}, u32[]{:S(2)}, u32[]{:S(2)}) collective-permute-start(bf16[750,250]{1,0:T(8,128)(2,1)S(1)} %collective-permute-done.12.refs_4_), channel_id=1, source_target_pairs={{0,7},{1,0},{2,1},{3,2},{4,3},{5,4},{6,5},{7,6},{8,15},{9,8},{10,9... | collective-permute-start | bytes 1125008 | tf_op jit(solution)/shard_map/ppermute | solution.py:29
  67.1 43.5 %copy-start.6 = (f32[2000]{0:T(1024)S(1)}, f32[2000]{0:T(1024)}, u32[]{:S(2)}) copy-start(f32[2000]{0:T(1024)} %param.9) | copy-start | bytes 24004
  67.1 32.8 %collective-permute-start.15 = (bf16[384,250]{1,0:T(8,128)(2,1)S(1)}, bf16[384,250]{1,0:T(8,128)(2,1)S(1)}, u32[]{:S(2)}, u32[]{:S(2)}) collective-permute-start(bf16[384,250]{1,0:T(8,128)(2,1)S(1)} %slice.16), channel_id=1, source_target_pairs={{0,1},{1,2},{2,3},{3,4},{4,5},{5,6},{6,7},{7,0},{8,9},{9,10},{10,1... | collective-permute-start | bytes 576008 | tf_op jit(solution)/shard_map/ppermute | solution.py:29
  67.3 8.4 %collective-permute-start.5 = (bf16[64,750]{1,0:T(8,128)(2,1)S(1)}, bf16[64,750]{1,0:T(8,128)(2,1)S(1)}, u32[]{:S(2)}, u32[]{:S(2)}) collective-permute-start(bf16[64,750]{1,0:T(8,128)(2,1)S(1)} %get-tuple-element.31), channel_id=1, source_target_pairs={{0,7},{1,0},{2,1},{3,2},{4,3},{5,4},{6,5},{7,6},{8,15},{9,8},{10,9... | collective-permute-start | bytes 288008 | tf_op jit(solution)/shard_map/ppermute | solution.py:29
  70.5 9.2 %collective-permute-start.2 = (bf16[128,750]{1,0:T(8,128)(2,1)S(1)}, bf16[128,750]{1,0:T(8,128)(2,1)S(1)}, u32[]{:S(2)}, u32[]{:S(2)}) collective-permute-start(bf16[128,750]{1,0:T(8,128)(2,1)S(1)} %add_convert_fusion.6), channel_id=1, source_target_pairs={{0,1},{1,2},{2,3},{3,4},{4,5},{5,6},{6,7},{7,0},{8,9},{9,10},{10,1... | collective-permute-start | bytes 576008 | tf_op jit(solution)/shard_map/ppermute | solution.py:29
  75.7 7.2 %collective-permute-start.6 = (bf16[128,750]{1,0:T(8,128)(2,1)S(1)}, bf16[128,750]{1,0:T(8,128)(2,1)S(1)}, u32[]{:S(2)}, u32[]{:S(2)}) collective-permute-start(bf16[128,750]{1,0:T(8,128)(2,1)S(1)} %add_convert_fusion.3), channel_id=1, source_target_pairs={{0,7},{1,0},{2,1},{3,2},{4,3},{5,4},{6,5},{7,6},{8,15},{9,8},{10,9... | collective-permute-start | bytes 576008 | tf_op jit(solution)/shard_map/ppermute | solution.py:29
  79.8 7.0 %collective-permute-start.3 = (bf16[128,750]{1,0:T(8,128)(2,1)S(1)}, bf16[128,750]{1,0:T(8,128)(2,1)S(1)}, u32[]{:S(2)}, u32[]{:S(2)}) collective-permute-start(bf16[128,750]{1,0:T(8,128)(2,1)S(1)} %add_convert_fusion.5), channel_id=1, source_target_pairs={{0,1},{1,2},{2,3},{3,4},{4,5},{5,6},{6,7},{7,0},{8,9},{9,10},{10,1... | collective-permute-start | bytes 576008 | tf_op jit(solution)/shard_map/ppermute | solution.py:29
  83.0 7.4 %collective-permute-start.7 = (bf16[128,750]{1,0:T(8,128)(2,1)S(1)}, bf16[128,750]{1,0:T(8,128)(2,1)S(1)}, u32[]{:S(2)}, u32[]{:S(2)}) collective-permute-start(bf16[128,750]{1,0:T(8,128)(2,1)S(1)} %add_convert_fusion.2), channel_id=1, source_target_pairs={{0,7},{1,0},{2,1},{3,2},{4,3},{5,4},{6,5},{7,6},{8,15},{9,8},{10,9... | collective-permute-start | bytes 576008 | tf_op jit(solution)/shard_map/ppermute | solution.py:29
  86.8 13.1 %collective-permute-start.4 = (bf16[128,750]{1,0:T(8,128)(2,1)S(1)}, bf16[128,750]{1,0:T(8,128)(2,1)S(1)}, u32[]{:S(2)}, u32[]{:S(2)}) collective-permute-start(bf16[128,750]{1,0:T(8,128)(2,1)S(1)} %add_convert_fusion.4), channel_id=1, source_target_pairs={{0,1},{1,2},{2,3},{3,4},{4,5},{5,6},{6,7},{7,0},{8,9},{9,10},{10,1... | collective-permute-start | bytes 576008 | tf_op jit(solution)/shard_map/ppermute | solution.py:29
  90.4 9.5 %collective-permute-start.8 = (bf16[128,750]{1,0:T(8,128)(2,1)S(1)}, bf16[128,750]{1,0:T(8,128)(2,1)S(1)}, u32[]{:S(2)}, u32[]{:S(2)}) collective-permute-start(bf16[128,750]{1,0:T(8,128)(2,1)S(1)} %add_convert_fusion.1), channel_id=1, source_target_pairs={{0,7},{1,0},{2,1},{3,2},{4,3},{5,4},{6,5},{7,6},{8,15},{9,8},{10,9... | collective-permute-start | bytes 576008 | tf_op jit(solution)/shard_map/ppermute | solution.py:29
  94.2 5.7 %collective-permute-start.16 = (bf16[366,250]{1,0:T(8,128)(2,1)S(1)}, bf16[366,250]{1,0:T(8,128)(2,1)S(1)}, u32[]{:S(2)}, u32[]{:S(2)}) collective-permute-start(bf16[366,250]{1,0:T(8,128)(2,1)S(1)} %slice.17), channel_id=1, source_target_pairs={{0,7},{1,0},{2,1},{3,2},{4,3},{5,4},{6,5},{7,6},{8,15},{9,8},{10,9... | collective-permute-start | bytes 549008 | tf_op jit(solution)/shard_map/ppermute | solution.py:29
  101.2 1.7 collective-permute-start.17
  103.6 15.3 %all-to-all-start.1 = ((bf16[8,64,256]{2,1,0:T(8,128)(2,1)}), bf16[8,64,256]{2,1,0:T(8,128)(2,1)S(1)}, u32[]{:S(2)}, u32[]{:S(2)}) async-start(bf16[8,64,256]{2,1,0:T(8,128)(2,1)} %add_convert_fusion), calls=%async_computation.1 | async-start | bytes 524288 | tf_op jit(solution)/shard_map/all_to_all | solution.py:50
  118.9 47.0 %copy-start.3 = (bf16[256,1500]{1,0:T(8,128)(2,1)S(1)}, bf16[256,1500]{1,0:T(8,128)(2,1)}, u32[]{:S(2)}) copy-start(bf16[256,1500]{1,0:T(8,128)(2,1)} %copy-done.2) | copy-start | bytes 2304004
  118.9 47.0 %copy-start.5 = (bf16[256,1500]{1,0:T(8,128)(2,1)S(1)}, bf16[256,1500]{1,0:T(8,128)(2,1)}, u32[]{:S(2)}) copy-start(bf16[256,1500]{1,0:T(8,128)(2,1)} %copy-done.4) | copy-start | bytes 2304004
  134.0 1.5 collective-permute-start.18
  137.1 8.5 %collective-permute-start.19 = (bf16[128,750]{1,0:T(8,128)(2,1)S(1)}, bf16[128,750]{1,0:T(8,128)(2,1)S(1)}, u32[]{:S(2)}, u32[]{:S(2)}) collective-permute-start(bf16[128,750]{1,0:T(8,128)(2,1)S(1)} %shard_map.68.refs_0_), channel_id=1, source_target_pairs={{0,1},{1,2},{2,3},{3,4},{4,5},{5,6},{6,7},{7,0},{8,9},{9,10},{10,1... | collective-permute-start | bytes 576008 | tf_op jit(solution)/shard_map/ppermute | solution.py:29
  137.2 8.4 %collective-permute-start.20 = (bf16[128,750]{1,0:T(8,128)(2,1)S(1)}, bf16[128,750]{1,0:T(8,128)(2,1)S(1)}, u32[]{:S(2)}, u32[]{:S(2)}) collective-permute-start(bf16[128,750]{1,0:T(8,128)(2,1)S(1)} %shard_map.68.refs_0_), channel_id=1, source_target_pairs={{0,7},{1,0},{2,1},{3,2},{4,3},{5,4},{6,5},{7,6},{8,15},{9,8},{10,9... | collective-permute-start | bytes 576008 | tf_op jit(solution)/shard_map/ppermute | solution.py:29
  145.6 7.5 %collective-permute-start.21 = (bf16[128,750]{1,0:T(8,128)(2,1)S(1)}, bf16[128,750]{1,0:T(8,128)(2,1)S(1)}, u32[]{:S(2)}, u32[]{:S(2)}) collective-permute-start(bf16[128,750]{1,0:T(8,128)(2,1)S(1)} %collective-permute-done.19.refs_1_), channel_id=1, source_target_pairs={{0,1},{1,2},{2,3},{3,4},{4,5},{5,6},{6,7},{7,0},{8,9},{9,10},{10,1... | collective-permute-start | bytes 576008 | tf_op jit(solution)/shard_map/ppermute | solution.py:29
  145.6 7.5 %collective-permute-start.22 = (bf16[128,750]{1,0:T(8,128)(2,1)S(1)}, bf16[128,750]{1,0:T(8,128)(2,1)S(1)}, u32[]{:S(2)}, u32[]{:S(2)}) collective-permute-start(bf16[128,750]{1,0:T(8,128)(2,1)S(1)} %collective-permute-done.20.refs_2_), channel_id=1, source_target_pairs={{0,7},{1,0},{2,1},{3,2},{4,3},{5,4},{6,5},{7,6},{8,15},{9,8},{10,9... | collective-permute-start | bytes 576008 | tf_op jit(solution)/shard_map/ppermute | solution.py:29
  153.2 6.9 %collective-permute-start.23 = (bf16[128,750]{1,0:T(8,128)(2,1)S(1)}, bf16[128,750]{1,0:T(8,128)(2,1)S(1)}, u32[]{:S(2)}, u32[]{:S(2)}) collective-permute-start(bf16[128,750]{1,0:T(8,128)(2,1)S(1)} %collective-permute-done.21.refs_3_), channel_id=1, source_target_pairs={{0,1},{1,2},{2,3},{3,4},{4,5},{5,6},{6,7},{7,0},{8,9},{9,10},{10,1... | collective-permute-start | bytes 576008 | tf_op jit(solution)/shard_map/ppermute | solution.py:29
  153.2 7.0 %collective-permute-start.24 = (bf16[128,750]{1,0:T(8,128)(2,1)S(1)}, bf16[128,750]{1,0:T(8,128)(2,1)S(1)}, u32[]{:S(2)}, u32[]{:S(2)}) collective-permute-start(bf16[128,750]{1,0:T(8,128)(2,1)S(1)} %collective-permute-done.22.refs_4_), channel_id=1, source_target_pairs={{0,7},{1,0},{2,1},{3,2},{4,3},{5,4},{6,5},{7,6},{8,15},{9,8},{10,9... | collective-permute-start | bytes 576008 | tf_op jit(solution)/shard_map/ppermute | solution.py:29
  160.0 5.9 %collective-permute-start.25 = (bf16[64,750]{1,0:T(8,128)(2,1)S(1)}, bf16[64,750]{1,0:T(8,128)(2,1)S(1)}, u32[]{:S(2)}, u32[]{:S(2)}) collective-permute-start(bf16[64,750]{1,0:T(8,128)(2,1)S(1)} %slice.18), channel_id=1, source_target_pairs={{0,1},{1,2},{2,3},{3,4},{4,5},{5,6},{6,7},{7,0},{8,9},{9,10},{10,1... | collective-permute-start | bytes 288008 | tf_op jit(solution)/shard_map/ppermute | solution.py:29
  160.2 5.8 %collective-permute-start.26 = (bf16[64,750]{1,0:T(8,128)(2,1)S(1)}, bf16[64,750]{1,0:T(8,128)(2,1)S(1)}, u32[]{:S(2)}, u32[]{:S(2)}) collective-permute-start(bf16[64,750]{1,0:T(8,128)(2,1)S(1)} %slice.19), channel_id=1, source_target_pairs={{0,7},{1,0},{2,1},{3,2},{4,3},{5,4},{6,5},{7,6},{8,15},{9,8},{10,9... | collective-permute-start | bytes 288008 | tf_op jit(solution)/shard_map/ppermute | solution.py:29

commit v2 on v1

--- a/solution.py
+++ b/solution.py
@@ -127,23 +127,29 @@
 
 
 def density_kernel(at, turned, other_turned, *refs):
-    *pieces, first, last, out = refs
+    *pieces, first, last, out, whole = refs
     k = at[1]
     size = len(pieces) + 1
-    share = turned.shape[0] // size
-    tile, rows = out.shape[0], first.shape[1]
+    block = first.shape[0]
+    share = block // CORES
+    rows, tile = first.shape[1], out.shape[0]
+
+    @pl.when(pl.program_id(0) == 0)
+    def _():
+        whole[: size * share, :] = turned[...]
+        whole[size * share :, :] = other_turned[...]
 
     def stretch(low, high):
         for p in range(out.shape[1]):
-            total = 0.0
-            for core, right in ((k, turned), (1 - k, other_turned)):
+            left = []
+            for core in (k, 1 - k):
                 start = pl.multiple_of(core * share, share)
-                near = pl.ds(CORES * p * share + start, share)
+                near = pl.ds(p * block + start, share)
                 at_block = {d: piece[near, low:high] for d, piece in zip(ring_order(size), pieces)}
                 at_block[size // 2] = (first, last)[p][pl.ds(start, share), low:high]
-                left = jnp.concatenate([at_block[d] for d in range(size)], axis=0)
-                total += dot(left, right[...], (0, 0))
-            out[: high - low, p, :] = total.astype(NARROW)
+                left += [at_block[d] for d in range(size)]
+            left = jnp.concatenate(left, axis=0)
+            out[: high - low, p, :] = dot(left, whole[...], (0, 0)).astype(NARROW)
 
     for n, low in enumerate(range(0, rows, tile)):
         pl.when(pl.program_id(0) == n)(functools.partial(stretch, low, min(low + tile, rows)))
@@ -230,6 +236,7 @@
         in_specs=[SCALAR] + [kept] * (2 + len(pieces)),
         out_specs=pl.BlockSpec((tile, perts, cols), lambda i: (i, 0, 0)),
         out_shape=shape_of(rows, perts, cols),
+        scratch_shapes=[pltpu.VMEM((nx * block, cols), NARROW)],
         compiler_params=ROOMY,
     )(at, turned, other_turned, *pieces)
     return jnp.transpose(total, (1, 0, 2))

time: 175 us -> 174 us (level)
  no operation moved by 1% of the time
where the time goes in v2:
time: 174 us; the launch traced here: 171 us
  starting transfers between devices  69.5 us (40%)
  waiting for transfers between devices  66.9 us (38%)
  blocking collectives  14.9 us (9%)
  Pallas kernels  12.3 us (7%)
  local copies, waits for them, and re-layouts  5.77 us (3%)
    ppermute x24, waiting for transfers between devices, turn(): lax.ppermute(shard, axis, [(i, (i + step) % size) for i in range(size)])  43 us
    ppermute x24, starting transfers between devices, turn(): lax.ppermute(shard, axis, [(i, (i + step) % size) for i in range(size)])  40.8 us
    all_to_all x2, starting transfers between devices, exchanged(): return lax.all_to_all(pieces, axis, split_axis=0, concat_axis=0, tiled=True)  28.5 us
    all_to_all x2, waiting for transfers between devices, exchanged(): return lax.all_to_all(pieces, axis, split_axis=0, concat_axis=0, tiled=True)  20.9 us
    all_to_all x1, blocking collectives, exchanged(): return lax.all_to_all(pieces, axis, split_axis=0, concat_axis=0, tiled=True)  14.9 us
    pallas_call x1, Pallas kernels, per_device(): pl.pallas_call(density_kernel, grid=(pl.cdiv(rows, tile),), in_specs=[SCA...  5.33 us
  transfers between devices with their start and end apart: 29, of which 15 were waited for; matrix products, arithmetic and copies ran while one was open for 2% of the time, Pallas kernels for 2%

profile of v2, /device:TPU:516, one launch (start us, length us, event | category | flops | bytes accessed | tf_op | source)
XLA Modules:
  0.0 171.3 jit_solution(17126385576840480085)
XLA Ops:
  0.0 1.8 %broadcast_in_dim.6 = bf16[8,32,1500]{2,1,0:T(8,128)(2,1)} broadcast(bf16[32,1500]{1,0:T(8,128)(2,1)} %bitcast.7), dimensions={1,2} | broadcast | bytes 864000 | tf_op jit(solution)/shard_map/broadcast_in_dim | solution.py:169
  1.9 22.7 %all-to-all-start = ((bf16[8,32,1500]{2,1,0:T(8,128)(2,1)}), bf16[8,32,1500]{2,1,0:T(8,128)(2,1)S(1)}, u32[]{:S(2)}, u32[]{:S(2)}) async-start(bf16[8,32,1500]{2,1,0:T(8,128)(2,1)} %broadcast_in_dim.6), calls=%async_computation | async-start | bytes 1572864 | tf_op jit(solution)/shard_map/all_to_all | solution.py:50
  24.6 0.0 collective-permute-start.9
  24.6 12.8 %all-to-all-done.held = bf16[8,32,1500]{2,1,0:T(8,128)(2,1)S(1)} async-done(((bf16[8,32,1500]{2,1,0:T(8,128)(2,1)}), bf16[8,32,1500]{2,1,0:T(8,128)(2,1)S(1)}, u32[]{:S(2)}, u32[]{:S(2)}) %all-to-all-start) | async-done | bytes 768032 | tf_op jit(solution)/shard_map/all_to_all | solution.py:50
  37.4 0.0 collective-permute-start
  37.4 4.6 %collective-permute-start.10 = (bf16[750,250]{1,0:T(8,128)(2,1)}, bf16[750,250]{1,0:T(8,128)(2,1)S(1)}, u32[]{:S(2)}, u32[]{:S(2)}) collective-permute-start(bf16[750,250]{1,0:T(8,128)(2,1)} %refs_0_.3), channel_id=1, source_target_pairs={{0,7},{1,0},{2,1},{3,2},{4,3},{5,4},{6,5},{7,6},{8,15},{9,8},{10,9... | collective-permute-start | bytes 1125008 | tf_op jit(solution)/shard_map/ppermute | solution.py:29
  42.0 0.0 collective-permute-done.9.refs_1_
  42.0 0.0 collective-permute-start.11
  42.0 9.2 %collective-permute-done.10.refs_2_ = bf16[750,250]{1,0:T(8,128)(2,1)S(1)} collective-permute-done((bf16[750,250]{1,0:T(8,128)(2,1)}, bf16[750,250]{1,0:T(8,128)(2,1)S(1)}, u32[]{:S(2)}, u32[]{:S(2)}) %collective-permute-start.10) | collective-permute-done | bytes 375032 | tf_op jit(solution)/shard_map/ppermute | solution.py:29
  51.2 3.6 %collective-permute-start.12 = (bf16[750,250]{1,0:T(8,128)(2,1)S(1)}, bf16[750,250]{1,0:T(8,128)(2,1)S(1)}, u32[]{:S(2)}, u32[]{:S(2)}) collective-permute-start(bf16[750,250]{1,0:T(8,128)(2,1)S(1)} %collective-permute-done.10.refs_2_), channel_id=1, source_target_pairs={{0,7},{1,0},{2,1},{3,2},{4,3},{5,4},{6,5},{7,6},{8,15},{9,8},{10,9... | collective-permute-start | bytes 1125008 | tf_op jit(solution)/shard_map/ppermute | solution.py:29
  54.7 3.0 %copy.7.pert = bf16[2,750,1500]{2,1,0:T(8,128)(2,1)S(1)} copy(bf16[2,750,1500]{2,0,1:T(2,128)(2,1)} %param.6) | data formatting | bytes 9000000 | tf_op args[0]
  57.8 0.1 pad_add_fusion.at
  57.9 2.0 %shard_map.64 = (bf16[256,1500]{1,0:T(8,128)(2,1)S(1)}, bf16[2,256,750]{2,1,0:T(8,128)(2,1)S(1)}) custom-call(s32[2]{0:T(128)S(1)} %pad_add_fusion.at, bf16[8,32,1500]{2,1,0:T(8,128)(2,1)S(1)} %all-to-all-done.held, bf16[2,750,1500]{2,1,0:T(8,128)(2,1)S(1)} %copy.7.pert), custom_call_target="tpu_custom_call" | custom-call | tf_op jit(solution)/shard_map/pallas_call | solution.py:176
  59.8 0.0 copy-start.2
  59.8 0.0 copy-start.1
  59.9 2.0 %shard_map.65 = (bf16[256,1500]{1,0:T(8,128)(2,1)S(1)}, bf16[64,750]{1,0:T(8,128)(2,1)S(1)}, bf16[64,750]{1,0:T(8,128)(2,1)S(1)}, bf16[128,750]{1,0:T(8,128)(2,1...) custom-call(s32[2]{0:T(128)S(1)} %pad_add_fusion.at, ...), custom_call_target="tpu_custom_call" | custom-call | tf_op jit(solution)/shard_map/pallas_call | solution.py:183
  61.9 0.0 copy-start.7
  61.9 0.1 collective-permute-start.1
  62.1 0.7 collective-permute-done.12.refs_4_
  62.8 3.7 %collective-permute-start.14 = (bf16[750,250]{1,0:T(8,128)(2,1)S(1)}, bf16[750,250]{1,0:T(8,128)(2,1)S(1)}, u32[]{:S(2)}, u32[]{:S(2)}) collective-permute-start(bf16[750,250]{1,0:T(8,128)(2,1)S(1)} %collective-permute-done.12.refs_4_), channel_id=1, source_target_pairs={{0,7},{1,0},{2,1},{3,2},{4,3},{5,4},{6,5},{7,6},{8,15},{9,8},{10,9... | collective-permute-start | bytes 1125008 | tf_op jit(solution)/shard_map/ppermute | solution.py:29
  66.4 0.7 collective-permute-done.13.refs_5_
  67.1 0.0 copy-start.6
  67.1 0.1 collective-permute-start.15
  67.3 3.2 %collective-permute-start.5 = (bf16[64,750]{1,0:T(8,128)(2,1)S(1)}, bf16[64,750]{1,0:T(8,128)(2,1)S(1)}, u32[]{:S(2)}, u32[]{:S(2)}) collective-permute-start(bf16[64,750]{1,0:T(8,128)(2,1)S(1)} %get-tuple-element.31), channel_id=1, source_target_pairs={{0,7},{1,0},{2,1},{3,2},{4,3},{5,4},{6,5},{7,6},{8,15},{9,8},{10,9... | collective-permute-start | bytes 288008 | tf_op jit(solution)/shard_map/ppermute | solution.py:29
  70.5 0.1 collective-permute-start.2
  70.7 5.0 %collective-permute-done.5 = bf16[64,750]{1,0:T(8,128)(2,1)S(1)} collective-permute-done((bf16[64,750]{1,0:T(8,128)(2,1)S(1)}, bf16[64,750]{1,0:T(8,128)(2,1)S(1)}, u32[]{:S(2)}, u32[]{:S(2)}) %collective-permute-start.5) | collective-permute-done | bytes 96032 | tf_op jit(solution)/shard_map/ppermute | solution.py:29
  75.7 4.0 %collective-permute-start.6 = (bf16[128,750]{1,0:T(8,128)(2,1)S(1)}, bf16[128,750]{1,0:T(8,128)(2,1)S(1)}, u32[]{:S(2)}, u32[]{:S(2)}) collective-permute-start(bf16[128,750]{1,0:T(8,128)(2,1)S(1)} %add_convert_fusion.3), channel_id=1, source_target_pairs={{0,7},{1,0},{2,1},{3,2},{4,3},{5,4},{6,5},{7,6},{8,15},{9,8},{10,9... | collective-permute-start | bytes 576008 | tf_op jit(solution)/shard_map/ppermute | solution.py:29
  79.7 0.0 collective-permute-done.2
  79.8 0.1 collective-permute-start.3
  79.9 3.0 %collective-permute-done.6 = bf16[128,750]{1,0:T(8,128)(2,1)S(1)} collective-permute-done((bf16[128,750]{1,0:T(8,128)(2,1)S(1)}, bf16[128,750]{1,0:T(8,128)(2,1)S(1)}, u32[]{:S(2)}, u32[]{:S(2)}) %collective-permute-start.6) | collective-permute-done | bytes 192032 | tf_op jit(solution)/shard_map/ppermute | solution.py:29
  83.0 3.8 %collective-permute-start.7 = (bf16[128,750]{1,0:T(8,128)(2,1)S(1)}, bf16[128,750]{1,0:T(8,128)(2,1)S(1)}, u32[]{:S(2)}, u32[]{:S(2)}) collective-permute-start(bf16[128,750]{1,0:T(8,128)(2,1)S(1)} %add_convert_fusion.2), channel_id=1, source_target_pairs={{0,7},{1,0},{2,1},{3,2},{4,3},{5,4},{6,5},{7,6},{8,15},{9,8},{10,9... | collective-permute-start | bytes 576008 | tf_op jit(solution)/shard_map/ppermute | solution.py:29
  86.8 0.0 collective-permute-done.3
  86.8 0.1 collective-permute-start.4
  87.0 3.4 %collective-permute-done.7 = bf16[128,750]{1,0:T(8,128)(2,1)S(1)} collective-permute-done((bf16[128,750]{1,0:T(8,128)(2,1)S(1)}, bf16[128,750]{1,0:T(8,128)(2,1)S(1)}, u32[]{:S(2)}, u32[]{:S(2)}) %collective-permute-start.7) | collective-permute-done | bytes 192032 | tf_op jit(solution)/shard_map/ppermute | solution.py:29
  90.4 3.8 %collective-permute-start.8 = (bf16[128,750]{1,0:T(8,128)(2,1)S(1)}, bf16[128,750]{1,0:T(8,128)(2,1)S(1)}, u32[]{:S(2)}, u32[]{:S(2)}) collective-permute-start(bf16[128,750]{1,0:T(8,128)(2,1)S(1)} %add_convert_fusion.1), channel_id=1, source_target_pairs={{0,7},{1,0},{2,1},{3,2},{4,3},{5,4},{6,5},{7,6},{8,15},{9,8},{10,9... | collective-permute-start | bytes 576008 | tf_op jit(solution)/shard_map/ppermute | solution.py:29
  94.2 0.2 collective-permute-start.16
  94.4 5.5 %collective-permute-done.16.refs_8_ = bf16[366,250]{1,0:T(8,128)(2,1)S(1)} collective-permute-done((bf16[366,250]{1,0:T(8,128)(2,1)S(1)}, bf16[366,250]{1,0:T(8,128)(2,1)S(1)}, u32[]{:S(2)}, u32[]{:S(2)}) %collective-permute-start.16) | collective-permute-done | bytes 183032 | tf_op jit(solution)/shard_map/ppermute | solution.py:29
  99.9 0.0 collective-permute-done.15.refs_7_
  99.9 0.0 collective-permute-done.4.down
  99.9 1.2 shard_map.66
  101.2 0.1 collective-permute-start.17
  101.4 1.5 collective-permute-done.17
  102.9 0.8 add_convert_fusion
  103.6 5.8 %all-to-all-start.1 = ((bf16[8,64,256]{2,1,0:T(8,128)(2,1)}), bf16[8,64,256]{2,1,0:T(8,128)(2,1)S(1)}, u32[]{:S(2)}, u32[]{:S(2)}) async-start(bf16[8,64,256]{2,1,0:T(8,128)(2,1)} %add_convert_fusion), calls=%async_computation.1 | async-start | bytes 524288 | tf_op jit(solution)/shard_map/all_to_all | solution.py:50
  109.5 0.6 dynamic_slice.9
  110.6 0.1 reshape.3
  110.7 0.1 dynamic-slice_bitcast_fusion
  110.8 0.1 copy.9.virtual
  110.9 8.1 %all-to-all-done.1.terms = bf16[8,64,256]{2,1,0:T(8,128)(2,1)S(1)} async-done(((bf16[8,64,256]{2,1,0:T(8,128)(2,1)}), bf16[8,64,256]{2,1,0:T(8,128)(2,1)S(1)}, u32[]{:S(2)}, u32[]{:S(2)}) %all-to-all-start.1) | async-done | bytes 262176 | tf_op jit(solution)/shard_map/all_to_all | solution.py:50
  119.0 0.1 shard_map.67
  119.0 14.9 %all_to_all.15.own = bf16[8,64,256]{2,1,0:T(8,128)(2,1)S(1)} all-to-all(bf16[8,64,256]{2,1,0:T(8,128)(2,1)S(1)} %shard_map.67), channel_id=1, replica_groups=mesh['grp'=2,'x'=8,'k'=2,'y'=8] {'x'}, dimensions={0} | all-to-all | bytes 524288 | tf_op jit(solution)/shard_map/all_to_all | solution.py:50
  134.0 1.5 collective-permute-done.18.other
  135.5 1.6 shard_map.68.refs_0_
  137.1 0.1 collective-permute-start.19
  137.2 3.3 %collective-permute-start.20 = (bf16[128,750]{1,0:T(8,128)(2,1)S(1)}, bf16[128,750]{1,0:T(8,128)(2,1)S(1)}, u32[]{:S(2)}, u32[]{:S(2)}) collective-permute-start(bf16[128,750]{1,0:T(8,128)(2,1)S(1)} %shard_map.68.refs_0_), channel_id=1, source_target_pairs={{0,7},{1,0},{2,1},{3,2},{4,3},{5,4},{6,5},{7,6},{8,15},{9,8},{10,9... | collective-permute-start | bytes 576008 | tf_op jit(solution)/shard_map/ppermute | solution.py:29
  140.5 5.1 %collective-permute-done.19.refs_1_ = bf16[128,750]{1,0:T(8,128)(2,1)S(1)} collective-permute-done((bf16[128,750]{1,0:T(8,128)(2,1)S(1)}, bf16[128,750]{1,0:T(8,128)(2,1)S(1)}, u32[]{:S(2)}, u32[]{:S(2)}) %collective-permute-start.19) | collective-permute-done | bytes 192032 | tf_op jit(solution)/shard_map/ppermute | solution.py:29
  145.6 3.2 %collective-permute-start.22 = (bf16[128,750]{1,0:T(8,128)(2,1)S(1)}, bf16[128,750]{1,0:T(8,128)(2,1)S(1)}, u32[]{:S(2)}, u32[]{:S(2)}) collective-permute-start(bf16[128,750]{1,0:T(8,128)(2,1)S(1)} %collective-permute-done.20.refs_2_), channel_id=1, source_target_pairs={{0,7},{1,0},{2,1},{3,2},{4,3},{5,4},{6,5},{7,6},{8,15},{9,8},{10,9... | collective-permute-start | bytes 576008 | tf_op jit(solution)/shard_map/ppermute | solution.py:29
  148.8 4.3 %collective-permute-done.21.refs_3_ = bf16[128,750]{1,0:T(8,128)(2,1)S(1)} collective-permute-done((bf16[128,750]{1,0:T(8,128)(2,1)S(1)}, bf16[128,750]{1,0:T(8,128)(2,1)S(1)}, u32[]{:S(2)}, u32[]{:S(2)}) %collective-permute-start.21) | collective-permute-done | bytes 192032 | tf_op jit(solution)/shard_map/ppermute | solution.py:29
  153.2 3.2 %collective-permute-start.24 = (bf16[128,750]{1,0:T(8,128)(2,1)S(1)}, bf16[128,750]{1,0:T(8,128)(2,1)S(1)}, u32[]{:S(2)}, u32[]{:S(2)}) collective-permute-start(bf16[128,750]{1,0:T(8,128)(2,1)S(1)} %collective-permute-done.22.refs_4_), channel_id=1, source_target_pairs={{0,7},{1,0},{2,1},{3,2},{4,3},{5,4},{6,5},{7,6},{8,15},{9,8},{10,9... | collective-permute-start | bytes 576008 | tf_op jit(solution)/shard_map/ppermute | solution.py:29
  156.4 3.6 %collective-permute-done.23.refs_5_ = bf16[128,750]{1,0:T(8,128)(2,1)S(1)} collective-permute-done((bf16[128,750]{1,0:T(8,128)(2,1)S(1)}, bf16[128,750]{1,0:T(8,128)(2,1)S(1)}, u32[]{:S(2)}, u32[]{:S(2)}) %collective-permute-start.23) | collective-permute-done | bytes 192032 | tf_op jit(solution)/shard_map/ppermute | solution.py:29
  160.0 0.1 collective-permute-start.25
  160.2 3.3 %collective-permute-start.26 = (bf16[64,750]{1,0:T(8,128)(2,1)S(1)}, bf16[64,750]{1,0:T(8,128)(2,1)S(1)}, u32[]{:S(2)}, u32[]{:S(2)}) collective-permute-start(bf16[64,750]{1,0:T(8,128)(2,1)S(1)} %slice.19), channel_id=1, source_target_pairs={{0,7},{1,0},{2,1},{3,2},{4,3},{5,4},{6,5},{7,6},{8,15},{9,8},{10,9... | collective-permute-start | bytes 288008 | tf_op jit(solution)/shard_map/ppermute | solution.py:29
  163.5 2.5 %collective-permute-done.25.refs_7_ = bf16[64,750]{1,0:T(8,128)(2,1)S(1)} collective-permute-done((bf16[64,750]{1,0:T(8,128)(2,1)S(1)}, bf16[64,750]{1,0:T(8,128)(2,1)S(1)}, u32[]{:S(2)}, u32[]{:S(2)}) %collective-permute-start.25) | collective-permute-done | bytes 96032 | tf_op jit(solution)/shard_map/ppermute | solution.py:29
  166.0 5.3 %shard_map.69 = bf16[750,2,1500]{2,1,0:T(2,128)(2,1)} custom-call(s32[2]{0:T(128)S(1)} %pad_add_fusion.at, bf16[256,1500]{1,0:T(8,128)(2,1)S(1)} %copy-done.3, bf16[256,1500]{1,0:T(8,128)(2,1)S(1)} %copy-done.5, bf16[128,750]{1,0:T(8,128)(2,1)S(1)} %shard_map.68.refs_0_, bf16[128,750]{1,0:T(8,128)(2,1)S(1)} %collective-permute-done.19.refs_1_, ...), custom_call_target="tpu_custom_call" | custom-call | tf_op jit(solution)/shard_map/pallas_call | solution.py:233
  (36 shorter events, 0.4 us)
Async XLA Ops:
  0.0 110.7 %copy-start = (f32[512]{0:T(512)S(1)}, f32[512]{0:T(512)}, u32[]{:S(2)}) copy-start(f32[512]{0:T(512)} %param.10) | copy-start | bytes 6148
  1.9 35.5 %all-to-all-start = ((bf16[8,32,1500]{2,1,0:T(8,128)(2,1)}), bf16[8,32,1500]{2,1,0:T(8,128)(2,1)S(1)}, u32[]{:S(2)}, u32[]{:S(2)}) async-start(bf16[8,32,1500]{2,1,0:T(8,128)(2,1)} %broadcast_in_dim.6), calls=%async_computation | async-start | bytes 1572864 | tf_op jit(solution)/shard_map/all_to_all | solution.py:50
  24.6 17.4 %collective-permute-start.9 = (bf16[750,250]{1,0:T(8,128)(2,1)}, bf16[750,250]{1,0:T(8,128)(2,1)S(1)}, u32[]{:S(2)}, u32[]{:S(2)}) collective-permute-start(bf16[750,250]{1,0:T(8,128)(2,1)} %refs_0_.3), channel_id=1, source_target_pairs={{0,1},{1,2},{2,3},{3,4},{4,5},{5,6},{6,7},{7,0},{8,9},{9,10},{10,1... | collective-permute-start | bytes 1125008 | tf_op jit(solution)/shard_map/ppermute | solution.py:29
  37.4 22.5 %collective-permute-start = (bf16[8,32,1500]{2,1,0:T(8,128)(2,1)S(1)}, bf16[8,32,1500]{2,1,0:T(8,128)(2,1)S(1)}, u32[]{:S(2)}, u32[]{:S(2)}) collective-permute-start(bf16[8,32,1500]{2,1,0:T(8,128)(2,1)S(1)} %all-to-all-done.held), channel_id=1, source_target_pairs={{0,8},{8,0},{1,9},{9,1},{2,10},{10,2},{3,11},{11,3},{4,12},{12,4},... | collective-permute-start | bytes 2304008 | tf_op jit(solution)/shard_map/ppermute | solution.py:170
  37.4 13.8 %collective-permute-start.10 = (bf16[750,250]{1,0:T(8,128)(2,1)}, bf16[750,250]{1,0:T(8,128)(2,1)S(1)}, u32[]{:S(2)}, u32[]{:S(2)}) collective-permute-start(bf16[750,250]{1,0:T(8,128)(2,1)} %refs_0_.3), channel_id=1, source_target_pairs={{0,7},{1,0},{2,1},{3,2},{4,3},{5,4},{6,5},{7,6},{8,15},{9,8},{10,9... | collective-permute-start | bytes 1125008 | tf_op jit(solution)/shard_map/ppermute | solution.py:29
  42.0 12.8 %collective-permute-start.11 = (bf16[750,250]{1,0:T(8,128)(2,1)S(1)}, bf16[750,250]{1,0:T(8,128)(2,1)S(1)}, u32[]{:S(2)}, u32[]{:S(2)}) collective-permute-start(bf16[750,250]{1,0:T(8,128)(2,1)S(1)} %collective-permute-done.9.refs_1_), channel_id=1, source_target_pairs={{0,1},{1,2},{2,3},{3,4},{4,5},{5,6},{6,7},{7,0},{8,9},{9,10},{10,1... | collective-permute-start | bytes 1125008 | tf_op jit(solution)/shard_map/ppermute | solution.py:29
  51.2 11.6 %collective-permute-start.12 = (bf16[750,250]{1,0:T(8,128)(2,1)S(1)}, bf16[750,250]{1,0:T(8,128)(2,1)S(1)}, u32[]{:S(2)}, u32[]{:S(2)}) collective-permute-start(bf16[750,250]{1,0:T(8,128)(2,1)S(1)} %collective-permute-done.10.refs_2_), channel_id=1, source_target_pairs={{0,7},{1,0},{2,1},{3,2},{4,3},{5,4},{6,5},{7,6},{8,15},{9,8},{10,9... | collective-permute-start | bytes 1125008 | tf_op jit(solution)/shard_map/ppermute | solution.py:29
  54.7 12.4 %collective-permute-start.13 = (bf16[750,250]{1,0:T(8,128)(2,1)S(1)}, bf16[750,250]{1,0:T(8,128)(2,1)S(1)}, u32[]{:S(2)}, u32[]{:S(2)}) collective-permute-start(bf16[750,250]{1,0:T(8,128)(2,1)S(1)} %collective-permute-done.11.refs_3_), channel_id=1, source_target_pairs={{0,1},{1,2},{2,3},{3,4},{4,5},{5,6},{6,7},{7,0},{8,9},{9,10},{10,1... | collective-permute-start | bytes 1125008 | tf_op jit(solution)/shard_map/ppermute | solution.py:29
  59.8 27.0 %copy-start.2 = (bf16[256,1500]{1,0:T(8,128)(2,1)}, bf16[256,1500]{1,0:T(8,128)(2,1)S(1)}, u32[]{:S(2)}) copy-start(bf16[256,1500]{1,0:T(8,128)(2,1)S(1)} %get-tuple-element.20.turned) | copy-start | bytes 2304004
  59.8 40.1 %copy-start.1 = (bf16[750,250]{1,0:T(8,128)(2,1)S(1)}, bf16[750,250]{1,0:T(8,128)(2,1)}, u32[]{:S(2)}) copy-start(bf16[750,250]{1,0:T(8,128)(2,1)} %refs_0_.3) | copy-start | bytes 1125004
  61.9 32.3 %copy-start.4 = (bf16[256,1500]{1,0:T(8,128)(2,1)}, bf16[256,1500]{1,0:T(8,128)(2,1)S(1)}, u32[]{:S(2)}) copy-start(bf16[256,1500]{1,0:T(8,128)(2,1)S(1)} %get-tuple-element.22.other_turned) | copy-start | bytes 2304004
  61.9 47.6 %copy-start.7 = (s32[8]{0:T(128)S(1)}, s32[8]{0:T(128)}, u32[]{:S(2)}) copy-start(s32[8]{0:T(128)} %constant.37.clone) | copy-start | bytes 100
  61.9 8.6 %collective-permute-start.1 = (bf16[64,750]{1,0:T(8,128)(2,1)S(1)}, bf16[64,750]{1,0:T(8,128)(2,1)S(1)}, u32[]{:S(2)}, u32[]{:S(2)}) collective-permute-start(bf16[64,750]{1,0:T(8,128)(2,1)S(1)} %get-tuple-element.27), channel_id=1, source_target_pairs={{0,1},{1,2},{2,3},{3,4},{4,5},{5,6},{6,7},{7,0},{8,9},{9,10},{10,1... | collective-permute-start | bytes 288008 | tf_op jit(solution)/shard_map/ppermute | solution.py:29
  62.8 31.5 %collective-permute-start.14 = (bf16[750,250]{1,0:T(8,128)(2,1)S(1)}, bf16[750,250]{1,0:T(8,128)(2,1)S(1)}, u32[]{:S(2)}, u32[]{:S(2)}) collective-permute-start(bf16[750,250]{1,0:T(8,128)(2,1)S(1)} %collective-permute-done.12.refs_4_), channel_id=1, source_target_pairs={{0,7},{1,0},{2,1},{3,2},{4,3},{5,4},{6,5},{7,6},{8,15},{9,8},{10,9... | collective-permute-start | bytes 1125008 | tf_op jit(solution)/shard_map/ppermute | solution.py:29
  67.1 43.5 %copy-start.6 = (f32[2000]{0:T(1024)S(1)}, f32[2000]{0:T(1024)}, u32[]{:S(2)}) copy-start(f32[2000]{0:T(1024)} %param.9) | copy-start | bytes 24004
  67.1 32.8 %collective-permute-start.15 = (bf16[384,250]{1,0:T(8,128)(2,1)S(1)}, bf16[384,250]{1,0:T(8,128)(2,1)S(1)}, u32[]{:S(2)}, u32[]{:S(2)}) collective-permute-start(bf16[384,250]{1,0:T(8,128)(2,1)S(1)} %slice.16), channel_id=1, source_target_pairs={{0,1},{1,2},{2,3},{3,4},{4,5},{5,6},{6,7},{7,0},{8,9},{9,10},{10,1... | collective-permute-start | bytes 576008 | tf_op jit(solution)/shard_map/ppermute | solution.py:29
  67.3 8.4 %collective-permute-start.5 = (bf16[64,750]{1,0:T(8,128)(2,1)S(1)}, bf16[64,750]{1,0:T(8,128)(2,1)S(1)}, u32[]{:S(2)}, u32[]{:S(2)}) collective-permute-start(bf16[64,750]{1,0:T(8,128)(2,1)S(1)} %get-tuple-element.31), channel_id=1, source_target_pairs={{0,7},{1,0},{2,1},{3,2},{4,3},{5,4},{6,5},{7,6},{8,15},{9,8},{10,9... | collective-permute-start | bytes 288008 | tf_op jit(solution)/shard_map/ppermute | solution.py:29
  70.5 9.2 %collective-permute-start.2 = (bf16[128,750]{1,0:T(8,128)(2,1)S(1)}, bf16[128,750]{1,0:T(8,128)(2,1)S(1)}, u32[]{:S(2)}, u32[]{:S(2)}) collective-permute-start(bf16[128,750]{1,0:T(8,128)(2,1)S(1)} %add_convert_fusion.6), channel_id=1, source_target_pairs={{0,1},{1,2},{2,3},{3,4},{4,5},{5,6},{6,7},{7,0},{8,9},{9,10},{10,1... | collective-permute-start | bytes 576008 | tf_op jit(solution)/shard_map/ppermute | solution.py:29
  75.7 7.2 %collective-permute-start.6 = (bf16[128,750]{1,0:T(8,128)(2,1)S(1)}, bf16[128,750]{1,0:T(8,128)(2,1)S(1)}, u32[]{:S(2)}, u32[]{:S(2)}) collective-permute-start(bf16[128,750]{1,0:T(8,128)(2,1)S(1)} %add_convert_fusion.3), channel_id=1, source_target_pairs={{0,7},{1,0},{2,1},{3,2},{4,3},{5,4},{6,5},{7,6},{8,15},{9,8},{10,9... | collective-permute-start | bytes 576008 | tf_op jit(solution)/shard_map/ppermute | solution.py:29
  79.8 7.0 %collective-permute-start.3 = (bf16[128,750]{1,0:T(8,128)(2,1)S(1)}, bf16[128,750]{1,0:T(8,128)(2,1)S(1)}, u32[]{:S(2)}, u32[]{:S(2)}) collective-permute-start(bf16[128,750]{1,0:T(8,128)(2,1)S(1)} %add_convert_fusion.5), channel_id=1, source_target_pairs={{0,1},{1,2},{2,3},{3,4},{4,5},{5,6},{6,7},{7,0},{8,9},{9,10},{10,1... | collective-permute-start | bytes 576008 | tf_op jit(solution)/shard_map/ppermute | solution.py:29
  83.0 7.4 %collective-permute-start.7 = (bf16[128,750]{1,0:T(8,128)(2,1)S(1)}, bf16[128,750]{1,0:T(8,128)(2,1)S(1)}, u32[]{:S(2)}, u32[]{:S(2)}) collective-permute-start(bf16[128,750]{1,0:T(8,128)(2,1)S(1)} %add_convert_fusion.2), channel_id=1, source_target_pairs={{0,7},{1,0},{2,1},{3,2},{4,3},{5,4},{6,5},{7,6},{8,15},{9,8},{10,9... | collective-permute-start | bytes 576008 | tf_op jit(solution)/shard_map/ppermute | solution.py:29
  86.8 13.1 %collective-permute-start.4 = (bf16[128,750]{1,0:T(8,128)(2,1)S(1)}, bf16[128,750]{1,0:T(8,128)(2,1)S(1)}, u32[]{:S(2)}, u32[]{:S(2)}) collective-permute-start(bf16[128,750]{1,0:T(8,128)(2,1)S(1)} %add_convert_fusion.4), channel_id=1, source_target_pairs={{0,1},{1,2},{2,3},{3,4},{4,5},{5,6},{6,7},{7,0},{8,9},{9,10},{10,1... | collective-permute-start | bytes 576008 | tf_op jit(solution)/shard_map/ppermute | solution.py:29
  90.4 9.5 %collective-permute-start.8 = (bf16[128,750]{1,0:T(8,128)(2,1)S(1)}, bf16[128,750]{1,0:T(8,128)(2,1)S(1)}, u32[]{:S(2)}, u32[]{:S(2)}) collective-permute-start(bf16[128,750]{1,0:T(8,128)(2,1)S(1)} %add_convert_fusion.1), channel_id=1, source_target_pairs={{0,7},{1,0},{2,1},{3,2},{4,3},{5,4},{6,5},{7,6},{8,15},{9,8},{10,9... | collective-permute-start | bytes 576008 | tf_op jit(solution)/shard_map/ppermute | solution.py:29
  94.2 5.7 %collective-permute-start.16 = (bf16[366,250]{1,0:T(8,128)(2,1)S(1)}, bf16[366,250]{1,0:T(8,128)(2,1)S(1)}, u32[]{:S(2)}, u32[]{:S(2)}) collective-permute-start(bf16[366,250]{1,0:T(8,128)(2,1)S(1)} %slice.17), channel_id=1, source_target_pairs={{0,7},{1,0},{2,1},{3,2},{4,3},{5,4},{6,5},{7,6},{8,15},{9,8},{10,9... | collective-permute-start | bytes 549008 | tf_op jit(solution)/shard_map/ppermute | solution.py:29
  101.2 1.7 collective-permute-start.17
  103.6 15.3 %all-to-all-start.1 = ((bf16[8,64,256]{2,1,0:T(8,128)(2,1)}), bf16[8,64,256]{2,1,0:T(8,128)(2,1)S(1)}, u32[]{:S(2)}, u32[]{:S(2)}) async-start(bf16[8,64,256]{2,1,0:T(8,128)(2,1)} %add_convert_fusion), calls=%async_computation.1 | async-start | bytes 524288 | tf_op jit(solution)/shard_map/all_to_all | solution.py:50
  118.9 47.0 %copy-start.3 = (bf16[256,1500]{1,0:T(8,128)(2,1)S(1)}, bf16[256,1500]{1,0:T(8,128)(2,1)}, u32[]{:S(2)}) copy-start(bf16[256,1500]{1,0:T(8,128)(2,1)} %copy-done.2) | copy-start | bytes 2304004
  118.9 47.0 %copy-start.5 = (bf16[256,1500]{1,0:T(8,128)(2,1)S(1)}, bf16[256,1500]{1,0:T(8,128)(2,1)}, u32[]{:S(2)}) copy-start(bf16[256,1500]{1,0:T(8,128)(2,1)} %copy-done.4) | copy-start | bytes 2304004
  134.0 1.5 collective-permute-start.18
  137.1 8.5 %collective-permute-start.19 = (bf16[128,750]{1,0:T(8,128)(2,1)S(1)}, bf16[128,750]{1,0:T(8,128)(2,1)S(1)}, u32[]{:S(2)}, u32[]{:S(2)}) collective-permute-start(bf16[128,750]{1,0:T(8,128)(2,1)S(1)} %shard_map.68.refs_0_), channel_id=1, source_target_pairs={{0,1},{1,2},{2,3},{3,4},{4,5},{5,6},{6,7},{7,0},{8,9},{9,10},{10,1... | collective-permute-start | bytes 576008 | tf_op jit(solution)/shard_map/ppermute | solution.py:29
  137.2 8.4 %collective-permute-start.20 = (bf16[128,750]{1,0:T(8,128)(2,1)S(1)}, bf16[128,750]{1,0:T(8,128)(2,1)S(1)}, u32[]{:S(2)}, u32[]{:S(2)}) collective-permute-start(bf16[128,750]{1,0:T(8,128)(2,1)S(1)} %shard_map.68.refs_0_), channel_id=1, source_target_pairs={{0,7},{1,0},{2,1},{3,2},{4,3},{5,4},{6,5},{7,6},{8,15},{9,8},{10,9... | collective-permute-start | bytes 576008 | tf_op jit(solution)/shard_map/ppermute | solution.py:29
  145.6 7.5 %collective-permute-start.21 = (bf16[128,750]{1,0:T(8,128)(2,1)S(1)}, bf16[128,750]{1,0:T(8,128)(2,1)S(1)}, u32[]{:S(2)}, u32[]{:S(2)}) collective-permute-start(bf16[128,750]{1,0:T(8,128)(2,1)S(1)} %collective-permute-done.19.refs_1_), channel_id=1, source_target_pairs={{0,1},{1,2},{2,3},{3,4},{4,5},{5,6},{6,7},{7,0},{8,9},{9,10},{10,1... | collective-permute-start | bytes 576008 | tf_op jit(solution)/shard_map/ppermute | solution.py:29
  145.6 7.5 %collective-permute-start.22 = (bf16[128,750]{1,0:T(8,128)(2,1)S(1)}, bf16[128,750]{1,0:T(8,128)(2,1)S(1)}, u32[]{:S(2)}, u32[]{:S(2)}) collective-permute-start(bf16[128,750]{1,0:T(8,128)(2,1)S(1)} %collective-permute-done.20.refs_2_), channel_id=1, source_target_pairs={{0,7},{1,0},{2,1},{3,2},{4,3},{5,4},{6,5},{7,6},{8,15},{9,8},{10,9... | collective-permute-start | bytes 576008 | tf_op jit(solution)/shard_map/ppermute | solution.py:29
  153.2 6.9 %collective-permute-start.23 = (bf16[128,750]{1,0:T(8,128)(2,1)S(1)}, bf16[128,750]{1,0:T(8,128)(2,1)S(1)}, u32[]{:S(2)}, u32[]{:S(2)}) collective-permute-start(bf16[128,750]{1,0:T(8,128)(2,1)S(1)} %collective-permute-done.21.refs_3_), channel_id=1, source_target_pairs={{0,1},{1,2},{2,3},{3,4},{4,5},{5,6},{6,7},{7,0},{8,9},{9,10},{10,1... | collective-permute-start | bytes 576008 | tf_op jit(solution)/shard_map/ppermute | solution.py:29
  153.2 7.0 %collective-permute-start.24 = (bf16[128,750]{1,0:T(8,128)(2,1)S(1)}, bf16[128,750]{1,0:T(8,128)(2,1)S(1)}, u32[]{:S(2)}, u32[]{:S(2)}) collective-permute-start(bf16[128,750]{1,0:T(8,128)(2,1)S(1)} %collective-permute-done.22.refs_4_), channel_id=1, source_target_pairs={{0,7},{1,0},{2,1},{3,2},{4,3},{5,4},{6,5},{7,6},{8,15},{9,8},{10,9... | collective-permute-start | bytes 576008 | tf_op jit(solution)/shard_map/ppermute | solution.py:29
  160.0 5.9 %collective-permute-start.25 = (bf16[64,750]{1,0:T(8,128)(2,1)S(1)}, bf16[64,750]{1,0:T(8,128)(2,1)S(1)}, u32[]{:S(2)}, u32[]{:S(2)}) collective-permute-start(bf16[64,750]{1,0:T(8,128)(2,1)S(1)} %slice.18), channel_id=1, source_target_pairs={{0,1},{1,2},{2,3},{3,4},{4,5},{5,6},{6,7},{7,0},{8,9},{9,10},{10,1... | collective-permute-start | bytes 288008 | tf_op jit(solution)/shard_map/ppermute | solution.py:29
  160.2 5.8 %collective-permute-start.26 = (bf16[64,750]{1,0:T(8,128)(2,1)S(1)}, bf16[64,750]{1,0:T(8,128)(2,1)S(1)}, u32[]{:S(2)}, u32[]{:S(2)}) collective-permute-start(bf16[64,750]{1,0:T(8,128)(2,1)S(1)} %slice.19), channel_id=1, source_target_pairs={{0,7},{1,0},{2,1},{3,2},{4,3},{5,4},{6,5},{7,6},{8,15},{9,8},{10,9... | collective-permute-start | bytes 288008 | tf_op jit(solution)/shard_map/ppermute | solution.py:29

commit v3 on v1

--- a/solution.py
+++ b/solution.py
@@ -1,5 +1,3 @@
-import functools
-
 import jax
 import jax.numpy as jnp
 from jax import lax
@@ -54,11 +52,21 @@
     return lax.dot_general(a, b, ((over[:1], over[1:]), ((), ())), preferred_element_type=WIDE)
 
 
+def copies_kernel(shard, out, sent):
+    copies = [pltpu.make_async_copy(shard, out.at[n], sent.at[n]) for n in range(out.shape[0])]
+    for copy in copies:
+        copy.start()
+    for copy in copies:
+        copy.wait()
+
+
 def turn_and_multiply(at, held, pert, turned, image):
     size, share, _ = held.shape
     for d in range(size):
         turned[d * share : (d + 1) * share, :] = held[lax.rem(at[0] + d, size)]
-    for p in range(pert.shape[0]):
+
+    @pl.loop(0, pert.shape[0])
+    def _(p):
         image[p] = dot(turned[...], pert[p], (1, 1)).astype(NARROW)
 
 
@@ -111,42 +119,54 @@
         out[n] = response
 
 
-def mixed_kernel(at, own, other, *refs):
+def mixed_kernel(response, *refs):
     *chunks, out = refs
-    k = at[1]
-    chunks = [c[...] for c in chunks]
     width = chunks[0].shape[1]
     total = 0.0
     for n, chunk in enumerate(chunks):
-        left = jnp.concatenate([own[n], other[n]], axis=0)[:, :width]
-        total += dot(left, chunk, (1, 1))
-    block = own.shape[1]
-    total = total.astype(NARROW)
-    for core, part in ((k, total[:block]), (1 - k, total[block:])):
-        out[pl.ds(pl.multiple_of(core * block, block), block), :] = part
-
-
-def density_kernel(at, turned, other_turned, *refs):
-    *pieces, first, last, out = refs
+        total += dot(response[n][:, :width], chunk[...], (1, 1))
+    out[...] = total.astype(NARROW)
+
+
+def join_kernel(low, high, out):
+    out[: low.shape[0], :] = low[...]
+    out[low.shape[0] :, :] = high[...]
+
+
+def density_kernel(at, turned, *refs):
+    *refs, out = refs
     k = at[1]
-    size = len(pieces) + 1
-    share = turned.shape[0] // size
-    tile, rows = out.shape[0], first.shape[1]
-
-    def stretch(low, high):
-        for p in range(out.shape[1]):
-            total = 0.0
-            for core, right in ((k, turned), (1 - k, other_turned)):
-                start = pl.multiple_of(core * share, share)
-                near = pl.ds(CORES * p * share + start, share)
-                at_block = {d: piece[near, low:high] for d, piece in zip(ring_order(size), pieces)}
-                at_block[size // 2] = (first, last)[p][pl.ds(start, share), low:high]
-                left = jnp.concatenate([at_block[d] for d in range(size)], axis=0)
-                total += dot(left, right[...], (0, 0))
-            out[: high - low, p, :] = total.astype(NARROW)
-
-    for n, low in enumerate(range(0, rows, tile)):
-        pl.when(pl.program_id(0) == n)(functools.partial(stretch, low, min(low + tile, rows)))
+    perts = out.shape[1]
+    group = len(refs) // perts
+    size = group - 1
+    block, rows = refs[0].shape
+    share, tile = block // CORES, out.shape[0]
+
+    def stretch(low, width):
+        lanes = pl.ds(low, width)
+        waves = []
+        for w in range(perts):
+            *pieces, first, last = refs[w * group : (w + 1) * group]
+            at_block = {d: piece[:, lanes] for d, piece in zip(ring_order(size), pieces)}
+            at_block[size // 2] = jnp.concatenate([first[:, lanes], last[:, lanes]], axis=0)
+            waves.append(at_block)
+        for p in range(perts):
+            mine, yours = waves
+            block_of = {d: jnp.where(k == p, mine[d], yours[d]) for d in range(size)}
+            left = [block_of[d][:share] for d in range(size)], [block_of[d][share:] for d in range(size)]
+            ahead = [jnp.where(k == 0, a, b) for a, b in zip(*left)]
+            left = jnp.concatenate(ahead + [jnp.where(k == 0, b, a) for a, b in zip(*left)], axis=0)
+            out[:width, p, :] = dot(left, turned[...], (0, 0)).astype(NARROW)
+
+    step, whole = pl.program_id(0), rows // tile
+
+    @pl.when(step < whole)
+    def _():
+        stretch(pl.multiple_of(step * tile, tile), tile)
+
+    @pl.when(step >= whole)
+    def _():
+        stretch(whole * tile, rows - whole * tile)
 
 
 def per_device(perturbation, occ_coeffs, vir_coeffs, occ_energies, vir_energies):
@@ -160,7 +180,15 @@
 
     mid = up_to(rows // 2, LANES)
     occ = ring_gather(occ_coeffs, "y", mid)
-    own = exchanged(jnp.broadcast_to(vir_coeffs.T, (nx, share, cols)), "x")
+    anywhere = pl.BlockSpec(memory_space=pl.ANY)
+    own = pl.pallas_call(
+        copies_kernel,
+        in_specs=[anywhere],
+        out_specs=anywhere,
+        out_shape=shape_of(nx, share, cols),
+        scratch_shapes=[pltpu.SemaphoreType.DMA((nx,))],
+    )(vir_coeffs.T)
+    own = exchanged(own, "x")
     other = lax.ppermute(own, "k", SWAP)
 
     piece = shape_of(perts * block, rows)
@@ -214,24 +242,32 @@
     )(terms, levels, virtual)
     response = exchanged(response, "x")
     sibling = lax.ppermute(response, "k", SWAP)
-    mixed = pl.pallas_call(
-        mixed_kernel,
-        in_specs=[SCALAR] + [kept] * (1 + len(occ)),
+    pieces = []
+    for part in (response, sibling):
+        mixed = pl.pallas_call(
+            mixed_kernel,
+            in_specs=[kept] * (1 + ny),
+            out_specs=kept,
+            out_shape=half,
+            compiler_params=ROOMY,
+        )(part, *occ[:-2], far)
+        pieces += ring_gather(mixed, "y", share)
+    turned = pl.pallas_call(
+        join_kernel,
+        in_specs=[kept] * 2,
         out_specs=kept,
-        out_shape=piece,
-        compiler_params=ROOMY,
-    )(at, response, sibling, *occ[:-2], far)
-
-    pieces = ring_gather(mixed, "y", block)
+        out_shape=shape_of(nx * block, cols),
+        compiler_params=ROOMY,
+    )(turned, other_turned)
     tile = 2 * LANES
     total = pl.pallas_call(
         density_kernel,
         grid=(pl.cdiv(rows, tile),),
-        in_specs=[SCALAR] + [kept] * (2 + len(pieces)),
+        in_specs=[SCALAR] + [kept] * (1 + len(pieces)),
         out_specs=pl.BlockSpec((tile, perts, cols), lambda i: (i, 0, 0)),
         out_shape=shape_of(rows, perts, cols),
         compiler_params=ROOMY,
-    )(at, turned, other_turned, *pieces)
+    )(at, turned, *pieces)
     return jnp.transpose(total, (1, 0, 2))
 
 

time: 175 us -> 197 us (1.13)
  Pallas kernels: 12.6 us -> 39.6 us
  waiting for transfers between devices: 66.9 us -> 50.9 us
  starting transfers between devices: 69.5 us -> 82.4 us
    pallas_call x1 -> x4, Pallas kernels: 1.59 us -> 27.1 us  [the longest x1 25 us: per_device(): pl.pallas_call(copies_kernel, in_specs=[anywhere], out_specs=anywhere, ou...]
    ppermute x24 -> x32, waiting for transfers between devices: 43 us -> 28.6 us  [turn(): lax.ppermute(shard, axis, [(i, (i + step) % size) for i in range(size)])]
    ppermute x24 -> x32, starting transfers between devices: 40.8 us -> 53.7 us  [turn(): lax.ppermute(shard, axis, [(i, (i + step) % size) for i in range(size)])]
  transfers between devices with their start and end apart: 29 -> 37, of which waited for: 15 -> 11; matrix products, arithmetic and copies ran while one was open for 2% -> 2% of each run, Pallas kernels for 2% -> 4%
where the time goes in v3:
time: 197 us; the launch traced here: 194 us
  starting transfers between devices  82.4 us (42%)
  waiting for transfers between devices  50.9 us (26%)
  Pallas kernels  39.6 us (20%)
  blocking collectives  14.9 us (8%)
  local copies, waits for them, and re-layouts  4.01 us (2%)
    ppermute x32, starting transfers between devices, turn(): lax.ppermute(shard, axis, [(i, (i + step) % size) for i in range(size)])  53.7 us
    ppermute x32, waiting for transfers between devices, turn(): lax.ppermute(shard, axis, [(i, (i + step) % size) for i in range(size)])  28.6 us
    all_to_all x2, starting transfers between devices, exchanged(): return lax.all_to_all(pieces, axis, split_axis=0, concat_axis=0, tiled=True)  28.6 us
    pallas_call x1, Pallas kernels, per_device(): pl.pallas_call(copies_kernel, in_specs=[anywhere], out_specs=anywhere, ou...  25 us
    all_to_all x2, waiting for transfers between devices, exchanged(): return lax.all_to_all(pieces, axis, split_axis=0, concat_axis=0, tiled=True)  20.7 us
    all_to_all x1, blocking collectives, exchanged(): return lax.all_to_all(pieces, axis, split_axis=0, concat_axis=0, tiled=True)  14.9 us
    pallas_call x1, Pallas kernels, per_device(): pl.pallas_call(density_kernel, grid=(pl.cdiv(rows, tile),), in_specs=[SCA...  5.67 us
  transfers between devices with their start and end apart: 37, of which 11 were waited for; matrix products, arithmetic and copies ran while one was open for 2% of the time, Pallas kernels for 4%

profile of v3, /device:TPU:516, one launch (start us, length us, event | category | flops | bytes accessed | tf_op | source)
XLA Modules:
  0.0 194.0 jit_solution(192418909686071751)
XLA Ops:
  0.0 25.0 %shard_map.64 = bf16[8,32,1500]{2,1,0:T(8,128)(2,1)} custom-call(bf16[32,1500]{1,0:T(8,128)(2,1)} %bitcast.7), custom_call_target="tpu_custom_call" | custom-call | tf_op jit(solution)/shard_map/pallas_call | solution.py:184
  25.0 22.7 %all-to-all-start = ((bf16[8,32,1500]{2,1,0:T(8,128)(2,1)}), bf16[8,32,1500]{2,1,0:T(8,128)(2,1)S(1)}, u32[]{:S(2)}, u32[]{:S(2)}) async-start(bf16[8,32,1500]{2,1,0:T(8,128)(2,1)} %shard_map.64), calls=%async_computation | async-start | bytes 1572864 | tf_op jit(solution)/shard_map/all_to_all | solution.py:48
  47.7 0.0 collective-permute-start.9
  47.7 12.8 %all-to-all-done.held = bf16[8,32,1500]{2,1,0:T(8,128)(2,1)S(1)} async-done(((bf16[8,32,1500]{2,1,0:T(8,128)(2,1)}), bf16[8,32,1500]{2,1,0:T(8,128)(2,1)S(1)}, u32[]{:S(2)}, u32[]{:S(2)}) %all-to-all-start) | async-done | bytes 768032 | tf_op jit(solution)/shard_map/all_to_all | solution.py:48
  60.5 0.0 collective-permute-start
  60.5 4.6 %collective-permute-start.10 = (bf16[750,250]{1,0:T(8,128)(2,1)}, bf16[750,250]{1,0:T(8,128)(2,1)S(1)}, u32[]{:S(2)}, u32[]{:S(2)}) collective-permute-start(bf16[750,250]{1,0:T(8,128)(2,1)} %refs_0_.5), channel_id=1, source_target_pairs={{0,7},{1,0},{2,1},{3,2},{4,3},{5,4},{6,5},{7,6},{8,15},{9,8},{10,9... | collective-permute-start | bytes 1125008 | tf_op jit(solution)/shard_map/ppermute | solution.py:27
  65.1 0.0 collective-permute-done.9.refs_1_
  65.1 9.2 %collective-permute-done.10.refs_2_ = bf16[750,250]{1,0:T(8,128)(2,1)S(1)} collective-permute-done((bf16[750,250]{1,0:T(8,128)(2,1)}, bf16[750,250]{1,0:T(8,128)(2,1)S(1)}, u32[]{:S(2)}, u32[]{:S(2)}) %collective-permute-start.10) | collective-permute-done | bytes 375032 | tf_op jit(solution)/shard_map/ppermute | solution.py:27
  74.3 3.6 %collective-permute-start.12 = (bf16[750,250]{1,0:T(8,128)(2,1)S(1)}, bf16[750,250]{1,0:T(8,128)(2,1)S(1)}, u32[]{:S(2)}, u32[]{:S(2)}) collective-permute-start(bf16[750,250]{1,0:T(8,128)(2,1)S(1)} %collective-permute-done.10.refs_2_), channel_id=1, source_target_pairs={{0,7},{1,0},{2,1},{3,2},{4,3},{5,4},{6,5},{7,6},{8,15},{9,8},{10,9... | collective-permute-start | bytes 1125008 | tf_op jit(solution)/shard_map/ppermute | solution.py:27
  77.9 3.0 %copy.7.pert = bf16[2,750,1500]{2,1,0:T(8,128)(2,1)S(1)} copy(bf16[2,750,1500]{2,0,1:T(2,128)(2,1)} %param.6) | data formatting | bytes 9000000 | tf_op args[0]
  80.9 0.1 pad_add_fusion.at
  81.0 2.2 %shard_map.65 = (bf16[256,1500]{1,0:T(8,128)(2,1)S(1)}, bf16[2,256,750]{2,1,0:T(8,128)(2,1)S(1)}) custom-call(s32[2]{0:T(128)S(1)} %pad_add_fusion.at, bf16[8,32,1500]{2,1,0:T(8,128)(2,1)S(1)} %all-to-all-done.held, bf16[2,750,1500]{2,1,0:T(8,128)(2,1)S(1)} %copy.7.pert), custom_call_target="tpu_custom_call" | custom-call | tf_op jit(solution)/shard_map/pallas_call | solution.py:198
  83.3 0.0 copy-start.2
  83.3 0.0 copy-start.1
  83.3 3.2 %shard_map.66 = (bf16[256,1500]{1,0:T(8,128)(2,1)S(1)}, bf16[64,750]{1,0:T(8,128)(2,1)S(1)}, bf16[64,750]{1,0:T(8,128)(2,1)S(1)}, bf16[128,750]{1,0:T(8,128)(2,1...) custom-call(s32[2]{0:T(128)S(1)} %pad_add_fusion.at, ...), custom_call_target="tpu_custom_call" | custom-call | tf_op jit(solution)/shard_map/pallas_call | solution.py:205
  86.6 0.0 copy-start.7
  86.6 0.1 collective-permute-start.1
  86.7 3.3 %collective-permute-start.14 = (bf16[750,250]{1,0:T(8,128)(2,1)S(1)}, bf16[750,250]{1,0:T(8,128)(2,1)S(1)}, u32[]{:S(2)}, u32[]{:S(2)}) collective-permute-start(bf16[750,250]{1,0:T(8,128)(2,1)S(1)} %collective-permute-done.12.refs_4_), channel_id=1, source_target_pairs={{0,7},{1,0},{2,1},{3,2},{4,3},{5,4},{6,5},{7,6},{8,15},{9,8},{10,9... | collective-permute-start | bytes 1125008 | tf_op jit(solution)/shard_map/ppermute | solution.py:27
  90.1 0.0 copy-start.6
  90.1 0.1 collective-permute-start.15
  90.2 3.2 %collective-permute-start.5 = (bf16[64,750]{1,0:T(8,128)(2,1)S(1)}, bf16[64,750]{1,0:T(8,128)(2,1)S(1)}, u32[]{:S(2)}, u32[]{:S(2)}) collective-permute-start(bf16[64,750]{1,0:T(8,128)(2,1)S(1)} %get-tuple-element.31), channel_id=1, source_target_pairs={{0,7},{1,0},{2,1},{3,2},{4,3},{5,4},{6,5},{7,6},{8,15},{9,8},{10,9... | collective-permute-start | bytes 288008 | tf_op jit(solution)/shard_map/ppermute | solution.py:27
  93.5 0.1 collective-permute-start.2
  93.6 6.0 %collective-permute-done.5 = bf16[64,750]{1,0:T(8,128)(2,1)S(1)} collective-permute-done((bf16[64,750]{1,0:T(8,128)(2,1)S(1)}, bf16[64,750]{1,0:T(8,128)(2,1)S(1)}, u32[]{:S(2)}, u32[]{:S(2)}) %collective-permute-start.5) | collective-permute-done | bytes 96032 | tf_op jit(solution)/shard_map/ppermute | solution.py:27
  99.7 3.8 %collective-permute-start.6 = (bf16[128,750]{1,0:T(8,128)(2,1)S(1)}, bf16[128,750]{1,0:T(8,128)(2,1)S(1)}, u32[]{:S(2)}, u32[]{:S(2)}) collective-permute-start(bf16[128,750]{1,0:T(8,128)(2,1)S(1)} %add_convert_fusion.3), channel_id=1, source_target_pairs={{0,7},{1,0},{2,1},{3,2},{4,3},{5,4},{6,5},{7,6},{8,15},{9,8},{10,9... | collective-permute-start | bytes 576008 | tf_op jit(solution)/shard_map/ppermute | solution.py:27
  103.5 0.3 collective-permute-start.3
  103.8 2.8 %collective-permute-done.6 = bf16[128,750]{1,0:T(8,128)(2,1)S(1)} collective-permute-done((bf16[128,750]{1,0:T(8,128)(2,1)S(1)}, bf16[128,750]{1,0:T(8,128)(2,1)S(1)}, u32[]{:S(2)}, u32[]{:S(2)}) %collective-permute-start.6) | collective-permute-done | bytes 192032 | tf_op jit(solution)/shard_map/ppermute | solution.py:27
  106.7 3.8 %collective-permute-start.7 = (bf16[128,750]{1,0:T(8,128)(2,1)S(1)}, bf16[128,750]{1,0:T(8,128)(2,1)S(1)}, u32[]{:S(2)}, u32[]{:S(2)}) collective-permute-start(bf16[128,750]{1,0:T(8,128)(2,1)S(1)} %add_convert_fusion.2), channel_id=1, source_target_pairs={{0,7},{1,0},{2,1},{3,2},{4,3},{5,4},{6,5},{7,6},{8,15},{9,8},{10,9... | collective-permute-start | bytes 576008 | tf_op jit(solution)/shard_map/ppermute | solution.py:27
  110.5 0.2 collective-permute-done.3
  110.8 0.1 collective-permute-start.4
  110.9 2.9 %collective-permute-done.7 = bf16[128,750]{1,0:T(8,128)(2,1)S(1)} collective-permute-done((bf16[128,750]{1,0:T(8,128)(2,1)S(1)}, bf16[128,750]{1,0:T(8,128)(2,1)S(1)}, u32[]{:S(2)}, u32[]{:S(2)}) %collective-permute-start.7) | collective-permute-done | bytes 192032 | tf_op jit(solution)/shard_map/ppermute | solution.py:27
  113.9 3.8 %collective-permute-start.8 = (bf16[128,750]{1,0:T(8,128)(2,1)S(1)}, bf16[128,750]{1,0:T(8,128)(2,1)S(1)}, u32[]{:S(2)}, u32[]{:S(2)}) collective-permute-start(bf16[128,750]{1,0:T(8,128)(2,1)S(1)} %add_convert_fusion.1), channel_id=1, source_target_pairs={{0,7},{1,0},{2,1},{3,2},{4,3},{5,4},{6,5},{7,6},{8,15},{9,8},{10,9... | collective-permute-start | bytes 576008 | tf_op jit(solution)/shard_map/ppermute | solution.py:27
  117.7 0.2 collective-permute-start.16
  117.8 5.5 %collective-permute-done.16.refs_8_ = bf16[366,250]{1,0:T(8,128)(2,1)S(1)} collective-permute-done((bf16[366,250]{1,0:T(8,128)(2,1)S(1)}, bf16[366,250]{1,0:T(8,128)(2,1)S(1)}, u32[]{:S(2)}, u32[]{:S(2)}) %collective-permute-start.16) | collective-permute-done | bytes 183032 | tf_op jit(solution)/shard_map/ppermute | solution.py:27
  123.4 1.2 shard_map.68
  124.7 0.1 collective-permute-start.17
  124.8 1.5 collective-permute-done.17
  126.3 0.8 add_convert_fusion
  127.1 5.8 %all-to-all-start.1 = ((bf16[8,64,256]{2,1,0:T(8,128)(2,1)}), bf16[8,64,256]{2,1,0:T(8,128)(2,1)S(1)}, u32[]{:S(2)}, u32[]{:S(2)}) async-start(bf16[8,64,256]{2,1,0:T(8,128)(2,1)} %add_convert_fusion), calls=%async_computation.1 | async-start | bytes 524288 | tf_op jit(solution)/shard_map/all_to_all | solution.py:48
  133.0 0.6 dynamic_slice.9
  134.2 0.1 reshape.3
  134.3 0.1 dynamic-slice_bitcast_fusion
  134.4 0.1 copy.9.virtual
  134.5 7.9 %all-to-all-done.1.terms = bf16[8,64,256]{2,1,0:T(8,128)(2,1)S(1)} async-done(((bf16[8,64,256]{2,1,0:T(8,128)(2,1)}), bf16[8,64,256]{2,1,0:T(8,128)(2,1)S(1)}, u32[]{:S(2)}, u32[]{:S(2)}) %all-to-all-start.1) | async-done | bytes 262176 | tf_op jit(solution)/shard_map/all_to_all | solution.py:48
  142.4 0.1 shard_map.69
  142.5 14.9 %all_to_all.15.response = bf16[8,64,256]{2,1,0:T(8,128)(2,1)S(1)} all-to-all(bf16[8,64,256]{2,1,0:T(8,128)(2,1)S(1)} %shard_map.69), channel_id=1, replica_groups=mesh['grp'=2,'x'=8,'k'=2,'y'=8] {'x'}, dimensions={0} | all-to-all | bytes 524288 | tf_op jit(solution)/shard_map/all_to_all | solution.py:48
  157.4 1.0 shard_map.70.refs_0_
  158.5 0.1 collective-permute-start.18
  158.6 3.3 %collective-permute-start.19 = (bf16[64,750]{1,0:T(8,128)(2,1)S(1)}, bf16[64,750]{1,0:T(8,128)(2,1)S(1)}, u32[]{:S(2)}, u32[]{:S(2)}) collective-permute-start(bf16[64,750]{1,0:T(8,128)(2,1)S(1)} %shard_map.70.refs_0_), channel_id=1, source_target_pairs={{0,7},{1,0},{2,1},{3,2},{4,3},{5,4},{6,5},{7,6},{8,15},{9,8},{10,9... | collective-permute-start | bytes 288008 | tf_op jit(solution)/shard_map/ppermute | solution.py:27
  161.9 1.0 shard_map.71.refs_9_
  162.9 0.1 collective-permute-start.27
  163.1 3.2 %collective-permute-start.28 = (bf16[64,750]{1,0:T(8,128)(2,1)S(1)}, bf16[64,750]{1,0:T(8,128)(2,1)S(1)}, u32[]{:S(2)}, u32[]{:S(2)}) collective-permute-start(bf16[64,750]{1,0:T(8,128)(2,1)S(1)} %shard_map.71.refs_9_), channel_id=1, source_target_pairs={{0,7},{1,0},{2,1},{3,2},{4,3},{5,4},{6,5},{7,6},{8,15},{9,8},{10,9... | collective-permute-start | bytes 288008 | tf_op jit(solution)/shard_map/ppermute | solution.py:27
  166.3 3.2 %collective-permute-start.21 = (bf16[64,750]{1,0:T(8,128)(2,1)S(1)}, bf16[64,750]{1,0:T(8,128)(2,1)S(1)}, u32[]{:S(2)}, u32[]{:S(2)}) collective-permute-start(bf16[64,750]{1,0:T(8,128)(2,1)S(1)} %collective-permute-done.19.refs_2_), channel_id=1, source_target_pairs={{0,7},{1,0},{2,1},{3,2},{4,3},{5,4},{6,5},{7,6},{8,15},{9,8},{10,9... | collective-permute-start | bytes 288008 | tf_op jit(solution)/shard_map/ppermute | solution.py:27
  169.5 0.0 collective-permute-start.29
  169.5 3.2 %collective-permute-start.30 = (bf16[64,750]{1,0:T(8,128)(2,1)S(1)}, bf16[64,750]{1,0:T(8,128)(2,1)S(1)}, u32[]{:S(2)}, u32[]{:S(2)}) collective-permute-start(bf16[64,750]{1,0:T(8,128)(2,1)S(1)} %collective-permute-done.28.refs_11_), channel_id=1, source_target_pairs={{0,7},{1,0},{2,1},{3,2},{4,3},{5,4},{6,5},{7,6},{8,15},{9,8},{10,9... | collective-permute-start | bytes 288008 | tf_op jit(solution)/shard_map/ppermute | solution.py:27
  172.8 3.2 %collective-permute-start.23 = (bf16[64,750]{1,0:T(8,128)(2,1)S(1)}, bf16[64,750]{1,0:T(8,128)(2,1)S(1)}, u32[]{:S(2)}, u32[]{:S(2)}) collective-permute-start(bf16[64,750]{1,0:T(8,128)(2,1)S(1)} %collective-permute-done.21.refs_4_), channel_id=1, source_target_pairs={{0,7},{1,0},{2,1},{3,2},{4,3},{5,4},{6,5},{7,6},{8,15},{9,8},{10,9... | collective-permute-start | bytes 288008 | tf_op jit(solution)/shard_map/ppermute | solution.py:27
  176.0 3.2 %collective-permute-start.32 = (bf16[64,750]{1,0:T(8,128)(2,1)S(1)}, bf16[64,750]{1,0:T(8,128)(2,1)S(1)}, u32[]{:S(2)}, u32[]{:S(2)}) collective-permute-start(bf16[64,750]{1,0:T(8,128)(2,1)S(1)} %collective-permute-done.30.refs_13_), channel_id=1, source_target_pairs={{0,7},{1,0},{2,1},{3,2},{4,3},{5,4},{6,5},{7,6},{8,15},{9,8},{10,9... | collective-permute-start | bytes 288008 | tf_op jit(solution)/shard_map/ppermute | solution.py:27
  179.3 0.1 collective-permute-done.22.refs_5_
  179.4 0.0 collective-permute-start.24
  179.4 3.4 %collective-permute-start.25 = (bf16[32,750]{1,0:T(8,128)(2,1)S(1)}, bf16[32,750]{1,0:T(8,128)(2,1)S(1)}, u32[]{:S(2)}, u32[]{:S(2)}) collective-permute-start(bf16[32,750]{1,0:T(8,128)(2,1)S(1)} %slice.27), channel_id=1, source_target_pairs={{0,7},{1,0},{2,1},{3,2},{4,3},{5,4},{6,5},{7,6},{8,15},{9,8},{10,9... | collective-permute-start | bytes 144008 | tf_op jit(solution)/shard_map/ppermute | solution.py:27
  182.9 0.1 collective-permute-start.33
  183.0 3.3 %collective-permute-start.34 = (bf16[32,750]{1,0:T(8,128)(2,1)S(1)}, bf16[32,750]{1,0:T(8,128)(2,1)S(1)}, u32[]{:S(2)}, u32[]{:S(2)}) collective-permute-start(bf16[32,750]{1,0:T(8,128)(2,1)S(1)} %slice.29), channel_id=1, source_target_pairs={{0,7},{1,0},{2,1},{3,2},{4,3},{5,4},{6,5},{7,6},{8,15},{9,8},{10,9... | collective-permute-start | bytes 144008 | tf_op jit(solution)/shard_map/ppermute | solution.py:27
  186.4 0.1 shard_map.67.turned
  186.5 1.8 collective-permute-done.33.refs_16_
  188.3 5.7 %shard_map.72 = bf16[750,2,1500]{2,1,0:T(2,128)(2,1)} custom-call(s32[2]{0:T(128)S(1)} %pad_add_fusion.at, bf16[512,1500]{1,0:T(8,128)(2,1)S(1)} %shard_map.67.turned, bf16[64,750]{1,0:T(8,128)(2,1)S(1)} %shard_map.70.refs_0_, bf16[64,750]{1,0:T(8,128)(2,1)S(1)} %collective-permute-done.18.refs_1_, bf16[64,750]{1,0:T(8,128)(2,1)S(1)} %collective-permute-done.19.refs_2_, ...), custom_call_target="tpu_custom_call" | custom-call | tf_op jit(solution)/shard_map/pallas_call | solution.py:263
  (56 shorter events, 0.4 us)
Async XLA Ops:
  0.0 134.3 %copy-start = (f32[512]{0:T(512)S(1)}, f32[512]{0:T(512)}, u32[]{:S(2)}) copy-start(f32[512]{0:T(512)} %param.10) | copy-start | bytes 6148
  25.0 35.5 %all-to-all-start = ((bf16[8,32,1500]{2,1,0:T(8,128)(2,1)}), bf16[8,32,1500]{2,1,0:T(8,128)(2,1)S(1)}, u32[]{:S(2)}, u32[]{:S(2)}) async-start(bf16[8,32,1500]{2,1,0:T(8,128)(2,1)} %shard_map.64), calls=%async_computation | async-start | bytes 1572864 | tf_op jit(solution)/shard_map/all_to_all | solution.py:48
  47.7 17.4 %collective-permute-start.9 = (bf16[750,250]{1,0:T(8,128)(2,1)}, bf16[750,250]{1,0:T(8,128)(2,1)S(1)}, u32[]{:S(2)}, u32[]{:S(2)}) collective-permute-start(bf16[750,250]{1,0:T(8,128)(2,1)} %refs_0_.5), channel_id=1, source_target_pairs={{0,1},{1,2},{2,3},{3,4},{4,5},{5,6},{6,7},{7,0},{8,9},{9,10},{10,1... | collective-permute-start | bytes 1125008 | tf_op jit(solution)/shard_map/ppermute | solution.py:27
  60.5 22.7 %collective-permute-start = (bf16[8,32,1500]{2,1,0:T(8,128)(2,1)S(1)}, bf16[8,32,1500]{2,1,0:T(8,128)(2,1)}, u32[]{:S(2)}, u32[]{:S(2)}) collective-permute-start(bf16[8,32,1500]{2,1,0:T(8,128)(2,1)S(1)} %all-to-all-done.held), channel_id=1, source_target_pairs={{0,8},{8,0},{1,9},{9,1},{2,10},{10,2},{3,11},{11,3},{4,12},{12,4},... | collective-permute-start | bytes 2304008 | tf_op jit(solution)/shard_map/ppermute | solution.py:192
  60.5 13.8 %collective-permute-start.10 = (bf16[750,250]{1,0:T(8,128)(2,1)}, bf16[750,250]{1,0:T(8,128)(2,1)S(1)}, u32[]{:S(2)}, u32[]{:S(2)}) collective-permute-start(bf16[750,250]{1,0:T(8,128)(2,1)} %refs_0_.5), channel_id=1, source_target_pairs={{0,7},{1,0},{2,1},{3,2},{4,3},{5,4},{6,5},{7,6},{8,15},{9,8},{10,9... | collective-permute-start | bytes 1125008 | tf_op jit(solution)/shard_map/ppermute | solution.py:27
  65.1 12.8 %collective-permute-start.11 = (bf16[750,250]{1,0:T(8,128)(2,1)S(1)}, bf16[750,250]{1,0:T(8,128)(2,1)S(1)}, u32[]{:S(2)}, u32[]{:S(2)}) collective-permute-start(bf16[750,250]{1,0:T(8,128)(2,1)S(1)} %collective-permute-done.9.refs_1_), channel_id=1, source_target_pairs={{0,1},{1,2},{2,3},{3,4},{4,5},{5,6},{6,7},{7,0},{8,9},{9,10},{10,1... | collective-permute-start | bytes 1125008 | tf_op jit(solution)/shard_map/ppermute | solution.py:27
  74.3 12.4 %collective-permute-start.12 = (bf16[750,250]{1,0:T(8,128)(2,1)S(1)}, bf16[750,250]{1,0:T(8,128)(2,1)S(1)}, u32[]{:S(2)}, u32[]{:S(2)}) collective-permute-start(bf16[750,250]{1,0:T(8,128)(2,1)S(1)} %collective-permute-done.10.refs_2_), channel_id=1, source_target_pairs={{0,7},{1,0},{2,1},{3,2},{4,3},{5,4},{6,5},{7,6},{8,15},{9,8},{10,9... | collective-permute-start | bytes 1125008 | tf_op jit(solution)/shard_map/ppermute | solution.py:27
  77.9 12.2 %collective-permute-start.13 = (bf16[750,250]{1,0:T(8,128)(2,1)S(1)}, bf16[750,250]{1,0:T(8,128)(2,1)S(1)}, u32[]{:S(2)}, u32[]{:S(2)}) collective-permute-start(bf16[750,250]{1,0:T(8,128)(2,1)S(1)} %collective-permute-done.11.refs_3_), channel_id=1, source_target_pairs={{0,1},{1,2},{2,3},{3,4},{4,5},{5,6},{6,7},{7,0},{8,9},{9,10},{10,1... | collective-permute-start | bytes 1125008 | tf_op jit(solution)/shard_map/ppermute | solution.py:27
  83.3 27.5 %copy-start.2 = (bf16[256,1500]{1,0:T(8,128)(2,1)}, bf16[256,1500]{1,0:T(8,128)(2,1)S(1)}, u32[]{:S(2)}) copy-start(bf16[256,1500]{1,0:T(8,128)(2,1)S(1)} %get-tuple-element.20.low) | copy-start | bytes 2304004
  83.3 40.1 %copy-start.1 = (bf16[750,250]{1,0:T(8,128)(2,1)S(1)}, bf16[750,250]{1,0:T(8,128)(2,1)}, u32[]{:S(2)}) copy-start(bf16[750,250]{1,0:T(8,128)(2,1)} %refs_0_.5) | copy-start | bytes 1125004
  86.6 36.8 %copy-start.4 = (bf16[256,1500]{1,0:T(8,128)(2,1)}, bf16[256,1500]{1,0:T(8,128)(2,1)S(1)}, u32[]{:S(2)}) copy-start(bf16[256,1500]{1,0:T(8,128)(2,1)S(1)} %get-tuple-element.22.high) | copy-start | bytes 2304004
  86.6 46.4 %copy-start.7 = (s32[8]{0:T(128)S(1)}, s32[8]{0:T(128)}, u32[]{:S(2)}) copy-start(s32[8]{0:T(128)} %constant.37.clone) | copy-start | bytes 100
  86.6 6.9 %collective-permute-start.1 = (bf16[64,750]{1,0:T(8,128)(2,1)S(1)}, bf16[64,750]{1,0:T(8,128)(2,1)S(1)}, u32[]{:S(2)}, u32[]{:S(2)}) collective-permute-start(bf16[64,750]{1,0:T(8,128)(2,1)S(1)} %get-tuple-element.27), channel_id=1, source_target_pairs={{0,1},{1,2},{2,3},{3,4},{4,5},{5,6},{6,7},{7,0},{8,9},{9,10},{10,1... | collective-permute-start | bytes 288008 | tf_op jit(solution)/shard_map/ppermute | solution.py:27
  86.7 30.9 %collective-permute-start.14 = (bf16[750,250]{1,0:T(8,128)(2,1)S(1)}, bf16[750,250]{1,0:T(8,128)(2,1)S(1)}, u32[]{:S(2)}, u32[]{:S(2)}) collective-permute-start(bf16[750,250]{1,0:T(8,128)(2,1)S(1)} %collective-permute-done.12.refs_4_), channel_id=1, source_target_pairs={{0,7},{1,0},{2,1},{3,2},{4,3},{5,4},{6,5},{7,6},{8,15},{9,8},{10,9... | collective-permute-start | bytes 1125008 | tf_op jit(solution)/shard_map/ppermute | solution.py:27
  90.1 44.1 %copy-start.6 = (f32[2000]{0:T(1024)S(1)}, f32[2000]{0:T(1024)}, u32[]{:S(2)}) copy-start(f32[2000]{0:T(1024)} %param.9) | copy-start | bytes 24004
  90.1 33.3 %collective-permute-start.15 = (bf16[384,250]{1,0:T(8,128)(2,1)S(1)}, bf16[384,250]{1,0:T(8,128)(2,1)S(1)}, u32[]{:S(2)}, u32[]{:S(2)}) collective-permute-start(bf16[384,250]{1,0:T(8,128)(2,1)S(1)} %slice.24), channel_id=1, source_target_pairs={{0,1},{1,2},{2,3},{3,4},{4,5},{5,6},{6,7},{7,0},{8,9},{9,10},{10,1... | collective-permute-start | bytes 576008 | tf_op jit(solution)/shard_map/ppermute | solution.py:27
  90.2 9.4 %collective-permute-start.5 = (bf16[64,750]{1,0:T(8,128)(2,1)S(1)}, bf16[64,750]{1,0:T(8,128)(2,1)S(1)}, u32[]{:S(2)}, u32[]{:S(2)}) collective-permute-start(bf16[64,750]{1,0:T(8,128)(2,1)S(1)} %get-tuple-element.31), channel_id=1, source_target_pairs={{0,7},{1,0},{2,1},{3,2},{4,3},{5,4},{6,5},{7,6},{8,15},{9,8},{10,9... | collective-permute-start | bytes 288008 | tf_op jit(solution)/shard_map/ppermute | solution.py:27
  93.5 10.0 %collective-permute-start.2 = (bf16[128,750]{1,0:T(8,128)(2,1)S(1)}, bf16[128,750]{1,0:T(8,128)(2,1)S(1)}, u32[]{:S(2)}, u32[]{:S(2)}) collective-permute-start(bf16[128,750]{1,0:T(8,128)(2,1)S(1)} %add_convert_fusion.6), channel_id=1, source_target_pairs={{0,1},{1,2},{2,3},{3,4},{4,5},{5,6},{6,7},{7,0},{8,9},{9,10},{10,1... | collective-permute-start | bytes 576008 | tf_op jit(solution)/shard_map/ppermute | solution.py:27
  99.7 7.0 %collective-permute-start.6 = (bf16[128,750]{1,0:T(8,128)(2,1)S(1)}, bf16[128,750]{1,0:T(8,128)(2,1)S(1)}, u32[]{:S(2)}, u32[]{:S(2)}) collective-permute-start(bf16[128,750]{1,0:T(8,128)(2,1)S(1)} %add_convert_fusion.3), channel_id=1, source_target_pairs={{0,7},{1,0},{2,1},{3,2},{4,3},{5,4},{6,5},{7,6},{8,15},{9,8},{10,9... | collective-permute-start | bytes 576008 | tf_op jit(solution)/shard_map/ppermute | solution.py:27
  103.5 7.2 %collective-permute-start.3 = (bf16[128,750]{1,0:T(8,128)(2,1)S(1)}, bf16[128,750]{1,0:T(8,128)(2,1)S(1)}, u32[]{:S(2)}, u32[]{:S(2)}) collective-permute-start(bf16[128,750]{1,0:T(8,128)(2,1)S(1)} %add_convert_fusion.5), channel_id=1, source_target_pairs={{0,1},{1,2},{2,3},{3,4},{4,5},{5,6},{6,7},{7,0},{8,9},{9,10},{10,1... | collective-permute-start | bytes 576008 | tf_op jit(solution)/shard_map/ppermute | solution.py:27
  106.7 7.1 %collective-permute-start.7 = (bf16[128,750]{1,0:T(8,128)(2,1)S(1)}, bf16[128,750]{1,0:T(8,128)(2,1)S(1)}, u32[]{:S(2)}, u32[]{:S(2)}) collective-permute-start(bf16[128,750]{1,0:T(8,128)(2,1)S(1)} %add_convert_fusion.2), channel_id=1, source_target_pairs={{0,7},{1,0},{2,1},{3,2},{4,3},{5,4},{6,5},{7,6},{8,15},{9,8},{10,9... | collective-permute-start | bytes 576008 | tf_op jit(solution)/shard_map/ppermute | solution.py:27
  110.8 12.6 %collective-permute-start.4 = (bf16[128,750]{1,0:T(8,128)(2,1)S(1)}, bf16[128,750]{1,0:T(8,128)(2,1)S(1)}, u32[]{:S(2)}, u32[]{:S(2)}) collective-permute-start(bf16[128,750]{1,0:T(8,128)(2,1)S(1)} %add_convert_fusion.4), channel_id=1, source_target_pairs={{0,1},{1,2},{2,3},{3,4},{4,5},{5,6},{6,7},{7,0},{8,9},{9,10},{10,1... | collective-permute-start | bytes 576008 | tf_op jit(solution)/shard_map/ppermute | solution.py:27
  113.9 9.5 %collective-permute-start.8 = (bf16[128,750]{1,0:T(8,128)(2,1)S(1)}, bf16[128,750]{1,0:T(8,128)(2,1)S(1)}, u32[]{:S(2)}, u32[]{:S(2)}) collective-permute-start(bf16[128,750]{1,0:T(8,128)(2,1)S(1)} %add_convert_fusion.1), channel_id=1, source_target_pairs={{0,7},{1,0},{2,1},{3,2},{4,3},{5,4},{6,5},{7,6},{8,15},{9,8},{10,9... | collective-permute-start | bytes 576008 | tf_op jit(solution)/shard_map/ppermute | solution.py:27
  117.7 5.7 %collective-permute-start.16 = (bf16[366,250]{1,0:T(8,128)(2,1)S(1)}, bf16[366,250]{1,0:T(8,128)(2,1)S(1)}, u32[]{:S(2)}, u32[]{:S(2)}) collective-permute-start(bf16[366,250]{1,0:T(8,128)(2,1)S(1)} %slice.25), channel_id=1, source_target_pairs={{0,7},{1,0},{2,1},{3,2},{4,3},{5,4},{6,5},{7,6},{8,15},{9,8},{10,9... | collective-permute-start | bytes 549008 | tf_op jit(solution)/shard_map/ppermute | solution.py:27
  124.7 1.7 collective-permute-start.17
  127.1 15.3 %all-to-all-start.1 = ((bf16[8,64,256]{2,1,0:T(8,128)(2,1)}), bf16[8,64,256]{2,1,0:T(8,128)(2,1)S(1)}, u32[]{:S(2)}, u32[]{:S(2)}) async-start(bf16[8,64,256]{2,1,0:T(8,128)(2,1)} %add_convert_fusion), calls=%async_computation.1 | async-start | bytes 524288 | tf_op jit(solution)/shard_map/all_to_all | solution.py:48
  142.4 43.9 %copy-start.3 = (bf16[256,1500]{1,0:T(8,128)(2,1)S(1)}, bf16[256,1500]{1,0:T(8,128)(2,1)}, u32[]{:S(2)}) copy-start(bf16[256,1500]{1,0:T(8,128)(2,1)} %copy-done.2) | copy-start | bytes 2304004
  142.4 43.9 %copy-start.5 = (bf16[256,1500]{1,0:T(8,128)(2,1)S(1)}, bf16[256,1500]{1,0:T(8,128)(2,1)}, u32[]{:S(2)}) copy-start(bf16[256,1500]{1,0:T(8,128)(2,1)} %copy-done.4) | copy-start | bytes 2304004
  157.4 4.5 %collective-permute-start.26 = (bf16[8,64,256]{2,1,0:T(8,128)(2,1)S(1)}, bf16[8,64,256]{2,1,0:T(8,128)(2,1)S(1)}, u32[]{:S(2)}, u32[]{:S(2)}) collective-permute-start(bf16[8,64,256]{2,1,0:T(8,128)(2,1)S(1)} %all_to_all.15.response), channel_id=1, source_target_pairs={{0,8},{8,0},{1,9},{9,1},{2,10},{10,2},{3,11},{11,3},{4,12},{12,4},... | collective-permute-start | bytes 786440 | tf_op jit(solution)/shard_map/ppermute | solution.py:244
  158.5 7.8 %collective-permute-start.18 = (bf16[64,750]{1,0:T(8,128)(2,1)S(1)}, bf16[64,750]{1,0:T(8,128)(2,1)S(1)}, u32[]{:S(2)}, u32[]{:S(2)}) collective-permute-start(bf16[64,750]{1,0:T(8,128)(2,1)S(1)} %shard_map.70.refs_0_), channel_id=1, source_target_pairs={{0,1},{1,2},{2,3},{3,4},{4,5},{5,6},{6,7},{7,0},{8,9},{9,10},{10,1... | collective-permute-start | bytes 288008 | tf_op jit(solution)/shard_map/ppermute | solution.py:27
  158.6 7.7 %collective-permute-start.19 = (bf16[64,750]{1,0:T(8,128)(2,1)S(1)}, bf16[64,750]{1,0:T(8,128)(2,1)S(1)}, u32[]{:S(2)}, u32[]{:S(2)}) collective-permute-start(bf16[64,750]{1,0:T(8,128)(2,1)S(1)} %shard_map.70.refs_0_), channel_id=1, source_target_pairs={{0,7},{1,0},{2,1},{3,2},{4,3},{5,4},{6,5},{7,6},{8,15},{9,8},{10,9... | collective-permute-start | bytes 288008 | tf_op jit(solution)/shard_map/ppermute | solution.py:27
  162.9 6.6 %collective-permute-start.27 = (bf16[64,750]{1,0:T(8,128)(2,1)S(1)}, bf16[64,750]{1,0:T(8,128)(2,1)S(1)}, u32[]{:S(2)}, u32[]{:S(2)}) collective-permute-start(bf16[64,750]{1,0:T(8,128)(2,1)S(1)} %shard_map.71.refs_9_), channel_id=1, source_target_pairs={{0,1},{1,2},{2,3},{3,4},{4,5},{5,6},{6,7},{7,0},{8,9},{9,10},{10,1... | collective-permute-start | bytes 288008 | tf_op jit(solution)/shard_map/ppermute | solution.py:27
  163.1 6.5 %collective-permute-start.28 = (bf16[64,750]{1,0:T(8,128)(2,1)S(1)}, bf16[64,750]{1,0:T(8,128)(2,1)S(1)}, u32[]{:S(2)}, u32[]{:S(2)}) collective-permute-start(bf16[64,750]{1,0:T(8,128)(2,1)S(1)} %shard_map.71.refs_9_), channel_id=1, source_target_pairs={{0,7},{1,0},{2,1},{3,2},{4,3},{5,4},{6,5},{7,6},{8,15},{9,8},{10,9... | collective-permute-start | bytes 288008 | tf_op jit(solution)/shard_map/ppermute | solution.py:27
  166.3 6.5 %collective-permute-start.20 = (bf16[64,750]{1,0:T(8,128)(2,1)S(1)}, bf16[64,750]{1,0:T(8,128)(2,1)S(1)}, u32[]{:S(2)}, u32[]{:S(2)}) collective-permute-start(bf16[64,750]{1,0:T(8,128)(2,1)S(1)} %collective-permute-done.18.refs_1_), channel_id=1, source_target_pairs={{0,1},{1,2},{2,3},{3,4},{4,5},{5,6},{6,7},{7,0},{8,9},{9,10},{10,1... | collective-permute-start | bytes 288008 | tf_op jit(solution)/shard_map/ppermute | solution.py:27
  166.3 6.5 %collective-permute-start.21 = (bf16[64,750]{1,0:T(8,128)(2,1)S(1)}, bf16[64,750]{1,0:T(8,128)(2,1)S(1)}, u32[]{:S(2)}, u32[]{:S(2)}) collective-permute-start(bf16[64,750]{1,0:T(8,128)(2,1)S(1)} %collective-permute-done.19.refs_2_), channel_id=1, source_target_pairs={{0,7},{1,0},{2,1},{3,2},{4,3},{5,4},{6,5},{7,6},{8,15},{9,8},{10,9... | collective-permute-start | bytes 288008 | tf_op jit(solution)/shard_map/ppermute | solution.py:27
  169.5 6.5 %collective-permute-start.29 = (bf16[64,750]{1,0:T(8,128)(2,1)S(1)}, bf16[64,750]{1,0:T(8,128)(2,1)S(1)}, u32[]{:S(2)}, u32[]{:S(2)}) collective-permute-start(bf16[64,750]{1,0:T(8,128)(2,1)S(1)} %collective-permute-done.27.refs_10_), channel_id=1, source_target_pairs={{0,1},{1,2},{2,3},{3,4},{4,5},{5,6},{6,7},{7,0},{8,9},{9,10},{10,1... | collective-permute-start | bytes 288008 | tf_op jit(solution)/shard_map/ppermute | solution.py:27
  169.5 6.5 %collective-permute-start.30 = (bf16[64,750]{1,0:T(8,128)(2,1)S(1)}, bf16[64,750]{1,0:T(8,128)(2,1)S(1)}, u32[]{:S(2)}, u32[]{:S(2)}) collective-permute-start(bf16[64,750]{1,0:T(8,128)(2,1)S(1)} %collective-permute-done.28.refs_11_), channel_id=1, source_target_pairs={{0,7},{1,0},{2,1},{3,2},{4,3},{5,4},{6,5},{7,6},{8,15},{9,8},{10,9... | collective-permute-start | bytes 288008 | tf_op jit(solution)/shard_map/ppermute | solution.py:27
  172.8 6.6 %collective-permute-start.22 = (bf16[64,750]{1,0:T(8,128)(2,1)S(1)}, bf16[64,750]{1,0:T(8,128)(2,1)S(1)}, u32[]{:S(2)}, u32[]{:S(2)}) collective-permute-start(bf16[64,750]{1,0:T(8,128)(2,1)S(1)} %collective-permute-done.20.refs_3_), channel_id=1, source_target_pairs={{0,1},{1,2},{2,3},{3,4},{4,5},{5,6},{6,7},{7,0},{8,9},{9,10},{10,1... | collective-permute-start | bytes 288008 | tf_op jit(solution)/shard_map/ppermute | solution.py:27
  172.8 6.6 %collective-permute-start.23 = (bf16[64,750]{1,0:T(8,128)(2,1)S(1)}, bf16[64,750]{1,0:T(8,128)(2,1)S(1)}, u32[]{:S(2)}, u32[]{:S(2)}) collective-permute-start(bf16[64,750]{1,0:T(8,128)(2,1)S(1)} %collective-permute-done.21.refs_4_), channel_id=1, source_target_pairs={{0,7},{1,0},{2,1},{3,2},{4,3},{5,4},{6,5},{7,6},{8,15},{9,8},{10,9... | collective-permute-start | bytes 288008 | tf_op jit(solution)/shard_map/ppermute | solution.py:27
  176.0 6.9 %collective-permute-start.31 = (bf16[64,750]{1,0:T(8,128)(2,1)S(1)}, bf16[64,750]{1,0:T(8,128)(2,1)S(1)}, u32[]{:S(2)}, u32[]{:S(2)}) collective-permute-start(bf16[64,750]{1,0:T(8,128)(2,1)S(1)} %collective-permute-done.29.refs_12_), channel_id=1, source_target_pairs={{0,1},{1,2},{2,3},{3,4},{4,5},{5,6},{6,7},{7,0},{8,9},{9,10},{10,1... | collective-permute-start | bytes 288008 | tf_op jit(solution)/shard_map/ppermute | solution.py:27
  176.0 7.0 %collective-permute-start.32 = (bf16[64,750]{1,0:T(8,128)(2,1)S(1)}, bf16[64,750]{1,0:T(8,128)(2,1)S(1)}, u32[]{:S(2)}, u32[]{:S(2)}) collective-permute-start(bf16[64,750]{1,0:T(8,128)(2,1)S(1)} %collective-permute-done.30.refs_13_), channel_id=1, source_target_pairs={{0,7},{1,0},{2,1},{3,2},{4,3},{5,4},{6,5},{7,6},{8,15},{9,8},{10,9... | collective-permute-start | bytes 288008 | tf_op jit(solution)/shard_map/ppermute | solution.py:27
  179.4 7.1 %collective-permute-start.24 = (bf16[32,750]{1,0:T(8,128)(2,1)S(1)}, bf16[32,750]{1,0:T(8,128)(2,1)S(1)}, u32[]{:S(2)}, u32[]{:S(2)}) collective-permute-start(bf16[32,750]{1,0:T(8,128)(2,1)S(1)} %slice.26), channel_id=1, source_target_pairs={{0,1},{1,2},{2,3},{3,4},{4,5},{5,6},{6,7},{7,0},{8,9},{9,10},{10,1... | collective-permute-start | bytes 144008 | tf_op jit(solution)/shard_map/ppermute | solution.py:27
  179.4 7.0 %collective-permute-start.25 = (bf16[32,750]{1,0:T(8,128)(2,1)S(1)}, bf16[32,750]{1,0:T(8,128)(2,1)S(1)}, u32[]{:S(2)}, u32[]{:S(2)}) collective-permute-start(bf16[32,750]{1,0:T(8,128)(2,1)S(1)} %slice.27), channel_id=1, source_target_pairs={{0,7},{1,0},{2,1},{3,2},{4,3},{5,4},{6,5},{7,6},{8,15},{9,8},{10,9... | collective-permute-start | bytes 144008 | tf_op jit(solution)/shard_map/ppermute | solution.py:27
  182.9 5.4 %collective-permute-start.33 = (bf16[32,750]{1,0:T(8,128)(2,1)S(1)}, bf16[32,750]{1,0:T(8,128)(2,1)S(1)}, u32[]{:S(2)}, u32[]{:S(2)}) collective-permute-start(bf16[32,750]{1,0:T(8,128)(2,1)S(1)} %slice.28), channel_id=1, source_target_pairs={{0,1},{1,2},{2,3},{3,4},{4,5},{5,6},{6,7},{7,0},{8,9},{9,10},{10,1... | collective-permute-start | bytes 144008 | tf_op jit(solution)/shard_map/ppermute | solution.py:27
  183.0 5.3 %collective-permute-start.34 = (bf16[32,750]{1,0:T(8,128)(2,1)S(1)}, bf16[32,750]{1,0:T(8,128)(2,1)S(1)}, u32[]{:S(2)}, u32[]{:S(2)}) collective-permute-start(bf16[32,750]{1,0:T(8,128)(2,1)S(1)} %slice.29), channel_id=1, source_target_pairs={{0,7},{1,0},{2,1},{3,2},{4,3},{5,4},{6,5},{7,6},{8,15},{9,8},{10,9... | collective-permute-start | bytes 144008 | tf_op jit(solution)/shard_map/ppermute | solution.py:27

commit v4 on v3

--- a/solution.py
+++ b/solution.py
@@ -52,21 +52,11 @@
     return lax.dot_general(a, b, ((over[:1], over[1:]), ((), ())), preferred_element_type=WIDE)
 
 
-def copies_kernel(shard, out, sent):
-    copies = [pltpu.make_async_copy(shard, out.at[n], sent.at[n]) for n in range(out.shape[0])]
-    for copy in copies:
-        copy.start()
-    for copy in copies:
-        copy.wait()
-
-
 def turn_and_multiply(at, held, pert, turned, image):
     size, share, _ = held.shape
     for d in range(size):
         turned[d * share : (d + 1) * share, :] = held[lax.rem(at[0] + d, size)]
-
-    @pl.loop(0, pert.shape[0])
-    def _(p):
+    for p in range(pert.shape[0]):
         image[p] = dot(turned[...], pert[p], (1, 1)).astype(NARROW)
 
 
@@ -125,12 +115,17 @@
     total = 0.0
     for n, chunk in enumerate(chunks):
         total += dot(response[n][:, :width], chunk[...], (1, 1))
-    out[...] = total.astype(NARROW)
-
-
-def join_kernel(low, high, out):
-    out[: low.shape[0], :] = low[...]
-    out[low.shape[0] :, :] = high[...]
+    rows = total.shape[1]
+    out[:, :rows] = total.astype(NARROW)
+    out[:, rows:] = jnp.zeros((out.shape[0], out.shape[1] - rows), NARROW)
+
+
+def join_kernel(at, mine, yours, out):
+    k = at[1]
+    size, _, share, _ = out.shape
+    for core, held in ((k, mine), (1 - k, yours)):
+        for d in range(size):
+            out[d, core] = held[d * share : (d + 1) * share, :]
 
 
 def density_kernel(at, turned, *refs):
@@ -139,34 +134,19 @@
     perts = out.shape[1]
     group = len(refs) // perts
     size = group - 1
-    block, rows = refs[0].shape
-    share, tile = block // CORES, out.shape[0]
-
-    def stretch(low, width):
-        lanes = pl.ds(low, width)
-        waves = []
-        for w in range(perts):
-            *pieces, first, last = refs[w * group : (w + 1) * group]
-            at_block = {d: piece[:, lanes] for d, piece in zip(ring_order(size), pieces)}
-            at_block[size // 2] = jnp.concatenate([first[:, lanes], last[:, lanes]], axis=0)
-            waves.append(at_block)
-        for p in range(perts):
-            mine, yours = waves
-            block_of = {d: jnp.where(k == p, mine[d], yours[d]) for d in range(size)}
-            left = [block_of[d][:share] for d in range(size)], [block_of[d][share:] for d in range(size)]
-            ahead = [jnp.where(k == 0, a, b) for a, b in zip(*left)]
-            left = jnp.concatenate(ahead + [jnp.where(k == 0, b, a) for a, b in zip(*left)], axis=0)
-            out[:width, p, :] = dot(left, turned[...], (0, 0)).astype(NARROW)
-
-    step, whole = pl.program_id(0), rows // tile
-
-    @pl.when(step < whole)
-    def _():
-        stretch(pl.multiple_of(step * tile, tile), tile)
-
-    @pl.when(step >= whole)
-    def _():
-        stretch(whole * tile, rows - whole * tile)
+    tile = out.shape[0]
+    lanes = pl.ds(pl.multiple_of(pl.program_id(0) * tile, tile), tile)
+    waves = []
+    for w in range(perts):
+        *pieces, first, last = refs[w * group : (w + 1) * group]
+        at_block = {d: piece[:, lanes] for d, piece in zip(ring_order(size), pieces)}
+        at_block[size // 2] = jnp.concatenate([first[:, lanes], last[:, lanes]], axis=0)
+        waves.append(at_block)
+    mine, yours = waves
+    for p in range(perts):
+        left = [jnp.where(k == p, mine[d], yours[d]) for d in range(size)]
+        total = dot(jnp.concatenate(left, axis=0), turned[...], (0, 0))
+        out[:, p, :] = total.astype(NARROW)
 
 
 def per_device(perturbation, occ_coeffs, vir_coeffs, occ_energies, vir_energies):
@@ -180,15 +160,7 @@
 
     mid = up_to(rows // 2, LANES)
     occ = ring_gather(occ_coeffs, "y", mid)
-    anywhere = pl.BlockSpec(memory_space=pl.ANY)
-    own = pl.pallas_call(
-        copies_kernel,
-        in_specs=[anywhere],
-        out_specs=anywhere,
-        out_shape=shape_of(nx, share, cols),
-        scratch_shapes=[pltpu.SemaphoreType.DMA((nx,))],
-    )(vir_coeffs.T)
-    own = exchanged(own, "x")
+    own = exchanged(jnp.broadcast_to(vir_coeffs.T, (nx, share, cols)), "x")
     other = lax.ppermute(own, "k", SWAP)
 
     piece = shape_of(perts * block, rows)
@@ -242,24 +214,24 @@
     )(terms, levels, virtual)
     response = exchanged(response, "x")
     sibling = lax.ppermute(response, "k", SWAP)
+    tile = 2 * LANES
     pieces = []
     for part in (response, sibling):
         mixed = pl.pallas_call(
             mixed_kernel,
             in_specs=[kept] * (1 + ny),
             out_specs=kept,
-            out_shape=half,
+            out_shape=shape_of(block, up_to(rows, tile)),
             compiler_params=ROOMY,
         )(part, *occ[:-2], far)
         pieces += ring_gather(mixed, "y", share)
     turned = pl.pallas_call(
         join_kernel,
-        in_specs=[kept] * 2,
+        in_specs=[SCALAR, kept, kept],
         out_specs=kept,
-        out_shape=shape_of(nx * block, cols),
-        compiler_params=ROOMY,
-    )(turned, other_turned)
-    tile = 2 * LANES
+        out_shape=shape_of(nx, CORES, share, cols),
+        compiler_params=ROOMY,
+    )(at, turned, other_turned).reshape(nx * block, cols)
     total = pl.pallas_call(
         density_kernel,
         grid=(pl.cdiv(rows, tile),),

time: 197 us -> 174 us (0.88)
  Pallas kernels: 39.6 us -> 14.6 us
    pallas_call x2 -> x1, Pallas kernels: 25.1 us -> 0.65 us  [per_device(): pl.pallas_call(join_kernel, in_specs=[SCALAR, kept, kept], out_specs=kept...]
  transfers between devices with their start and end apart: 37 -> 37, of which waited for: 11 -> 10; matrix products, arithmetic and copies ran while one was open for 2% -> 3% of each run, Pallas kernels for 4% -> 4%
where the time goes in v4:
time: 174 us; the launch traced here: 170 us
  starting transfers between devices  82.5 us (47%)
  waiting for transfers between devices  50.5 us (29%)
  blocking collectives  14.9 us (9%)
  Pallas kernels  14.6 us (8%)
  local copies, waits for them, and re-layouts  5.86 us (3%)
    ppermute x32, starting transfers between devices, turn(): lax.ppermute(shard, axis, [(i, (i + step) % size) for i in range(size)])  53.8 us
    all_to_all x2, starting transfers between devices, exchanged(): return lax.all_to_all(pieces, axis, split_axis=0, concat_axis=0, tiled=True)  28.5 us
    ppermute x32, waiting for transfers between devices, turn(): lax.ppermute(shard, axis, [(i, (i + step) % size) for i in range(size)])  28.3 us
    all_to_all x2, waiting for transfers between devices, exchanged(): return lax.all_to_all(pieces, axis, split_axis=0, concat_axis=0, tiled=True)  20.7 us
    all_to_all x1, blocking collectives, exchanged(): return lax.all_to_all(pieces, axis, split_axis=0, concat_axis=0, tiled=True)  14.9 us
    pallas_call x1, Pallas kernels, per_device(): pl.pallas_call(density_kernel, grid=(pl.cdiv(rows, tile),), in_specs=[SCA...  5.63 us
  transfers between devices with their start and end apart: 37, of which 10 were waited for; matrix products, arithmetic and copies ran while one was open for 3% of the time, Pallas kernels for 4%

profile of v4, /device:TPU:516, one launch (start us, length us, event | category | flops | bytes accessed | tf_op | source)
XLA Modules:
  0.0 170.5 jit_solution(1557971742910949548)
XLA Ops:
  0.0 1.8 %broadcast_in_dim.6 = bf16[8,32,1500]{2,1,0:T(8,128)(2,1)} broadcast(bf16[32,1500]{1,0:T(8,128)(2,1)} %bitcast.9), dimensions={1,2} | broadcast | bytes 864000 | tf_op jit(solution)/shard_map/broadcast_in_dim | solution.py:163
  1.9 22.7 %all-to-all-start = ((bf16[8,32,1500]{2,1,0:T(8,128)(2,1)}), bf16[8,32,1500]{2,1,0:T(8,128)(2,1)S(1)}, u32[]{:S(2)}, u32[]{:S(2)}) async-start(bf16[8,32,1500]{2,1,0:T(8,128)(2,1)} %broadcast_in_dim.6), calls=%async_computation | async-start | bytes 1572864 | tf_op jit(solution)/shard_map/all_to_all | solution.py:48
  24.6 0.0 collective-permute-start.9
  24.6 12.8 %all-to-all-done.held = bf16[8,32,1500]{2,1,0:T(8,128)(2,1)S(1)} async-done(((bf16[8,32,1500]{2,1,0:T(8,128)(2,1)}), bf16[8,32,1500]{2,1,0:T(8,128)(2,1)S(1)}, u32[]{:S(2)}, u32[]{:S(2)}) %all-to-all-start) | async-done | bytes 768032 | tf_op jit(solution)/shard_map/all_to_all | solution.py:48
  37.4 0.0 collective-permute-start
  37.4 4.6 %collective-permute-start.10 = (bf16[750,250]{1,0:T(8,128)(2,1)}, bf16[750,250]{1,0:T(8,128)(2,1)S(1)}, u32[]{:S(2)}, u32[]{:S(2)}) collective-permute-start(bf16[750,250]{1,0:T(8,128)(2,1)} %refs_0_.5), channel_id=1, source_target_pairs={{0,7},{1,0},{2,1},{3,2},{4,3},{5,4},{6,5},{7,6},{8,15},{9,8},{10,9... | collective-permute-start | bytes 1125008 | tf_op jit(solution)/shard_map/ppermute | solution.py:27
  42.0 0.0 collective-permute-done.9.refs_1_
  42.0 0.0 collective-permute-start.11
  42.0 9.2 %collective-permute-done.10.refs_2_ = bf16[750,250]{1,0:T(8,128)(2,1)S(1)} collective-permute-done((bf16[750,250]{1,0:T(8,128)(2,1)}, bf16[750,250]{1,0:T(8,128)(2,1)S(1)}, u32[]{:S(2)}, u32[]{:S(2)}) %collective-permute-start.10) | collective-permute-done | bytes 375032 | tf_op jit(solution)/shard_map/ppermute | solution.py:27
  51.2 3.6 %collective-permute-start.12 = (bf16[750,250]{1,0:T(8,128)(2,1)S(1)}, bf16[750,250]{1,0:T(8,128)(2,1)S(1)}, u32[]{:S(2)}, u32[]{:S(2)}) collective-permute-start(bf16[750,250]{1,0:T(8,128)(2,1)S(1)} %collective-permute-done.10.refs_2_), channel_id=1, source_target_pairs={{0,7},{1,0},{2,1},{3,2},{4,3},{5,4},{6,5},{7,6},{8,15},{9,8},{10,9... | collective-permute-start | bytes 1125008 | tf_op jit(solution)/shard_map/ppermute | solution.py:27
  54.7 3.0 %copy.7.pert = bf16[2,750,1500]{2,1,0:T(8,128)(2,1)S(1)} copy(bf16[2,750,1500]{2,0,1:T(2,128)(2,1)} %param.6) | data formatting | bytes 9000000 | tf_op args[0]
  57.8 0.1 pad_add_fusion.at
  57.9 2.0 %shard_map.64 = (bf16[256,1500]{1,0:T(8,128)(2,1)S(1)}, bf16[2,256,750]{2,1,0:T(8,128)(2,1)S(1)}) custom-call(s32[2]{0:T(128)S(1)} %pad_add_fusion.at, bf16[8,32,1500]{2,1,0:T(8,128)(2,1)S(1)} %all-to-all-done.held, bf16[2,750,1500]{2,1,0:T(8,128)(2,1)S(1)} %copy.7.pert), custom_call_target="tpu_custom_call" | custom-call | tf_op jit(solution)/shard_map/pallas_call | solution.py:170
  59.8 0.0 copy-start.2
  59.9 0.0 copy-start.1
  59.9 2.9 %shard_map.65 = (bf16[256,1500]{1,0:T(8,128)(2,1)S(1)}, bf16[64,750]{1,0:T(8,128)(2,1)S(1)}, bf16[64,750]{1,0:T(8,128)(2,1)S(1)}, bf16[128,750]{1,0:T(8,128)(2,1...) custom-call(s32[2]{0:T(128)S(1)} %pad_add_fusion.at, ...), custom_call_target="tpu_custom_call" | custom-call | tf_op jit(solution)/shard_map/pallas_call | solution.py:177
  62.8 0.0 copy-start.7
  62.9 0.1 collective-permute-start.1
  63.0 3.4 %collective-permute-start.14 = (bf16[750,250]{1,0:T(8,128)(2,1)S(1)}, bf16[750,250]{1,0:T(8,128)(2,1)S(1)}, u32[]{:S(2)}, u32[]{:S(2)}) collective-permute-start(bf16[750,250]{1,0:T(8,128)(2,1)S(1)} %collective-permute-done.12.refs_4_), channel_id=1, source_target_pairs={{0,7},{1,0},{2,1},{3,2},{4,3},{5,4},{6,5},{7,6},{8,15},{9,8},{10,9... | collective-permute-start | bytes 1125008 | tf_op jit(solution)/shard_map/ppermute | solution.py:27
  66.5 0.0 copy-start.6
  66.5 0.1 collective-permute-start.15
  66.6 3.2 %collective-permute-start.5 = (bf16[64,750]{1,0:T(8,128)(2,1)S(1)}, bf16[64,750]{1,0:T(8,128)(2,1)S(1)}, u32[]{:S(2)}, u32[]{:S(2)}) collective-permute-start(bf16[64,750]{1,0:T(8,128)(2,1)S(1)} %get-tuple-element.31), channel_id=1, source_target_pairs={{0,7},{1,0},{2,1},{3,2},{4,3},{5,4},{6,5},{7,6},{8,15},{9,8},{10,9... | collective-permute-start | bytes 288008 | tf_op jit(solution)/shard_map/ppermute | solution.py:27
  69.9 0.1 collective-permute-start.2
  70.0 5.9 %collective-permute-done.5 = bf16[64,750]{1,0:T(8,128)(2,1)S(1)} collective-permute-done((bf16[64,750]{1,0:T(8,128)(2,1)S(1)}, bf16[64,750]{1,0:T(8,128)(2,1)S(1)}, u32[]{:S(2)}, u32[]{:S(2)}) %collective-permute-start.5) | collective-permute-done | bytes 96032 | tf_op jit(solution)/shard_map/ppermute | solution.py:27
  75.9 4.0 %collective-permute-start.6 = (bf16[128,750]{1,0:T(8,128)(2,1)S(1)}, bf16[128,750]{1,0:T(8,128)(2,1)S(1)}, u32[]{:S(2)}, u32[]{:S(2)}) collective-permute-start(bf16[128,750]{1,0:T(8,128)(2,1)S(1)} %add_convert_fusion.3), channel_id=1, source_target_pairs={{0,7},{1,0},{2,1},{3,2},{4,3},{5,4},{6,5},{7,6},{8,15},{9,8},{10,9... | collective-permute-start | bytes 576008 | tf_op jit(solution)/shard_map/ppermute | solution.py:27
  80.0 0.1 collective-permute-start.3
  80.1 3.0 %collective-permute-done.6 = bf16[128,750]{1,0:T(8,128)(2,1)S(1)} collective-permute-done((bf16[128,750]{1,0:T(8,128)(2,1)S(1)}, bf16[128,750]{1,0:T(8,128)(2,1)S(1)}, u32[]{:S(2)}, u32[]{:S(2)}) %collective-permute-start.6) | collective-permute-done | bytes 192032 | tf_op jit(solution)/shard_map/ppermute | solution.py:27
  83.2 3.8 %collective-permute-start.7 = (bf16[128,750]{1,0:T(8,128)(2,1)S(1)}, bf16[128,750]{1,0:T(8,128)(2,1)S(1)}, u32[]{:S(2)}, u32[]{:S(2)}) collective-permute-start(bf16[128,750]{1,0:T(8,128)(2,1)S(1)} %add_convert_fusion.2), channel_id=1, source_target_pairs={{0,7},{1,0},{2,1},{3,2},{4,3},{5,4},{6,5},{7,6},{8,15},{9,8},{10,9... | collective-permute-start | bytes 576008 | tf_op jit(solution)/shard_map/ppermute | solution.py:27
  87.0 0.0 collective-permute-done.3
  87.0 0.1 collective-permute-start.4
  87.2 3.2 %collective-permute-done.7 = bf16[128,750]{1,0:T(8,128)(2,1)S(1)} collective-permute-done((bf16[128,750]{1,0:T(8,128)(2,1)S(1)}, bf16[128,750]{1,0:T(8,128)(2,1)S(1)}, u32[]{:S(2)}, u32[]{:S(2)}) %collective-permute-start.7) | collective-permute-done | bytes 192032 | tf_op jit(solution)/shard_map/ppermute | solution.py:27
  90.4 3.8 %collective-permute-start.8 = (bf16[128,750]{1,0:T(8,128)(2,1)S(1)}, bf16[128,750]{1,0:T(8,128)(2,1)S(1)}, u32[]{:S(2)}, u32[]{:S(2)}) collective-permute-start(bf16[128,750]{1,0:T(8,128)(2,1)S(1)} %add_convert_fusion.1), channel_id=1, source_target_pairs={{0,7},{1,0},{2,1},{3,2},{4,3},{5,4},{6,5},{7,6},{8,15},{9,8},{10,9... | collective-permute-start | bytes 576008 | tf_op jit(solution)/shard_map/ppermute | solution.py:27
  94.2 0.2 collective-permute-start.16
  94.4 5.5 %collective-permute-done.16.refs_8_ = bf16[366,250]{1,0:T(8,128)(2,1)S(1)} collective-permute-done((bf16[366,250]{1,0:T(8,128)(2,1)S(1)}, bf16[366,250]{1,0:T(8,128)(2,1)S(1)}, u32[]{:S(2)}, u32[]{:S(2)}) %collective-permute-start.16) | collective-permute-done | bytes 183032 | tf_op jit(solution)/shard_map/ppermute | solution.py:27
  100.0 1.3 shard_map.67
  101.2 0.1 collective-permute-start.17
  101.4 1.5 collective-permute-done.17
  102.9 0.8 add_convert_fusion
  103.7 5.8 %all-to-all-start.1 = ((bf16[8,64,256]{2,1,0:T(8,128)(2,1)}), bf16[8,64,256]{2,1,0:T(8,128)(2,1)S(1)}, u32[]{:S(2)}, u32[]{:S(2)}) async-start(bf16[8,64,256]{2,1,0:T(8,128)(2,1)} %add_convert_fusion), calls=%async_computation.1 | async-start | bytes 524288 | tf_op jit(solution)/shard_map/all_to_all | solution.py:48
  109.5 0.6 dynamic_slice.9
  110.8 0.1 reshape.7
  110.9 0.1 dynamic-slice_bitcast_fusion
  111.0 0.1 copy.9.virtual
  111.1 7.9 %all-to-all-done.1.terms = bf16[8,64,256]{2,1,0:T(8,128)(2,1)S(1)} async-done(((bf16[8,64,256]{2,1,0:T(8,128)(2,1)}), bf16[8,64,256]{2,1,0:T(8,128)(2,1)S(1)}, u32[]{:S(2)}, u32[]{:S(2)}) %all-to-all-start.1) | async-done | bytes 262176 | tf_op jit(solution)/shard_map/all_to_all | solution.py:48
  119.0 0.1 shard_map.68
  119.1 14.9 %all_to_all.15.response = bf16[8,64,256]{2,1,0:T(8,128)(2,1)S(1)} all-to-all(bf16[8,64,256]{2,1,0:T(8,128)(2,1)S(1)} %shard_map.68), channel_id=1, replica_groups=mesh['grp'=2,'x'=8,'k'=2,'y'=8] {'x'}, dimensions={0} | all-to-all | bytes 524288 | tf_op jit(solution)/shard_map/all_to_all | solution.py:48
  134.0 1.0 shard_map.69.refs_0_
  135.0 0.1 collective-permute-start.18
  135.1 3.3 %collective-permute-start.19 = (bf16[64,768]{1,0:T(8,128)(2,1)S(1)}, bf16[64,768]{1,0:T(8,128)(2,1)S(1)}, u32[]{:S(2)}, u32[]{:S(2)}) collective-permute-start(bf16[64,768]{1,0:T(8,128)(2,1)S(1)} %shard_map.69.refs_0_), channel_id=1, source_target_pairs={{0,7},{1,0},{2,1},{3,2},{4,3},{5,4},{6,5},{7,6},{8,15},{9,8},{10,9... | collective-permute-start | bytes 294920 | tf_op jit(solution)/shard_map/ppermute | solution.py:27
  138.4 1.0 shard_map.70.refs_9_
  139.5 0.1 collective-permute-start.27
  139.6 3.2 %collective-permute-start.28 = (bf16[64,768]{1,0:T(8,128)(2,1)S(1)}, bf16[64,768]{1,0:T(8,128)(2,1)S(1)}, u32[]{:S(2)}, u32[]{:S(2)}) collective-permute-start(bf16[64,768]{1,0:T(8,128)(2,1)S(1)} %shard_map.70.refs_9_), channel_id=1, source_target_pairs={{0,7},{1,0},{2,1},{3,2},{4,3},{5,4},{6,5},{7,6},{8,15},{9,8},{10,9... | collective-permute-start | bytes 294920 | tf_op jit(solution)/shard_map/ppermute | solution.py:27
  142.8 3.2 %collective-permute-start.21 = (bf16[64,768]{1,0:T(8,128)(2,1)S(1)}, bf16[64,768]{1,0:T(8,128)(2,1)S(1)}, u32[]{:S(2)}, u32[]{:S(2)}) collective-permute-start(bf16[64,768]{1,0:T(8,128)(2,1)S(1)} %collective-permute-done.19.refs_2_), channel_id=1, source_target_pairs={{0,7},{1,0},{2,1},{3,2},{4,3},{5,4},{6,5},{7,6},{8,15},{9,8},{10,9... | collective-permute-start | bytes 294920 | tf_op jit(solution)/shard_map/ppermute | solution.py:27
  146.1 3.2 %collective-permute-start.30 = (bf16[64,768]{1,0:T(8,128)(2,1)S(1)}, bf16[64,768]{1,0:T(8,128)(2,1)S(1)}, u32[]{:S(2)}, u32[]{:S(2)}) collective-permute-start(bf16[64,768]{1,0:T(8,128)(2,1)S(1)} %collective-permute-done.28.refs_11_), channel_id=1, source_target_pairs={{0,7},{1,0},{2,1},{3,2},{4,3},{5,4},{6,5},{7,6},{8,15},{9,8},{10,9... | collective-permute-start | bytes 294920 | tf_op jit(solution)/shard_map/ppermute | solution.py:27
  149.3 3.2 %collective-permute-start.23 = (bf16[64,768]{1,0:T(8,128)(2,1)S(1)}, bf16[64,768]{1,0:T(8,128)(2,1)S(1)}, u32[]{:S(2)}, u32[]{:S(2)}) collective-permute-start(bf16[64,768]{1,0:T(8,128)(2,1)S(1)} %collective-permute-done.21.refs_4_), channel_id=1, source_target_pairs={{0,7},{1,0},{2,1},{3,2},{4,3},{5,4},{6,5},{7,6},{8,15},{9,8},{10,9... | collective-permute-start | bytes 294920 | tf_op jit(solution)/shard_map/ppermute | solution.py:27
  152.6 3.2 %collective-permute-start.32 = (bf16[64,768]{1,0:T(8,128)(2,1)S(1)}, bf16[64,768]{1,0:T(8,128)(2,1)S(1)}, u32[]{:S(2)}, u32[]{:S(2)}) collective-permute-start(bf16[64,768]{1,0:T(8,128)(2,1)S(1)} %collective-permute-done.30.refs_13_), channel_id=1, source_target_pairs={{0,7},{1,0},{2,1},{3,2},{4,3},{5,4},{6,5},{7,6},{8,15},{9,8},{10,9... | collective-permute-start | bytes 294920 | tf_op jit(solution)/shard_map/ppermute | solution.py:27
  155.8 0.1 collective-permute-done.22.refs_5_
  155.9 0.0 collective-permute-start.24
  156.0 3.4 %collective-permute-start.25 = (bf16[32,768]{1,0:T(8,128)(2,1)S(1)}, bf16[32,768]{1,0:T(8,128)(2,1)S(1)}, u32[]{:S(2)}, u32[]{:S(2)}) collective-permute-start(bf16[32,768]{1,0:T(8,128)(2,1)S(1)} %slice.27), channel_id=1, source_target_pairs={{0,7},{1,0},{2,1},{3,2},{4,3},{5,4},{6,5},{7,6},{8,15},{9,8},{10,9... | collective-permute-start | bytes 147464 | tf_op jit(solution)/shard_map/ppermute | solution.py:27
  159.4 0.1 collective-permute-start.33
  159.6 3.3 %collective-permute-start.34 = (bf16[32,768]{1,0:T(8,128)(2,1)S(1)}, bf16[32,768]{1,0:T(8,128)(2,1)S(1)}, u32[]{:S(2)}, u32[]{:S(2)}) collective-permute-start(bf16[32,768]{1,0:T(8,128)(2,1)S(1)} %slice.29), channel_id=1, source_target_pairs={{0,7},{1,0},{2,1},{3,2},{4,3},{5,4},{6,5},{7,6},{8,15},{9,8},{10,9... | collective-permute-start | bytes 147464 | tf_op jit(solution)/shard_map/ppermute | solution.py:27
  162.9 0.6 shard_map.66
  163.6 1.3 collective-permute-done.33.refs_16_
  164.8 5.6 %shard_map.71 = bf16[750,2,1500]{2,1,0:T(2,128)(2,1)} custom-call(s32[2]{0:T(128)S(1)} %pad_add_fusion.at, bf16[512,1500]{1,0:T(8,128)(2,1)S(1)} %bitcast.8, bf16[64,768]{1,0:T(8,128)(2,1)S(1)} %shard_map.69.refs_0_, bf16[64,768]{1,0:T(8,128)(2,1)S(1)} %collective-permute-done.18.refs_1_, bf16[64,768]{1,0:T(8,128)(2,1)S(1)} %collective-permute-done.19.refs_2_, ...), custom_call_target="tpu_custom_call" | custom-call | tf_op jit(solution)/shard_map/pallas_call | solution.py:235
  (56 shorter events, 0.4 us)
Async XLA Ops:
  0.0 110.9 %copy-start = (f32[512]{0:T(512)S(1)}, f32[512]{0:T(512)}, u32[]{:S(2)}) copy-start(f32[512]{0:T(512)} %param.10) | copy-start | bytes 6148
  1.9 35.5 %all-to-all-start = ((bf16[8,32,1500]{2,1,0:T(8,128)(2,1)}), bf16[8,32,1500]{2,1,0:T(8,128)(2,1)S(1)}, u32[]{:S(2)}, u32[]{:S(2)}) async-start(bf16[8,32,1500]{2,1,0:T(8,128)(2,1)} %broadcast_in_dim.6), calls=%async_computation | async-start | bytes 1572864 | tf_op jit(solution)/shard_map/all_to_all | solution.py:48
  24.6 17.4 %collective-permute-start.9 = (bf16[750,250]{1,0:T(8,128)(2,1)}, bf16[750,250]{1,0:T(8,128)(2,1)S(1)}, u32[]{:S(2)}, u32[]{:S(2)}) collective-permute-start(bf16[750,250]{1,0:T(8,128)(2,1)} %refs_0_.5), channel_id=1, source_target_pairs={{0,1},{1,2},{2,3},{3,4},{4,5},{5,6},{6,7},{7,0},{8,9},{9,10},{10,1... | collective-permute-start | bytes 1125008 | tf_op jit(solution)/shard_map/ppermute | solution.py:27
  37.4 22.5 %collective-permute-start = (bf16[8,32,1500]{2,1,0:T(8,128)(2,1)S(1)}, bf16[8,32,1500]{2,1,0:T(8,128)(2,1)}, u32[]{:S(2)}, u32[]{:S(2)}) collective-permute-start(bf16[8,32,1500]{2,1,0:T(8,128)(2,1)S(1)} %all-to-all-done.held), channel_id=1, source_target_pairs={{0,8},{8,0},{1,9},{9,1},{2,10},{10,2},{3,11},{11,3},{4,12},{12,4},... | collective-permute-start | bytes 2304008 | tf_op jit(solution)/shard_map/ppermute | solution.py:164
  37.4 13.8 %collective-permute-start.10 = (bf16[750,250]{1,0:T(8,128)(2,1)}, bf16[750,250]{1,0:T(8,128)(2,1)S(1)}, u32[]{:S(2)}, u32[]{:S(2)}) collective-permute-start(bf16[750,250]{1,0:T(8,128)(2,1)} %refs_0_.5), channel_id=1, source_target_pairs={{0,7},{1,0},{2,1},{3,2},{4,3},{5,4},{6,5},{7,6},{8,15},{9,8},{10,9... | collective-permute-start | bytes 1125008 | tf_op jit(solution)/shard_map/ppermute | solution.py:27
  42.0 12.8 %collective-permute-start.11 = (bf16[750,250]{1,0:T(8,128)(2,1)S(1)}, bf16[750,250]{1,0:T(8,128)(2,1)S(1)}, u32[]{:S(2)}, u32[]{:S(2)}) collective-permute-start(bf16[750,250]{1,0:T(8,128)(2,1)S(1)} %collective-permute-done.9.refs_1_), channel_id=1, source_target_pairs={{0,1},{1,2},{2,3},{3,4},{4,5},{5,6},{6,7},{7,0},{8,9},{9,10},{10,1... | collective-permute-start | bytes 1125008 | tf_op jit(solution)/shard_map/ppermute | solution.py:27
  51.2 11.8 %collective-permute-start.12 = (bf16[750,250]{1,0:T(8,128)(2,1)S(1)}, bf16[750,250]{1,0:T(8,128)(2,1)S(1)}, u32[]{:S(2)}, u32[]{:S(2)}) collective-permute-start(bf16[750,250]{1,0:T(8,128)(2,1)S(1)} %collective-permute-done.10.refs_2_), channel_id=1, source_target_pairs={{0,7},{1,0},{2,1},{3,2},{4,3},{5,4},{6,5},{7,6},{8,15},{9,8},{10,9... | collective-permute-start | bytes 1125008 | tf_op jit(solution)/shard_map/ppermute | solution.py:27
  54.7 11.7 %collective-permute-start.13 = (bf16[750,250]{1,0:T(8,128)(2,1)S(1)}, bf16[750,250]{1,0:T(8,128)(2,1)S(1)}, u32[]{:S(2)}, u32[]{:S(2)}) collective-permute-start(bf16[750,250]{1,0:T(8,128)(2,1)S(1)} %collective-permute-done.11.refs_3_), channel_id=1, source_target_pairs={{0,1},{1,2},{2,3},{3,4},{4,5},{5,6},{6,7},{7,0},{8,9},{9,10},{10,1... | collective-permute-start | bytes 1125008 | tf_op jit(solution)/shard_map/ppermute | solution.py:27
  59.8 27.2 %copy-start.2 = (bf16[256,1500]{1,0:T(8,128)(2,1)}, bf16[256,1500]{1,0:T(8,128)(2,1)S(1)}, u32[]{:S(2)}) copy-start(bf16[256,1500]{1,0:T(8,128)(2,1)S(1)} %get-tuple-element.20.mine) | copy-start | bytes 2304004
  59.9 40.1 %copy-start.1 = (bf16[750,250]{1,0:T(8,128)(2,1)S(1)}, bf16[750,250]{1,0:T(8,128)(2,1)}, u32[]{:S(2)}) copy-start(bf16[750,250]{1,0:T(8,128)(2,1)} %refs_0_.5) | copy-start | bytes 1125004
  62.8 37.1 %copy-start.4 = (bf16[256,1500]{1,0:T(8,128)(2,1)}, bf16[256,1500]{1,0:T(8,128)(2,1)S(1)}, u32[]{:S(2)}) copy-start(bf16[256,1500]{1,0:T(8,128)(2,1)S(1)} %get-tuple-element.22.yours) | copy-start | bytes 2304004
  62.8 46.6 %copy-start.7 = (s32[8]{0:T(128)S(1)}, s32[8]{0:T(128)}, u32[]{:S(2)}) copy-start(s32[8]{0:T(128)} %constant.37.clone) | copy-start | bytes 100
  62.9 7.0 %collective-permute-start.1 = (bf16[64,750]{1,0:T(8,128)(2,1)S(1)}, bf16[64,750]{1,0:T(8,128)(2,1)S(1)}, u32[]{:S(2)}, u32[]{:S(2)}) collective-permute-start(bf16[64,750]{1,0:T(8,128)(2,1)S(1)} %get-tuple-element.27), channel_id=1, source_target_pairs={{0,1},{1,2},{2,3},{3,4},{4,5},{5,6},{6,7},{7,0},{8,9},{9,10},{10,1... | collective-permute-start | bytes 288008 | tf_op jit(solution)/shard_map/ppermute | solution.py:27
  63.0 31.2 %collective-permute-start.14 = (bf16[750,250]{1,0:T(8,128)(2,1)S(1)}, bf16[750,250]{1,0:T(8,128)(2,1)S(1)}, u32[]{:S(2)}, u32[]{:S(2)}) collective-permute-start(bf16[750,250]{1,0:T(8,128)(2,1)S(1)} %collective-permute-done.12.refs_4_), channel_id=1, source_target_pairs={{0,7},{1,0},{2,1},{3,2},{4,3},{5,4},{6,5},{7,6},{8,15},{9,8},{10,9... | collective-permute-start | bytes 1125008 | tf_op jit(solution)/shard_map/ppermute | solution.py:27
  66.5 44.3 %copy-start.6 = (f32[2000]{0:T(1024)S(1)}, f32[2000]{0:T(1024)}, u32[]{:S(2)}) copy-start(f32[2000]{0:T(1024)} %param.9) | copy-start | bytes 24004
  66.5 33.5 %collective-permute-start.15 = (bf16[384,250]{1,0:T(8,128)(2,1)S(1)}, bf16[384,250]{1,0:T(8,128)(2,1)S(1)}, u32[]{:S(2)}, u32[]{:S(2)}) collective-permute-start(bf16[384,250]{1,0:T(8,128)(2,1)S(1)} %slice.24), channel_id=1, source_target_pairs={{0,1},{1,2},{2,3},{3,4},{4,5},{5,6},{6,7},{7,0},{8,9},{9,10},{10,1... | collective-permute-start | bytes 576008 | tf_op jit(solution)/shard_map/ppermute | solution.py:27
  66.6 9.3 %collective-permute-start.5 = (bf16[64,750]{1,0:T(8,128)(2,1)S(1)}, bf16[64,750]{1,0:T(8,128)(2,1)S(1)}, u32[]{:S(2)}, u32[]{:S(2)}) collective-permute-start(bf16[64,750]{1,0:T(8,128)(2,1)S(1)} %get-tuple-element.31), channel_id=1, source_target_pairs={{0,7},{1,0},{2,1},{3,2},{4,3},{5,4},{6,5},{7,6},{8,15},{9,8},{10,9... | collective-permute-start | bytes 288008 | tf_op jit(solution)/shard_map/ppermute | solution.py:27
  69.9 10.1 %collective-permute-start.2 = (bf16[128,750]{1,0:T(8,128)(2,1)S(1)}, bf16[128,750]{1,0:T(8,128)(2,1)S(1)}, u32[]{:S(2)}, u32[]{:S(2)}) collective-permute-start(bf16[128,750]{1,0:T(8,128)(2,1)S(1)} %add_convert_fusion.6), channel_id=1, source_target_pairs={{0,1},{1,2},{2,3},{3,4},{4,5},{5,6},{6,7},{7,0},{8,9},{9,10},{10,1... | collective-permute-start | bytes 576008 | tf_op jit(solution)/shard_map/ppermute | solution.py:27
  75.9 7.2 %collective-permute-start.6 = (bf16[128,750]{1,0:T(8,128)(2,1)S(1)}, bf16[128,750]{1,0:T(8,128)(2,1)S(1)}, u32[]{:S(2)}, u32[]{:S(2)}) collective-permute-start(bf16[128,750]{1,0:T(8,128)(2,1)S(1)} %add_convert_fusion.3), channel_id=1, source_target_pairs={{0,7},{1,0},{2,1},{3,2},{4,3},{5,4},{6,5},{7,6},{8,15},{9,8},{10,9... | collective-permute-start | bytes 576008 | tf_op jit(solution)/shard_map/ppermute | solution.py:27
  80.0 7.0 %collective-permute-start.3 = (bf16[128,750]{1,0:T(8,128)(2,1)S(1)}, bf16[128,750]{1,0:T(8,128)(2,1)S(1)}, u32[]{:S(2)}, u32[]{:S(2)}) collective-permute-start(bf16[128,750]{1,0:T(8,128)(2,1)S(1)} %add_convert_fusion.5), channel_id=1, source_target_pairs={{0,1},{1,2},{2,3},{3,4},{4,5},{5,6},{6,7},{7,0},{8,9},{9,10},{10,1... | collective-permute-start | bytes 576008 | tf_op jit(solution)/shard_map/ppermute | solution.py:27
  83.2 7.2 %collective-permute-start.7 = (bf16[128,750]{1,0:T(8,128)(2,1)S(1)}, bf16[128,750]{1,0:T(8,128)(2,1)S(1)}, u32[]{:S(2)}, u32[]{:S(2)}) collective-permute-start(bf16[128,750]{1,0:T(8,128)(2,1)S(1)} %add_convert_fusion.2), channel_id=1, source_target_pairs={{0,7},{1,0},{2,1},{3,2},{4,3},{5,4},{6,5},{7,6},{8,15},{9,8},{10,9... | collective-permute-start | bytes 576008 | tf_op jit(solution)/shard_map/ppermute | solution.py:27
  87.0 12.9 %collective-permute-start.4 = (bf16[128,750]{1,0:T(8,128)(2,1)S(1)}, bf16[128,750]{1,0:T(8,128)(2,1)S(1)}, u32[]{:S(2)}, u32[]{:S(2)}) collective-permute-start(bf16[128,750]{1,0:T(8,128)(2,1)S(1)} %add_convert_fusion.4), channel_id=1, source_target_pairs={{0,1},{1,2},{2,3},{3,4},{4,5},{5,6},{6,7},{7,0},{8,9},{9,10},{10,1... | collective-permute-start | bytes 576008 | tf_op jit(solution)/shard_map/ppermute | solution.py:27
  90.4 9.5 %collective-permute-start.8 = (bf16[128,750]{1,0:T(8,128)(2,1)S(1)}, bf16[128,750]{1,0:T(8,128)(2,1)S(1)}, u32[]{:S(2)}, u32[]{:S(2)}) collective-permute-start(bf16[128,750]{1,0:T(8,128)(2,1)S(1)} %add_convert_fusion.1), channel_id=1, source_target_pairs={{0,7},{1,0},{2,1},{3,2},{4,3},{5,4},{6,5},{7,6},{8,15},{9,8},{10,9... | collective-permute-start | bytes 576008 | tf_op jit(solution)/shard_map/ppermute | solution.py:27
  94.2 5.7 %collective-permute-start.16 = (bf16[366,250]{1,0:T(8,128)(2,1)S(1)}, bf16[366,250]{1,0:T(8,128)(2,1)S(1)}, u32[]{:S(2)}, u32[]{:S(2)}) collective-permute-start(bf16[366,250]{1,0:T(8,128)(2,1)S(1)} %slice.25), channel_id=1, source_target_pairs={{0,7},{1,0},{2,1},{3,2},{4,3},{5,4},{6,5},{7,6},{8,15},{9,8},{10,9... | collective-permute-start | bytes 549008 | tf_op jit(solution)/shard_map/ppermute | solution.py:27
  101.2 1.7 collective-permute-start.17
  103.7 15.3 %all-to-all-start.1 = ((bf16[8,64,256]{2,1,0:T(8,128)(2,1)}), bf16[8,64,256]{2,1,0:T(8,128)(2,1)S(1)}, u32[]{:S(2)}, u32[]{:S(2)}) async-start(bf16[8,64,256]{2,1,0:T(8,128)(2,1)} %add_convert_fusion), calls=%async_computation.1 | async-start | bytes 524288 | tf_op jit(solution)/shard_map/all_to_all | solution.py:48
  119.0 43.9 %copy-start.3 = (bf16[256,1500]{1,0:T(8,128)(2,1)S(1)}, bf16[256,1500]{1,0:T(8,128)(2,1)}, u32[]{:S(2)}) copy-start(bf16[256,1500]{1,0:T(8,128)(2,1)} %copy-done.2) | copy-start | bytes 2304004
  119.0 43.9 %copy-start.5 = (bf16[256,1500]{1,0:T(8,128)(2,1)S(1)}, bf16[256,1500]{1,0:T(8,128)(2,1)}, u32[]{:S(2)}) copy-start(bf16[256,1500]{1,0:T(8,128)(2,1)} %copy-done.4) | copy-start | bytes 2304004
  134.0 4.5 %collective-permute-start.26 = (bf16[8,64,256]{2,1,0:T(8,128)(2,1)S(1)}, bf16[8,64,256]{2,1,0:T(8,128)(2,1)S(1)}, u32[]{:S(2)}, u32[]{:S(2)}) collective-permute-start(bf16[8,64,256]{2,1,0:T(8,128)(2,1)S(1)} %all_to_all.15.response), channel_id=1, source_target_pairs={{0,8},{8,0},{1,9},{9,1},{2,10},{10,2},{3,11},{11,3},{4,12},{12,4},... | collective-permute-start | bytes 786440 | tf_op jit(solution)/shard_map/ppermute | solution.py:216
  135.0 7.8 %collective-permute-start.18 = (bf16[64,768]{1,0:T(8,128)(2,1)S(1)}, bf16[64,768]{1,0:T(8,128)(2,1)S(1)}, u32[]{:S(2)}, u32[]{:S(2)}) collective-permute-start(bf16[64,768]{1,0:T(8,128)(2,1)S(1)} %shard_map.69.refs_0_), channel_id=1, source_target_pairs={{0,1},{1,2},{2,3},{3,4},{4,5},{5,6},{6,7},{7,0},{8,9},{9,10},{10,1... | collective-permute-start | bytes 294920 | tf_op jit(solution)/shard_map/ppermute | solution.py:27
  135.1 7.7 %collective-permute-start.19 = (bf16[64,768]{1,0:T(8,128)(2,1)S(1)}, bf16[64,768]{1,0:T(8,128)(2,1)S(1)}, u32[]{:S(2)}, u32[]{:S(2)}) collective-permute-start(bf16[64,768]{1,0:T(8,128)(2,1)S(1)} %shard_map.69.refs_0_), channel_id=1, source_target_pairs={{0,7},{1,0},{2,1},{3,2},{4,3},{5,4},{6,5},{7,6},{8,15},{9,8},{10,9... | collective-permute-start | bytes 294920 | tf_op jit(solution)/shard_map/ppermute | solution.py:27
  139.5 6.6 %collective-permute-start.27 = (bf16[64,768]{1,0:T(8,128)(2,1)S(1)}, bf16[64,768]{1,0:T(8,128)(2,1)S(1)}, u32[]{:S(2)}, u32[]{:S(2)}) collective-permute-start(bf16[64,768]{1,0:T(8,128)(2,1)S(1)} %shard_map.70.refs_9_), channel_id=1, source_target_pairs={{0,1},{1,2},{2,3},{3,4},{4,5},{5,6},{6,7},{7,0},{8,9},{9,10},{10,1... | collective-permute-start | bytes 294920 | tf_op jit(solution)/shard_map/ppermute | solution.py:27
  139.6 6.5 %collective-permute-start.28 = (bf16[64,768]{1,0:T(8,128)(2,1)S(1)}, bf16[64,768]{1,0:T(8,128)(2,1)S(1)}, u32[]{:S(2)}, u32[]{:S(2)}) collective-permute-start(bf16[64,768]{1,0:T(8,128)(2,1)S(1)} %shard_map.70.refs_9_), channel_id=1, source_target_pairs={{0,7},{1,0},{2,1},{3,2},{4,3},{5,4},{6,5},{7,6},{8,15},{9,8},{10,9... | collective-permute-start | bytes 294920 | tf_op jit(solution)/shard_map/ppermute | solution.py:27
  142.8 6.5 %collective-permute-start.20 = (bf16[64,768]{1,0:T(8,128)(2,1)S(1)}, bf16[64,768]{1,0:T(8,128)(2,1)S(1)}, u32[]{:S(2)}, u32[]{:S(2)}) collective-permute-start(bf16[64,768]{1,0:T(8,128)(2,1)S(1)} %collective-permute-done.18.refs_1_), channel_id=1, source_target_pairs={{0,1},{1,2},{2,3},{3,4},{4,5},{5,6},{6,7},{7,0},{8,9},{9,10},{10,1... | collective-permute-start | bytes 294920 | tf_op jit(solution)/shard_map/ppermute | solution.py:27
  142.8 6.5 %collective-permute-start.21 = (bf16[64,768]{1,0:T(8,128)(2,1)S(1)}, bf16[64,768]{1,0:T(8,128)(2,1)S(1)}, u32[]{:S(2)}, u32[]{:S(2)}) collective-permute-start(bf16[64,768]{1,0:T(8,128)(2,1)S(1)} %collective-permute-done.19.refs_2_), channel_id=1, source_target_pairs={{0,7},{1,0},{2,1},{3,2},{4,3},{5,4},{6,5},{7,6},{8,15},{9,8},{10,9... | collective-permute-start | bytes 294920 | tf_op jit(solution)/shard_map/ppermute | solution.py:27
  146.1 6.5 %collective-permute-start.29 = (bf16[64,768]{1,0:T(8,128)(2,1)S(1)}, bf16[64,768]{1,0:T(8,128)(2,1)S(1)}, u32[]{:S(2)}, u32[]{:S(2)}) collective-permute-start(bf16[64,768]{1,0:T(8,128)(2,1)S(1)} %collective-permute-done.27.refs_10_), channel_id=1, source_target_pairs={{0,1},{1,2},{2,3},{3,4},{4,5},{5,6},{6,7},{7,0},{8,9},{9,10},{10,1... | collective-permute-start | bytes 294920 | tf_op jit(solution)/shard_map/ppermute | solution.py:27
  146.1 6.5 %collective-permute-start.30 = (bf16[64,768]{1,0:T(8,128)(2,1)S(1)}, bf16[64,768]{1,0:T(8,128)(2,1)S(1)}, u32[]{:S(2)}, u32[]{:S(2)}) collective-permute-start(bf16[64,768]{1,0:T(8,128)(2,1)S(1)} %collective-permute-done.28.refs_11_), channel_id=1, source_target_pairs={{0,7},{1,0},{2,1},{3,2},{4,3},{5,4},{6,5},{7,6},{8,15},{9,8},{10,9... | collective-permute-start | bytes 294920 | tf_op jit(solution)/shard_map/ppermute | solution.py:27
  149.3 6.6 %collective-permute-start.22 = (bf16[64,768]{1,0:T(8,128)(2,1)S(1)}, bf16[64,768]{1,0:T(8,128)(2,1)S(1)}, u32[]{:S(2)}, u32[]{:S(2)}) collective-permute-start(bf16[64,768]{1,0:T(8,128)(2,1)S(1)} %collective-permute-done.20.refs_3_), channel_id=1, source_target_pairs={{0,1},{1,2},{2,3},{3,4},{4,5},{5,6},{6,7},{7,0},{8,9},{9,10},{10,1... | collective-permute-start | bytes 294920 | tf_op jit(solution)/shard_map/ppermute | solution.py:27
  149.3 6.6 %collective-permute-start.23 = (bf16[64,768]{1,0:T(8,128)(2,1)S(1)}, bf16[64,768]{1,0:T(8,128)(2,1)S(1)}, u32[]{:S(2)}, u32[]{:S(2)}) collective-permute-start(bf16[64,768]{1,0:T(8,128)(2,1)S(1)} %collective-permute-done.21.refs_4_), channel_id=1, source_target_pairs={{0,7},{1,0},{2,1},{3,2},{4,3},{5,4},{6,5},{7,6},{8,15},{9,8},{10,9... | collective-permute-start | bytes 294920 | tf_op jit(solution)/shard_map/ppermute | solution.py:27
  152.5 6.9 %collective-permute-start.31 = (bf16[64,768]{1,0:T(8,128)(2,1)S(1)}, bf16[64,768]{1,0:T(8,128)(2,1)S(1)}, u32[]{:S(2)}, u32[]{:S(2)}) collective-permute-start(bf16[64,768]{1,0:T(8,128)(2,1)S(1)} %collective-permute-done.29.refs_12_), channel_id=1, source_target_pairs={{0,1},{1,2},{2,3},{3,4},{4,5},{5,6},{6,7},{7,0},{8,9},{9,10},{10,1... | collective-permute-start | bytes 294920 | tf_op jit(solution)/shard_map/ppermute | solution.py:27
  152.6 7.0 %collective-permute-start.32 = (bf16[64,768]{1,0:T(8,128)(2,1)S(1)}, bf16[64,768]{1,0:T(8,128)(2,1)S(1)}, u32[]{:S(2)}, u32[]{:S(2)}) collective-permute-start(bf16[64,768]{1,0:T(8,128)(2,1)S(1)} %collective-permute-done.30.refs_13_), channel_id=1, source_target_pairs={{0,7},{1,0},{2,1},{3,2},{4,3},{5,4},{6,5},{7,6},{8,15},{9,8},{10,9... | collective-permute-start | bytes 294920 | tf_op jit(solution)/shard_map/ppermute | solution.py:27
  155.9 7.6 %collective-permute-start.24 = (bf16[32,768]{1,0:T(8,128)(2,1)S(1)}, bf16[32,768]{1,0:T(8,128)(2,1)S(1)}, u32[]{:S(2)}, u32[]{:S(2)}) collective-permute-start(bf16[32,768]{1,0:T(8,128)(2,1)S(1)} %slice.26), channel_id=1, source_target_pairs={{0,1},{1,2},{2,3},{3,4},{4,5},{5,6},{6,7},{7,0},{8,9},{9,10},{10,1... | collective-permute-start | bytes 147464 | tf_op jit(solution)/shard_map/ppermute | solution.py:27
  156.0 7.6 %collective-permute-start.25 = (bf16[32,768]{1,0:T(8,128)(2,1)S(1)}, bf16[32,768]{1,0:T(8,128)(2,1)S(1)}, u32[]{:S(2)}, u32[]{:S(2)}) collective-permute-start(bf16[32,768]{1,0:T(8,128)(2,1)S(1)} %slice.27), channel_id=1, source_target_pairs={{0,7},{1,0},{2,1},{3,2},{4,3},{5,4},{6,5},{7,6},{8,15},{9,8},{10,9... | collective-permute-start | bytes 147464 | tf_op jit(solution)/shard_map/ppermute | solution.py:27
  159.4 5.4 %collective-permute-start.33 = (bf16[32,768]{1,0:T(8,128)(2,1)S(1)}, bf16[32,768]{1,0:T(8,128)(2,1)S(1)}, u32[]{:S(2)}, u32[]{:S(2)}) collective-permute-start(bf16[32,768]{1,0:T(8,128)(2,1)S(1)} %slice.28), channel_id=1, source_target_pairs={{0,1},{1,2},{2,3},{3,4},{4,5},{5,6},{6,7},{7,0},{8,9},{9,10},{10,1... | collective-permute-start | bytes 147464 | tf_op jit(solution)/shard_map/ppermute | solution.py:27
  159.6 5.3 %collective-permute-start.34 = (bf16[32,768]{1,0:T(8,128)(2,1)S(1)}, bf16[32,768]{1,0:T(8,128)(2,1)S(1)}, u32[]{:S(2)}, u32[]{:S(2)}) collective-permute-start(bf16[32,768]{1,0:T(8,128)(2,1)S(1)} %slice.29), channel_id=1, source_target_pairs={{0,7},{1,0},{2,1},{3,2},{4,3},{5,4},{6,5},{7,6},{8,15},{9,8},{10,9... | collective-permute-start | bytes 147464 | tf_op jit(solution)/shard_map/ppermute | solution.py:27

commit v5 on v2

--- a/solution.py
+++ b/solution.py
@@ -29,12 +29,16 @@
     return lax.ppermute(shard, axis, [(i, (i + step) % size) for i in range(size)])
 
 
-def ring_gather(shard, axis, mid):
+def ring_gather(shard, axis, mid, straight=False):
     half = lax.axis_size(axis) // 2
     pieces, down, up = [shard], shard, shard
+    if straight:
+        far = [turn(shard[:mid], axis, half), turn(shard[mid:], axis, -half)]
     for _ in range(half - 1):
         down, up = turn(down, axis, 1), turn(up, axis, -1)
         pieces += [down, up]
+    if straight:
+        return pieces + far
     far = [turn(down[:mid], axis, 1), turn(up[mid:], axis, -1)]
     return pieces + far
 
@@ -228,7 +232,7 @@
         compiler_params=ROOMY,
     )(at, response, sibling, *occ[:-2], far)
 
-    pieces = ring_gather(mixed, "y", block)
+    pieces = ring_gather(mixed, "y", block, straight=True)
     tile = 2 * LANES
     total = pl.pallas_call(
         density_kernel,

time: 174 us -> 177 us (1.017)
  starting transfers between devices: 69.5 us -> 71.9 us
    ppermute x24, starting transfers between devices: 40.8 us -> 43.2 us  [turn(): lax.ppermute(shard, axis, [(i, (i + step) % size) for i in range(size)])]
  transfers between devices with their start and end apart: 29 -> 29, of which waited for: 15 -> 13; matrix products, arithmetic and copies ran while one was open for 2% -> 2% of each run, Pallas kernels for 2% -> 3%
where the time goes in v5:
time: 177 us; the launch traced here: 174 us
  starting transfers between devices  71.9 us (41%)
  waiting for transfers between devices  66 us (37%)
  blocking collectives  14.9 us (8%)
  Pallas kernels  13.2 us (7%)
  local copies, waits for them, and re-layouts  5.82 us (3%)
    ppermute x24, starting transfers between devices, turn(): lax.ppermute(shard, axis, [(i, (i + step) % size) for i in range(size)])  43.2 us
    ppermute x24, waiting for transfers between devices, turn(): lax.ppermute(shard, axis, [(i, (i + step) % size) for i in range(size)])  42.2 us
    all_to_all x2, starting transfers between devices, exchanged(): return lax.all_to_all(pieces, axis, split_axis=0, concat_axis=0, tiled=True)  28.5 us
    all_to_all x2, waiting for transfers between devices, exchanged(): return lax.all_to_all(pieces, axis, split_axis=0, concat_axis=0, tiled=True)  20.7 us
    all_to_all x1, blocking collectives, exchanged(): return lax.all_to_all(pieces, axis, split_axis=0, concat_axis=0, tiled=True)  14.9 us
    pallas_call x1, Pallas kernels, per_device(): pl.pallas_call(density_kernel, grid=(pl.cdiv(rows, tile),), in_specs=[SCA...  5.36 us
  transfers between devices with their start and end apart: 29, of which 13 were waited for; matrix products, arithmetic and copies ran while one was open for 2% of the time, Pallas kernels for 3%

profile of v5, /device:TPU:516, one launch (start us, length us, event | category | flops | bytes accessed | tf_op | source)
XLA Modules:
  0.0 173.9 jit_solution(18366489282742702984)
XLA Ops:
  0.0 1.8 %broadcast_in_dim.6 = bf16[8,32,1500]{2,1,0:T(8,128)(2,1)} broadcast(bf16[32,1500]{1,0:T(8,128)(2,1)} %bitcast.7), dimensions={1,2} | broadcast | bytes 864000 | tf_op jit(solution)/shard_map/broadcast_in_dim | solution.py:173
  1.9 22.7 %all-to-all-start = ((bf16[8,32,1500]{2,1,0:T(8,128)(2,1)}), bf16[8,32,1500]{2,1,0:T(8,128)(2,1)S(1)}, u32[]{:S(2)}, u32[]{:S(2)}) async-start(bf16[8,32,1500]{2,1,0:T(8,128)(2,1)} %broadcast_in_dim.6), calls=%async_computation | async-start | bytes 1572864 | tf_op jit(solution)/shard_map/all_to_all | solution.py:54
  24.6 0.0 collective-permute-start.9
  24.6 12.8 %all-to-all-done.held = bf16[8,32,1500]{2,1,0:T(8,128)(2,1)S(1)} async-done(((bf16[8,32,1500]{2,1,0:T(8,128)(2,1)}), bf16[8,32,1500]{2,1,0:T(8,128)(2,1)S(1)}, u32[]{:S(2)}, u32[]{:S(2)}) %all-to-all-start) | async-done | bytes 768032 | tf_op jit(solution)/shard_map/all_to_all | solution.py:54
  37.4 0.0 collective-permute-start
  37.4 4.6 %collective-permute-start.10 = (bf16[750,250]{1,0:T(8,128)(2,1)}, bf16[750,250]{1,0:T(8,128)(2,1)S(1)}, u32[]{:S(2)}, u32[]{:S(2)}) collective-permute-start(bf16[750,250]{1,0:T(8,128)(2,1)} %refs_0_.3), channel_id=1, source_target_pairs={{0,7},{1,0},{2,1},{3,2},{4,3},{5,4},{6,5},{7,6},{8,15},{9,8},{10,9... | collective-permute-start | bytes 1125008 | tf_op jit(solution)/shard_map/ppermute | solution.py:29
  42.0 0.0 collective-permute-done.9.refs_1_
  42.0 0.0 collective-permute-start.11
  42.0 9.2 %collective-permute-done.10.refs_2_ = bf16[750,250]{1,0:T(8,128)(2,1)S(1)} collective-permute-done((bf16[750,250]{1,0:T(8,128)(2,1)}, bf16[750,250]{1,0:T(8,128)(2,1)S(1)}, u32[]{:S(2)}, u32[]{:S(2)}) %collective-permute-start.10) | collective-permute-done | bytes 375032 | tf_op jit(solution)/shard_map/ppermute | solution.py:29
  51.2 3.6 %collective-permute-start.12 = (bf16[750,250]{1,0:T(8,128)(2,1)S(1)}, bf16[750,250]{1,0:T(8,128)(2,1)S(1)}, u32[]{:S(2)}, u32[]{:S(2)}) collective-permute-start(bf16[750,250]{1,0:T(8,128)(2,1)S(1)} %collective-permute-done.10.refs_2_), channel_id=1, source_target_pairs={{0,7},{1,0},{2,1},{3,2},{4,3},{5,4},{6,5},{7,6},{8,15},{9,8},{10,9... | collective-permute-start | bytes 1125008 | tf_op jit(solution)/shard_map/ppermute | solution.py:29
  54.7 3.0 %copy.7.pert = bf16[2,750,1500]{2,1,0:T(8,128)(2,1)S(1)} copy(bf16[2,750,1500]{2,0,1:T(2,128)(2,1)} %param.6) | data formatting | bytes 9000000 | tf_op args[0]
  57.8 0.1 pad_add_fusion.at
  57.9 2.0 %shard_map.64 = (bf16[256,1500]{1,0:T(8,128)(2,1)S(1)}, bf16[2,256,750]{2,1,0:T(8,128)(2,1)S(1)}) custom-call(s32[2]{0:T(128)S(1)} %pad_add_fusion.at, bf16[8,32,1500]{2,1,0:T(8,128)(2,1)S(1)} %all-to-all-done.held, bf16[2,750,1500]{2,1,0:T(8,128)(2,1)S(1)} %copy.7.pert), custom_call_target="tpu_custom_call" | custom-call | tf_op jit(solution)/shard_map/pallas_call | solution.py:180
  59.8 0.0 copy-start.2
  59.9 0.0 collective-permute-done.held
  59.9 0.0 copy-start.1
  59.9 2.9 %shard_map.65 = (bf16[256,1500]{1,0:T(8,128)(2,1)S(1)}, bf16[64,750]{1,0:T(8,128)(2,1)S(1)}, bf16[64,750]{1,0:T(8,128)(2,1)S(1)}, bf16[128,750]{1,0:T(8,128)(2,1...) custom-call(s32[2]{0:T(128)S(1)} %pad_add_fusion.at, ...), custom_call_target="tpu_custom_call" | custom-call | tf_op jit(solution)/shard_map/pallas_call | solution.py:187
  62.8 0.0 copy-start.7
  62.9 0.1 collective-permute-start.1
  63.0 0.0 collective-permute-done.12.refs_4_
  63.0 3.4 %collective-permute-start.14 = (bf16[750,250]{1,0:T(8,128)(2,1)S(1)}, bf16[750,250]{1,0:T(8,128)(2,1)S(1)}, u32[]{:S(2)}, u32[]{:S(2)}) collective-permute-start(bf16[750,250]{1,0:T(8,128)(2,1)S(1)} %collective-permute-done.12.refs_4_), channel_id=1, source_target_pairs={{0,7},{1,0},{2,1},{3,2},{4,3},{5,4},{6,5},{7,6},{8,15},{9,8},{10,9... | collective-permute-start | bytes 1125008 | tf_op jit(solution)/shard_map/ppermute | solution.py:29
  66.4 0.0 collective-permute-done.13.refs_5_
  66.5 0.0 copy-start.6
  66.5 0.1 collective-permute-start.15
  66.6 3.2 %collective-permute-start.5 = (bf16[64,750]{1,0:T(8,128)(2,1)S(1)}, bf16[64,750]{1,0:T(8,128)(2,1)S(1)}, u32[]{:S(2)}, u32[]{:S(2)}) collective-permute-start(bf16[64,750]{1,0:T(8,128)(2,1)S(1)} %get-tuple-element.31), channel_id=1, source_target_pairs={{0,7},{1,0},{2,1},{3,2},{4,3},{5,4},{6,5},{7,6},{8,15},{9,8},{10,9... | collective-permute-start | bytes 288008 | tf_op jit(solution)/shard_map/ppermute | solution.py:29
  69.9 0.1 collective-permute-start.2
  70.0 5.9 %collective-permute-done.5 = bf16[64,750]{1,0:T(8,128)(2,1)S(1)} collective-permute-done((bf16[64,750]{1,0:T(8,128)(2,1)S(1)}, bf16[64,750]{1,0:T(8,128)(2,1)S(1)}, u32[]{:S(2)}, u32[]{:S(2)}) %collective-permute-start.5) | collective-permute-done | bytes 96032 | tf_op jit(solution)/shard_map/ppermute | solution.py:29
  75.9 4.0 %collective-permute-start.6 = (bf16[128,750]{1,0:T(8,128)(2,1)S(1)}, bf16[128,750]{1,0:T(8,128)(2,1)S(1)}, u32[]{:S(2)}, u32[]{:S(2)}) collective-permute-start(bf16[128,750]{1,0:T(8,128)(2,1)S(1)} %add_convert_fusion.3), channel_id=1, source_target_pairs={{0,7},{1,0},{2,1},{3,2},{4,3},{5,4},{6,5},{7,6},{8,15},{9,8},{10,9... | collective-permute-start | bytes 576008 | tf_op jit(solution)/shard_map/ppermute | solution.py:29
  79.9 0.0 collective-permute-done.2
  80.0 0.1 collective-permute-start.3
  80.1 3.0 %collective-permute-done.6 = bf16[128,750]{1,0:T(8,128)(2,1)S(1)} collective-permute-done((bf16[128,750]{1,0:T(8,128)(2,1)S(1)}, bf16[128,750]{1,0:T(8,128)(2,1)S(1)}, u32[]{:S(2)}, u32[]{:S(2)}) %collective-permute-start.6) | collective-permute-done | bytes 192032 | tf_op jit(solution)/shard_map/ppermute | solution.py:29
  83.2 3.8 %collective-permute-start.7 = (bf16[128,750]{1,0:T(8,128)(2,1)S(1)}, bf16[128,750]{1,0:T(8,128)(2,1)S(1)}, u32[]{:S(2)}, u32[]{:S(2)}) collective-permute-start(bf16[128,750]{1,0:T(8,128)(2,1)S(1)} %add_convert_fusion.2), channel_id=1, source_target_pairs={{0,7},{1,0},{2,1},{3,2},{4,3},{5,4},{6,5},{7,6},{8,15},{9,8},{10,9... | collective-permute-start | bytes 576008 | tf_op jit(solution)/shard_map/ppermute | solution.py:29
  87.0 0.0 collective-permute-done.3
  87.0 0.1 collective-permute-start.4
  87.2 3.2 %collective-permute-done.7 = bf16[128,750]{1,0:T(8,128)(2,1)S(1)} collective-permute-done((bf16[128,750]{1,0:T(8,128)(2,1)S(1)}, bf16[128,750]{1,0:T(8,128)(2,1)S(1)}, u32[]{:S(2)}, u32[]{:S(2)}) %collective-permute-start.7) | collective-permute-done | bytes 192032 | tf_op jit(solution)/shard_map/ppermute | solution.py:29
  90.4 3.8 %collective-permute-start.8 = (bf16[128,750]{1,0:T(8,128)(2,1)S(1)}, bf16[128,750]{1,0:T(8,128)(2,1)S(1)}, u32[]{:S(2)}, u32[]{:S(2)}) collective-permute-start(bf16[128,750]{1,0:T(8,128)(2,1)S(1)} %add_convert_fusion.1), channel_id=1, source_target_pairs={{0,7},{1,0},{2,1},{3,2},{4,3},{5,4},{6,5},{7,6},{8,15},{9,8},{10,9... | collective-permute-start | bytes 576008 | tf_op jit(solution)/shard_map/ppermute | solution.py:29
  94.2 0.2 collective-permute-start.16
  94.4 5.5 %collective-permute-done.16.refs_8_ = bf16[366,250]{1,0:T(8,128)(2,1)S(1)} collective-permute-done((bf16[366,250]{1,0:T(8,128)(2,1)S(1)}, bf16[366,250]{1,0:T(8,128)(2,1)S(1)}, u32[]{:S(2)}, u32[]{:S(2)}) %collective-permute-start.16) | collective-permute-done | bytes 183032 | tf_op jit(solution)/shard_map/ppermute | solution.py:29
  99.9 0.0 collective-permute-done.4.down
  100.0 1.2 shard_map.66
  101.2 0.1 collective-permute-start.17
  101.4 1.5 collective-permute-done.17
  102.9 0.8 add_convert_fusion
  103.6 5.8 %all-to-all-start.1 = ((bf16[8,64,256]{2,1,0:T(8,128)(2,1)}), bf16[8,64,256]{2,1,0:T(8,128)(2,1)S(1)}, u32[]{:S(2)}, u32[]{:S(2)}) async-start(bf16[8,64,256]{2,1,0:T(8,128)(2,1)} %add_convert_fusion), calls=%async_computation.1 | async-start | bytes 524288 | tf_op jit(solution)/shard_map/all_to_all | solution.py:54
  109.5 0.6 dynamic_slice.9
  110.7 0.1 reshape.3
  110.8 0.1 dynamic-slice_bitcast_fusion
  110.9 0.1 copy.9.virtual
  111.0 7.9 %all-to-all-done.1.terms = bf16[8,64,256]{2,1,0:T(8,128)(2,1)S(1)} async-done(((bf16[8,64,256]{2,1,0:T(8,128)(2,1)}), bf16[8,64,256]{2,1,0:T(8,128)(2,1)S(1)}, u32[]{:S(2)}, u32[]{:S(2)}) %all-to-all-start.1) | async-done | bytes 262176 | tf_op jit(solution)/shard_map/all_to_all | solution.py:54
  118.9 0.1 shard_map.67
  119.0 14.9 %all_to_all.15.own = bf16[8,64,256]{2,1,0:T(8,128)(2,1)S(1)} all-to-all(bf16[8,64,256]{2,1,0:T(8,128)(2,1)S(1)} %shard_map.67), channel_id=1, replica_groups=mesh['grp'=2,'x'=8,'k'=2,'y'=8] {'x'}, dimensions={0} | all-to-all | bytes 524288 | tf_op jit(solution)/shard_map/all_to_all | solution.py:54
  134.0 1.5 collective-permute-done.18.other
  135.5 1.6 shard_map.68.refs_0_
  137.1 0.1 collective-permute-start.19
  137.2 3.3 %collective-permute-start.20 = (bf16[128,750]{1,0:T(8,128)(2,1)S(1)}, bf16[128,750]{1,0:T(8,128)(2,1)S(1)}, u32[]{:S(2)}, u32[]{:S(2)}) collective-permute-start(bf16[128,750]{1,0:T(8,128)(2,1)S(1)} %shard_map.68.refs_0_), channel_id=1, source_target_pairs={{0,7},{1,0},{2,1},{3,2},{4,3},{5,4},{6,5},{7,6},{8,15},{9,8},{10,9... | collective-permute-start | bytes 576008 | tf_op jit(solution)/shard_map/ppermute | solution.py:29
  140.5 5.1 %collective-permute-done.19.refs_1_ = bf16[128,750]{1,0:T(8,128)(2,1)S(1)} collective-permute-done((bf16[128,750]{1,0:T(8,128)(2,1)S(1)}, bf16[128,750]{1,0:T(8,128)(2,1)S(1)}, u32[]{:S(2)}, u32[]{:S(2)}) %collective-permute-start.19) | collective-permute-done | bytes 192032 | tf_op jit(solution)/shard_map/ppermute | solution.py:29
  145.6 3.2 %collective-permute-start.22 = (bf16[128,750]{1,0:T(8,128)(2,1)S(1)}, bf16[128,750]{1,0:T(8,128)(2,1)S(1)}, u32[]{:S(2)}, u32[]{:S(2)}) collective-permute-start(bf16[128,750]{1,0:T(8,128)(2,1)S(1)} %collective-permute-done.20.refs_2_), channel_id=1, source_target_pairs={{0,7},{1,0},{2,1},{3,2},{4,3},{5,4},{6,5},{7,6},{8,15},{9,8},{10,9... | collective-permute-start | bytes 576008 | tf_op jit(solution)/shard_map/ppermute | solution.py:29
  148.9 4.3 %collective-permute-done.21.refs_3_ = bf16[128,750]{1,0:T(8,128)(2,1)S(1)} collective-permute-done((bf16[128,750]{1,0:T(8,128)(2,1)S(1)}, bf16[128,750]{1,0:T(8,128)(2,1)S(1)}, u32[]{:S(2)}, u32[]{:S(2)}) %collective-permute-start.21) | collective-permute-done | bytes 192032 | tf_op jit(solution)/shard_map/ppermute | solution.py:29
  153.2 3.2 %collective-permute-start.24 = (bf16[128,750]{1,0:T(8,128)(2,1)S(1)}, bf16[128,750]{1,0:T(8,128)(2,1)S(1)}, u32[]{:S(2)}, u32[]{:S(2)}) collective-permute-start(bf16[128,750]{1,0:T(8,128)(2,1)S(1)} %collective-permute-done.22.refs_4_), channel_id=1, source_target_pairs={{0,7},{1,0},{2,1},{3,2},{4,3},{5,4},{6,5},{7,6},{8,15},{9,8},{10,9... | collective-permute-start | bytes 576008 | tf_op jit(solution)/shard_map/ppermute | solution.py:29
  156.4 0.1 collective-permute-start.25
  156.6 5.9 %collective-permute-start.26 = (bf16[64,750]{1,0:T(8,128)(2,1)S(1)}, bf16[64,750]{1,0:T(8,128)(2,1)S(1)}, u32[]{:S(2)}, u32[]{:S(2)}) collective-permute-start(bf16[64,750]{1,0:T(8,128)(2,1)S(1)} %get-tuple-element.35), channel_id=1, source_target_pairs={{0,4},{1,5},{2,6},{3,7},{4,0},{5,1},{6,2},{7,3},{8,12},{9,13},{10,... | collective-permute-start | bytes 288008 | tf_op jit(solution)/shard_map/ppermute | solution.py:29
  162.5 5.0 %collective-permute-done.25.refs_7_ = bf16[64,750]{1,0:T(8,128)(2,1)S(1)} collective-permute-done((bf16[64,750]{1,0:T(8,128)(2,1)S(1)}, bf16[64,750]{1,0:T(8,128)(2,1)S(1)}, u32[]{:S(2)}, u32[]{:S(2)}) %collective-permute-start.25) | collective-permute-done | bytes 96032 | tf_op jit(solution)/shard_map/ppermute | solution.py:29
  167.5 1.1 collective-permute-done.26.refs_8_
  168.5 5.4 %shard_map.69 = bf16[750,2,1500]{2,1,0:T(2,128)(2,1)} custom-call(s32[2]{0:T(128)S(1)} %pad_add_fusion.at, bf16[256,1500]{1,0:T(8,128)(2,1)S(1)} %copy-done.3, bf16[256,1500]{1,0:T(8,128)(2,1)S(1)} %copy-done.5, bf16[128,750]{1,0:T(8,128)(2,1)S(1)} %shard_map.68.refs_0_, bf16[128,750]{1,0:T(8,128)(2,1)S(1)} %collective-permute-done.19.refs_1_, ...), custom_call_target="tpu_custom_call" | custom-call | tf_op jit(solution)/shard_map/pallas_call | solution.py:237
  (35 shorter events, 0.4 us)
Async XLA Ops:
  0.0 110.8 %copy-start = (f32[512]{0:T(512)S(1)}, f32[512]{0:T(512)}, u32[]{:S(2)}) copy-start(f32[512]{0:T(512)} %param.10) | copy-start | bytes 6148
  1.9 35.5 %all-to-all-start = ((bf16[8,32,1500]{2,1,0:T(8,128)(2,1)}), bf16[8,32,1500]{2,1,0:T(8,128)(2,1)S(1)}, u32[]{:S(2)}, u32[]{:S(2)}) async-start(bf16[8,32,1500]{2,1,0:T(8,128)(2,1)} %broadcast_in_dim.6), calls=%async_computation | async-start | bytes 1572864 | tf_op jit(solution)/shard_map/all_to_all | solution.py:54
  24.6 17.4 %collective-permute-start.9 = (bf16[750,250]{1,0:T(8,128)(2,1)}, bf16[750,250]{1,0:T(8,128)(2,1)S(1)}, u32[]{:S(2)}, u32[]{:S(2)}) collective-permute-start(bf16[750,250]{1,0:T(8,128)(2,1)} %refs_0_.3), channel_id=1, source_target_pairs={{0,1},{1,2},{2,3},{3,4},{4,5},{5,6},{6,7},{7,0},{8,9},{9,10},{10,1... | collective-permute-start | bytes 1125008 | tf_op jit(solution)/shard_map/ppermute | solution.py:29
  37.4 22.5 %collective-permute-start = (bf16[8,32,1500]{2,1,0:T(8,128)(2,1)S(1)}, bf16[8,32,1500]{2,1,0:T(8,128)(2,1)}, u32[]{:S(2)}, u32[]{:S(2)}) collective-permute-start(bf16[8,32,1500]{2,1,0:T(8,128)(2,1)S(1)} %all-to-all-done.held), channel_id=1, source_target_pairs={{0,8},{8,0},{1,9},{9,1},{2,10},{10,2},{3,11},{11,3},{4,12},{12,4},... | collective-permute-start | bytes 2304008 | tf_op jit(solution)/shard_map/ppermute | solution.py:174
  37.4 13.8 %collective-permute-start.10 = (bf16[750,250]{1,0:T(8,128)(2,1)}, bf16[750,250]{1,0:T(8,128)(2,1)S(1)}, u32[]{:S(2)}, u32[]{:S(2)}) collective-permute-start(bf16[750,250]{1,0:T(8,128)(2,1)} %refs_0_.3), channel_id=1, source_target_pairs={{0,7},{1,0},{2,1},{3,2},{4,3},{5,4},{6,5},{7,6},{8,15},{9,8},{10,9... | collective-permute-start | bytes 1125008 | tf_op jit(solution)/shard_map/ppermute | solution.py:29
  42.0 12.8 %collective-permute-start.11 = (bf16[750,250]{1,0:T(8,128)(2,1)S(1)}, bf16[750,250]{1,0:T(8,128)(2,1)S(1)}, u32[]{:S(2)}, u32[]{:S(2)}) collective-permute-start(bf16[750,250]{1,0:T(8,128)(2,1)S(1)} %collective-permute-done.9.refs_1_), channel_id=1, source_target_pairs={{0,1},{1,2},{2,3},{3,4},{4,5},{5,6},{6,7},{7,0},{8,9},{9,10},{10,1... | collective-permute-start | bytes 1125008 | tf_op jit(solution)/shard_map/ppermute | solution.py:29
  51.2 11.8 %collective-permute-start.12 = (bf16[750,250]{1,0:T(8,128)(2,1)S(1)}, bf16[750,250]{1,0:T(8,128)(2,1)S(1)}, u32[]{:S(2)}, u32[]{:S(2)}) collective-permute-start(bf16[750,250]{1,0:T(8,128)(2,1)S(1)} %collective-permute-done.10.refs_2_), channel_id=1, source_target_pairs={{0,7},{1,0},{2,1},{3,2},{4,3},{5,4},{6,5},{7,6},{8,15},{9,8},{10,9... | collective-permute-start | bytes 1125008 | tf_op jit(solution)/shard_map/ppermute | solution.py:29
  54.7 11.7 %collective-permute-start.13 = (bf16[750,250]{1,0:T(8,128)(2,1)S(1)}, bf16[750,250]{1,0:T(8,128)(2,1)S(1)}, u32[]{:S(2)}, u32[]{:S(2)}) collective-permute-start(bf16[750,250]{1,0:T(8,128)(2,1)S(1)} %collective-permute-done.11.refs_3_), channel_id=1, source_target_pairs={{0,1},{1,2},{2,3},{3,4},{4,5},{5,6},{6,7},{7,0},{8,9},{9,10},{10,1... | collective-permute-start | bytes 1125008 | tf_op jit(solution)/shard_map/ppermute | solution.py:29
  59.8 27.2 %copy-start.2 = (bf16[256,1500]{1,0:T(8,128)(2,1)}, bf16[256,1500]{1,0:T(8,128)(2,1)S(1)}, u32[]{:S(2)}) copy-start(bf16[256,1500]{1,0:T(8,128)(2,1)S(1)} %get-tuple-element.20.turned) | copy-start | bytes 2304004
  59.9 40.1 %copy-start.1 = (bf16[750,250]{1,0:T(8,128)(2,1)S(1)}, bf16[750,250]{1,0:T(8,128)(2,1)}, u32[]{:S(2)}) copy-start(bf16[750,250]{1,0:T(8,128)(2,1)} %refs_0_.3) | copy-start | bytes 1125004
  62.8 31.4 %copy-start.4 = (bf16[256,1500]{1,0:T(8,128)(2,1)}, bf16[256,1500]{1,0:T(8,128)(2,1)S(1)}, u32[]{:S(2)}) copy-start(bf16[256,1500]{1,0:T(8,128)(2,1)S(1)} %get-tuple-element.22.other_turned) | copy-start | bytes 2304004
  62.8 46.6 %copy-start.7 = (s32[8]{0:T(128)S(1)}, s32[8]{0:T(128)}, u32[]{:S(2)}) copy-start(s32[8]{0:T(128)} %constant.37.clone) | copy-start | bytes 100
  62.9 7.0 %collective-permute-start.1 = (bf16[64,750]{1,0:T(8,128)(2,1)S(1)}, bf16[64,750]{1,0:T(8,128)(2,1)S(1)}, u32[]{:S(2)}, u32[]{:S(2)}) collective-permute-start(bf16[64,750]{1,0:T(8,128)(2,1)S(1)} %get-tuple-element.27), channel_id=1, source_target_pairs={{0,1},{1,2},{2,3},{3,4},{4,5},{5,6},{6,7},{7,0},{8,9},{9,10},{10,1... | collective-permute-start | bytes 288008 | tf_op jit(solution)/shard_map/ppermute | solution.py:29
  63.0 31.2 %collective-permute-start.14 = (bf16[750,250]{1,0:T(8,128)(2,1)S(1)}, bf16[750,250]{1,0:T(8,128)(2,1)S(1)}, u32[]{:S(2)}, u32[]{:S(2)}) collective-permute-start(bf16[750,250]{1,0:T(8,128)(2,1)S(1)} %collective-permute-done.12.refs_4_), channel_id=1, source_target_pairs={{0,7},{1,0},{2,1},{3,2},{4,3},{5,4},{6,5},{7,6},{8,15},{9,8},{10,9... | collective-permute-start | bytes 1125008 | tf_op jit(solution)/shard_map/ppermute | solution.py:29
  66.5 44.3 %copy-start.6 = (f32[2000]{0:T(1024)S(1)}, f32[2000]{0:T(1024)}, u32[]{:S(2)}) copy-start(f32[2000]{0:T(1024)} %param.9) | copy-start | bytes 24004
  66.5 33.5 %collective-permute-start.15 = (bf16[384,250]{1,0:T(8,128)(2,1)S(1)}, bf16[384,250]{1,0:T(8,128)(2,1)S(1)}, u32[]{:S(2)}, u32[]{:S(2)}) collective-permute-start(bf16[384,250]{1,0:T(8,128)(2,1)S(1)} %slice.16), channel_id=1, source_target_pairs={{0,1},{1,2},{2,3},{3,4},{4,5},{5,6},{6,7},{7,0},{8,9},{9,10},{10,1... | collective-permute-start | bytes 576008 | tf_op jit(solution)/shard_map/ppermute | solution.py:29
  66.6 9.3 %collective-permute-start.5 = (bf16[64,750]{1,0:T(8,128)(2,1)S(1)}, bf16[64,750]{1,0:T(8,128)(2,1)S(1)}, u32[]{:S(2)}, u32[]{:S(2)}) collective-permute-start(bf16[64,750]{1,0:T(8,128)(2,1)S(1)} %get-tuple-element.31), channel_id=1, source_target_pairs={{0,7},{1,0},{2,1},{3,2},{4,3},{5,4},{6,5},{7,6},{8,15},{9,8},{10,9... | collective-permute-start | bytes 288008 | tf_op jit(solution)/shard_map/ppermute | solution.py:29
  69.9 10.1 %collective-permute-start.2 = (bf16[128,750]{1,0:T(8,128)(2,1)S(1)}, bf16[128,750]{1,0:T(8,128)(2,1)S(1)}, u32[]{:S(2)}, u32[]{:S(2)}) collective-permute-start(bf16[128,750]{1,0:T(8,128)(2,1)S(1)} %add_convert_fusion.6), channel_id=1, source_target_pairs={{0,1},{1,2},{2,3},{3,4},{4,5},{5,6},{6,7},{7,0},{8,9},{9,10},{10,1... | collective-permute-start | bytes 576008 | tf_op jit(solution)/shard_map/ppermute | solution.py:29
  75.9 7.2 %collective-permute-start.6 = (bf16[128,750]{1,0:T(8,128)(2,1)S(1)}, bf16[128,750]{1,0:T(8,128)(2,1)S(1)}, u32[]{:S(2)}, u32[]{:S(2)}) collective-permute-start(bf16[128,750]{1,0:T(8,128)(2,1)S(1)} %add_convert_fusion.3), channel_id=1, source_target_pairs={{0,7},{1,0},{2,1},{3,2},{4,3},{5,4},{6,5},{7,6},{8,15},{9,8},{10,9... | collective-permute-start | bytes 576008 | tf_op jit(solution)/shard_map/ppermute | solution.py:29
  80.0 7.0 %collective-permute-start.3 = (bf16[128,750]{1,0:T(8,128)(2,1)S(1)}, bf16[128,750]{1,0:T(8,128)(2,1)S(1)}, u32[]{:S(2)}, u32[]{:S(2)}) collective-permute-start(bf16[128,750]{1,0:T(8,128)(2,1)S(1)} %add_convert_fusion.5), channel_id=1, source_target_pairs={{0,1},{1,2},{2,3},{3,4},{4,5},{5,6},{6,7},{7,0},{8,9},{9,10},{10,1... | collective-permute-start | bytes 576008 | tf_op jit(solution)/shard_map/ppermute | solution.py:29
  83.2 7.2 %collective-permute-start.7 = (bf16[128,750]{1,0:T(8,128)(2,1)S(1)}, bf16[128,750]{1,0:T(8,128)(2,1)S(1)}, u32[]{:S(2)}, u32[]{:S(2)}) collective-permute-start(bf16[128,750]{1,0:T(8,128)(2,1)S(1)} %add_convert_fusion.2), channel_id=1, source_target_pairs={{0,7},{1,0},{2,1},{3,2},{4,3},{5,4},{6,5},{7,6},{8,15},{9,8},{10,9... | collective-permute-start | bytes 576008 | tf_op jit(solution)/shard_map/ppermute | solution.py:29
  87.0 12.9 %collective-permute-start.4 = (bf16[128,750]{1,0:T(8,128)(2,1)S(1)}, bf16[128,750]{1,0:T(8,128)(2,1)S(1)}, u32[]{:S(2)}, u32[]{:S(2)}) collective-permute-start(bf16[128,750]{1,0:T(8,128)(2,1)S(1)} %add_convert_fusion.4), channel_id=1, source_target_pairs={{0,1},{1,2},{2,3},{3,4},{4,5},{5,6},{6,7},{7,0},{8,9},{9,10},{10,1... | collective-permute-start | bytes 576008 | tf_op jit(solution)/shard_map/ppermute | solution.py:29
  90.4 9.5 %collective-permute-start.8 = (bf16[128,750]{1,0:T(8,128)(2,1)S(1)}, bf16[128,750]{1,0:T(8,128)(2,1)S(1)}, u32[]{:S(2)}, u32[]{:S(2)}) collective-permute-start(bf16[128,750]{1,0:T(8,128)(2,1)S(1)} %add_convert_fusion.1), channel_id=1, source_target_pairs={{0,7},{1,0},{2,1},{3,2},{4,3},{5,4},{6,5},{7,6},{8,15},{9,8},{10,9... | collective-permute-start | bytes 576008 | tf_op jit(solution)/shard_map/ppermute | solution.py:29
  94.2 5.7 %collective-permute-start.16 = (bf16[366,250]{1,0:T(8,128)(2,1)S(1)}, bf16[366,250]{1,0:T(8,128)(2,1)S(1)}, u32[]{:S(2)}, u32[]{:S(2)}) collective-permute-start(bf16[366,250]{1,0:T(8,128)(2,1)S(1)} %slice.17), channel_id=1, source_target_pairs={{0,7},{1,0},{2,1},{3,2},{4,3},{5,4},{6,5},{7,6},{8,15},{9,8},{10,9... | collective-permute-start | bytes 549008 | tf_op jit(solution)/shard_map/ppermute | solution.py:29
  101.2 1.7 collective-permute-start.17
  103.6 15.3 %all-to-all-start.1 = ((bf16[8,64,256]{2,1,0:T(8,128)(2,1)}), bf16[8,64,256]{2,1,0:T(8,128)(2,1)S(1)}, u32[]{:S(2)}, u32[]{:S(2)}) async-start(bf16[8,64,256]{2,1,0:T(8,128)(2,1)} %add_convert_fusion), calls=%async_computation.1 | async-start | bytes 524288 | tf_op jit(solution)/shard_map/all_to_all | solution.py:54
  118.9 49.6 %copy-start.3 = (bf16[256,1500]{1,0:T(8,128)(2,1)S(1)}, bf16[256,1500]{1,0:T(8,128)(2,1)}, u32[]{:S(2)}) copy-start(bf16[256,1500]{1,0:T(8,128)(2,1)} %copy-done.2) | copy-start | bytes 2304004
  118.9 49.6 %copy-start.5 = (bf16[256,1500]{1,0:T(8,128)(2,1)S(1)}, bf16[256,1500]{1,0:T(8,128)(2,1)}, u32[]{:S(2)}) copy-start(bf16[256,1500]{1,0:T(8,128)(2,1)} %copy-done.4) | copy-start | bytes 2304004
  134.0 1.5 collective-permute-start.18
  137.1 8.5 %collective-permute-start.19 = (bf16[128,750]{1,0:T(8,128)(2,1)S(1)}, bf16[128,750]{1,0:T(8,128)(2,1)S(1)}, u32[]{:S(2)}, u32[]{:S(2)}) collective-permute-start(bf16[128,750]{1,0:T(8,128)(2,1)S(1)} %shard_map.68.refs_0_), channel_id=1, source_target_pairs={{0,1},{1,2},{2,3},{3,4},{4,5},{5,6},{6,7},{7,0},{8,9},{9,10},{10,1... | collective-permute-start | bytes 576008 | tf_op jit(solution)/shard_map/ppermute | solution.py:29
  137.2 8.4 %collective-permute-start.20 = (bf16[128,750]{1,0:T(8,128)(2,1)S(1)}, bf16[128,750]{1,0:T(8,128)(2,1)S(1)}, u32[]{:S(2)}, u32[]{:S(2)}) collective-permute-start(bf16[128,750]{1,0:T(8,128)(2,1)S(1)} %shard_map.68.refs_0_), channel_id=1, source_target_pairs={{0,7},{1,0},{2,1},{3,2},{4,3},{5,4},{6,5},{7,6},{8,15},{9,8},{10,9... | collective-permute-start | bytes 576008 | tf_op jit(solution)/shard_map/ppermute | solution.py:29
  145.6 7.5 %collective-permute-start.21 = (bf16[128,750]{1,0:T(8,128)(2,1)S(1)}, bf16[128,750]{1,0:T(8,128)(2,1)S(1)}, u32[]{:S(2)}, u32[]{:S(2)}) collective-permute-start(bf16[128,750]{1,0:T(8,128)(2,1)S(1)} %collective-permute-done.19.refs_1_), channel_id=1, source_target_pairs={{0,1},{1,2},{2,3},{3,4},{4,5},{5,6},{6,7},{7,0},{8,9},{9,10},{10,1... | collective-permute-start | bytes 576008 | tf_op jit(solution)/shard_map/ppermute | solution.py:29
  145.6 7.5 %collective-permute-start.22 = (bf16[128,750]{1,0:T(8,128)(2,1)S(1)}, bf16[128,750]{1,0:T(8,128)(2,1)S(1)}, u32[]{:S(2)}, u32[]{:S(2)}) collective-permute-start(bf16[128,750]{1,0:T(8,128)(2,1)S(1)} %collective-permute-done.20.refs_2_), channel_id=1, source_target_pairs={{0,7},{1,0},{2,1},{3,2},{4,3},{5,4},{6,5},{7,6},{8,15},{9,8},{10,9... | collective-permute-start | bytes 576008 | tf_op jit(solution)/shard_map/ppermute | solution.py:29
  153.2 15.4 %collective-permute-start.23 = (bf16[128,750]{1,0:T(8,128)(2,1)S(1)}, bf16[128,750]{1,0:T(8,128)(2,1)S(1)}, u32[]{:S(2)}, u32[]{:S(2)}) collective-permute-start(bf16[128,750]{1,0:T(8,128)(2,1)S(1)} %collective-permute-done.21.refs_3_), channel_id=1, source_target_pairs={{0,1},{1,2},{2,3},{3,4},{4,5},{5,6},{6,7},{7,0},{8,9},{9,10},{10,1... | collective-permute-start | bytes 576008 | tf_op jit(solution)/shard_map/ppermute | solution.py:29
  153.2 15.4 %collective-permute-start.24 = (bf16[128,750]{1,0:T(8,128)(2,1)S(1)}, bf16[128,750]{1,0:T(8,128)(2,1)S(1)}, u32[]{:S(2)}, u32[]{:S(2)}) collective-permute-start(bf16[128,750]{1,0:T(8,128)(2,1)S(1)} %collective-permute-done.22.refs_4_), channel_id=1, source_target_pairs={{0,7},{1,0},{2,1},{3,2},{4,3},{5,4},{6,5},{7,6},{8,15},{9,8},{10,9... | collective-permute-start | bytes 576008 | tf_op jit(solution)/shard_map/ppermute | solution.py:29
  156.4 11.1 %collective-permute-start.25 = (bf16[64,750]{1,0:T(8,128)(2,1)S(1)}, bf16[64,750]{1,0:T(8,128)(2,1)S(1)}, u32[]{:S(2)}, u32[]{:S(2)}) collective-permute-start(bf16[64,750]{1,0:T(8,128)(2,1)S(1)} %get-tuple-element.36), channel_id=1, source_target_pairs={{0,4},{1,5},{2,6},{3,7},{4,0},{5,1},{6,2},{7,3},{8,12},{9,13},{10,... | collective-permute-start | bytes 288008 | tf_op jit(solution)/shard_map/ppermute | solution.py:29
  156.6 12.0 %collective-permute-start.26 = (bf16[64,750]{1,0:T(8,128)(2,1)S(1)}, bf16[64,750]{1,0:T(8,128)(2,1)S(1)}, u32[]{:S(2)}, u32[]{:S(2)}) collective-permute-start(bf16[64,750]{1,0:T(8,128)(2,1)S(1)} %get-tuple-element.35), channel_id=1, source_target_pairs={{0,4},{1,5},{2,6},{3,7},{4,0},{5,1},{6,2},{7,3},{8,12},{9,13},{10,... | collective-permute-start | bytes 288008 | tf_op jit(solution)/shard_map/ppermute | solution.py:29
